TPU v7x, 32 devices: a whole 2x2x4 slice. The times are simulated.
32 devices in a mesh: hx: 8 (over z, x), hy: 4 (over y, core).
Axes of the slice: x: 2, y: 2, z: 4, core: 2. Of those that a mesh axis runs over, the one named last changes fastest.
Arguments:
- source: float32 [512, 512], P('hx', 'hy'), may hold values from -27 to 27
- coeffs: float32 [65, 65], replicated, may hold values from -0.13 to 0.13
- row_factor: float32 [512, 512], P('hx'), may hold values from -0.075 to 0.575
- col_factor: float32 [512, 512], P(None, 'hy'), may hold values from -0.075 to 0.575
- tile_mask: int32 [2, 2], replicated, may hold values 0 or 1
Outputs:
- solution: float32 [512, 512], P('hx', 'hy')
- norm_values: float32 [8], replicated
Inputs may be any that keep to these rules, and one draw needn't show every extreme that they name: tile_mask[a, b] is 1 where the tile of rows a * 256 onward and columns b * 256 onward carries a block coupling, else 0.
All inputs are finite; a program needn't handle non-finite values.
Results may differ from a plain program's by a relative error of at most 0.0003.
Values sent between devices are 32-bit elements; how exact they have to be, the bound alone decides.
No kernel may reach another device: no remote copies, remote signals or barrier semaphores. Data moves between devices by JAX's collectives and lax.ppermute only.
A program may use at most 64 MiB of HBM per device.

v0:
```python
import functools
import jax
import jax.numpy as jnp
import numpy as np
from jax import lax
from jax.experimental import pallas as pl
from jax.experimental.pallas import tpu as pltpu
from jax.sharding import PartitionSpec as P

TILE = 256
ITERS = 8
HALF = TILE // 2
LANES = 128
GRID_BYTES = 2 * 1024 * 1024


relax_step = 0.25
highest = lax.Precision.HIGHEST
tiny_square = 1e-06


def with_halo(value, sides, width):
    for axis, dim in sides:
        count, length = (lax.axis_size(axis), value.shape[dim])
        up = [(i, (i + 1) % count) for i in range(count - 1)]
        down = [(j, i) for i, j in up]
        last = lax.slice_in_dim(value, length - width, length, axis=dim)
        initial = lax.slice_in_dim(value, 0, width, axis=dim)
        before = lax.ppermute(last, axis, up)
        after = lax.ppermute(initial, axis, down)
        value = jnp.concatenate([before, value, after], axis=dim)
    return value


def swapped(value, axis, apart):
    return lax.ppermute(value, axis, [(i, i ^ 1 << apart) for i in range(lax.axis_size(axis))])


def row_panels(coeffs, row_count, band_width):
    tap_count = 2 * band_width + 1
    padded_rows = row_count + 2 * band_width
    shape_three = (tap_count, row_count, padded_rows)
    tap_index = lax.broadcasted_iota(jnp.int32, shape_three, 0)
    target = lax.broadcasted_iota(jnp.int32, shape_three, 1)
    source_row = lax.broadcasted_iota(jnp.int32, shape_three, 2)
    picker = (source_row == target + 2 * band_width - tap_index).astype(jnp.float32)
    panels = jnp.einsum("pq,pmi->mqi", coeffs, picker, precision=highest)
    return panels.reshape(row_count, tap_count * padded_rows)


def banded_product(field_now, panels, band_width):
    col_count = field_now.shape[1]
    padded = with_halo(field_now, (("hx", 0), ("hy", 1)), band_width)
    pieces = [
        padded[:, 2 * band_width - offset : 2 * band_width - offset + col_count]
        for offset in range(2 * band_width + 1)
    ]
    stacked = jnp.concatenate(pieces, axis=0)
    return jnp.dot(panels, stacked, precision=highest, preferred_element_type=jnp.float32)


def joined(block, partner, upper_half, axis_dim):
    return jnp.where(
        upper_half,
        jnp.concatenate([partner, block], axis_dim),
        jnp.concatenate([block, partner], axis_dim),
    )


def distributed(source, coeffs, row_factor, col_factor, tile_mask):
    row_count, col_count = source.shape
    band_width = (coeffs.shape[0] - 1) // 2
    row_group = TILE // row_count
    col_group = TILE // col_count
    row_index = lax.axis_index("hx")
    col_index = lax.axis_index("hy")
    tile_row = row_index // row_group
    tile_col = col_index // col_group
    panels = row_panels(coeffs, row_count, band_width)
    row_factor_tile = lax.dynamic_slice_in_dim(row_factor, tile_col * TILE, TILE, 1)
    col_factor_tile = lax.dynamic_slice_in_dim(col_factor, tile_row * TILE, TILE, 0)
    mask_rows = lax.broadcasted_iota(jnp.int32, tile_mask.shape, 0)
    mask_cols = lax.broadcasted_iota(jnp.int32, tile_mask.shape, 1)
    chosen = (mask_rows == tile_row) & (mask_cols == tile_col)
    active = jnp.sum(jnp.where(chosen, tile_mask, 0)).astype(jnp.float32)
    solution = source
    squares = []
    for step_index in range(ITERS):
        wide_block = solution
        bit_level = 0
        partner = swapped(wide_block, "hy", bit_level)
        upper_half = col_index // (1 << bit_level) % 2 == 1
        wide_block = joined(wide_block, partner, upper_half, 1)
        mixed_cols = jnp.dot(
            wide_block, col_factor_tile, precision=highest, preferred_element_type=jnp.float32
        )
        tall_block = mixed_cols
        for bit_level in range(row_group.bit_length() - 1):
            partner = swapped(tall_block, "hx", bit_level)
            upper_half = row_index // (1 << bit_level) % 2 == 1
            tall_block = joined(tall_block, partner, upper_half, 0)
        result = jnp.dot(
            row_factor_tile, tall_block, precision=highest, preferred_element_type=jnp.float32
        )
        applied = solution + banded_product(solution, panels, band_width) + active * result
        residual = source - applied
        local_square = jnp.sum(residual * residual)
        squares.append(lax.psum(local_square, ("hx", "hy")))
        solution = solution + relax_step * residual
    summed = jnp.stack(squares)
    cell_count = row_count * col_count * lax.axis_size("hx") * lax.axis_size("hy")
    norm_values = jnp.sqrt(summed / cell_count + tiny_square)
    return (solution, norm_values)


def packed_dft():
    place = np.arange(TILE)
    freq = np.arange(HALF)
    phase = 2 * np.pi * ((freq[:, None] * place[None, :]) % TILE) / TILE
    forward = np.concatenate([np.cos(phase), np.sin(phase)], 0)
    forward[HALF] = np.cos(np.pi * place)
    weight = np.full((TILE, 1), 2.0 / TILE)
    weight[0] = weight[HALF] = 1.0 / TILE
    return forward, (forward * weight).T


def tap_waves(band_width):
    offset = np.arange(-band_width, band_width + 1)
    freq = np.concatenate([np.arange(HALF), np.arange(HALF)])
    freq[HALF] = HALF
    phase = 2 * np.pi * ((freq[:, None] * offset[None, :]) % TILE) / TILE
    return np.concatenate([np.cos(phase), np.sin(phase)], 0).astype(np.float32)


def split_np(value):
    high = value.astype(jnp.bfloat16)
    return high, (value - high.astype(np.float64)).astype(jnp.bfloat16)


def window_mats(length, band_width):
    forward, inverse = packed_dft()
    count = length // HALF - 1
    mats = [[], [], [], []]
    spans = []
    for w in range(count):
        first, last = w == 0, w == count - 1
        taken = np.ones(TILE)
        if first:
            taken[TILE - band_width :] = 0
        if last:
            taken[:band_width] = 0
        low = 0 if first else HALF // 2
        high = TILE if last else TILE - HALF // 2
        spans.append((low, high))
        kept = np.zeros(TILE)
        kept[low:high] = 1
        fh, fl = split_np(forward * taken[None, :])
        gh, gl = split_np(inverse * kept[:, None])
        mats[0].append(np.concatenate([fh, fh, fl], 1))
        mats[1].append(np.concatenate([fh.T, fh.T, fl.T], 0))
        mats[2].append(np.concatenate([gh, gh, gl], 1))
        mats[3].append(np.concatenate([gh.T, gh.T, gl.T], 0))
    return [np.stack(m) for m in mats], spans


def tap_spectrum(coeffs):
    waves = jnp.asarray(tap_waves((coeffs.shape[0] - 1) // 2))
    mixed = jnp.dot(jnp.dot(waves, coeffs, precision=highest), waves.T, precision=highest)
    sign = np.where(np.arange(TILE) < HALF, -1.0, 1.0).astype(np.float32)
    quarter = [[mixed[i * TILE : (i + 1) * TILE, j * TILE : (j + 1) * TILE] for j in (0, 1)] for i in (0, 1)]
    return jnp.stack(
        [
            quarter[0][0],
            quarter[1][0] * sign[:, None],
            quarter[0][1] * sign[None, :],
            quarter[1][1] * (sign[:, None] * sign[None, :]),
        ]
    )


def split(value):
    high = value.astype(jnp.bfloat16)
    return high, (value - high.astype(jnp.float32)).astype(jnp.bfloat16)


def dot32(left, right):
    return jnp.dot(left, right, preferred_element_type=jnp.float32)


def replicated_kernel(
    row_spans, hx_bits, col_places, place, mask, s_own, s_far, r_own, r_far, c_own, c_far, spectrum,
    row_fwd, col_fwd, row_inv, col_inv, out, squares,
    state, total, w_hi, w_lo, z_hi, z_lo, y_hi, y_lo, u_hi, u_lo, t_hi, t_lo, wave, left, right,
):
    rows, cols = state.shape
    row_windows, col_windows = row_fwd.shape[0], col_fwd.shape[0]
    tile_rows, tile_cols = rows // TILE, cols // TILE
    block_rows, block_cols = s_own.shape[-2:]
    here_x, here_y, here_c = place[0], place[1], place[2]
    for pos in range(s_own.shape[0]):
        s_row = (here_x ^ hx_bits[0][pos]) * block_rows
        s_row = pl.multiple_of(s_row, block_rows)
        for far, ref in ((0, s_own), (1, s_far)):
            for k in range(s_own.shape[1]):
                s_col = ((here_y ^ k) * 2 + (here_c ^ far)) * block_cols
                s_col = pl.multiple_of(s_col, block_cols)
                value = ref[pos, k]
                state[pl.ds(s_row, block_rows), pl.ds(s_col, block_cols)] = value
                total[pl.ds(s_row, block_rows), pl.ds(s_col, block_cols)] = value
                high, low = split(value)
                w_hi[pl.ds(s_row, block_rows), pl.ds(s_col, block_cols)] = high
                w_lo[pl.ds(s_row, block_rows), pl.ds(s_col, block_cols)] = low
    share = TILE // block_rows
    for pos in range(r_own.shape[0]):
        index = here_x ^ hx_bits[1][pos]
        a = index // share
        sub = pl.multiple_of((index % share) * block_rows, block_rows)
        for far, ref in ((0, r_own), (1, r_far)):
            side = here_c ^ far
            for k in range(r_own.shape[1]):
                lane = side * (cols // 2) + k * LANES
                b = lane // TILE
                at = pl.multiple_of(lane % TILE, LANES)
                high, low = split(ref[pos, k] * mask[a, b].astype(jnp.float32))
                for third, part in enumerate((high, high, low)):
                    left[a, b, pl.ds(sub, block_rows), pl.ds(pl.multiple_of(at + third * TILE, LANES), LANES)] = part
    for k in range(c_own.shape[0]):
        for far, ref in ((0, c_own), (1, c_far)):
            lane = ((here_y ^ k) * 2 + (here_c ^ far)) * block_cols
            b = lane // TILE
            at = pl.multiple_of(lane % TILE, block_cols)
            for a in range(tile_rows):
                high, low = split(ref[k, pl.ds(a * TILE, TILE), :])
                for third, part in enumerate((high, high, low)):
                    right[a, b, pl.ds(third * TILE, TILE), pl.ds(at, block_cols)] = part

    def triple(hi_ref, lo_ref, row_at, col_at, axis):
        high = hi_ref[row_at, col_at]
        return jnp.concatenate([high, lo_ref[row_at, col_at], high], axis)

    def step(k, carry):
        keep = jnp.where(k == 0, 0.0, 1.0 - relax_step)
        take = jnp.where(k == 0, 1.0, relax_step)
        every = pl.ds(0, rows)
        for b in range(col_windows):
            z = dot32(triple(w_hi, w_lo, every, pl.ds(b * HALF, TILE), 1), col_fwd[b])
            z_hi[:, pl.ds(b * TILE, TILE)], z_lo[:, pl.ds(b * TILE, TILE)] = split(z)
        for a in range(row_windows):
            for b in range(col_windows):
                cells = triple(z_hi, z_lo, pl.ds(a * HALF, TILE), pl.ds(b * TILE, TILE), 0)
                wave[...] = dot32(row_fwd[a], cells)
                for i in (0, 1):
                    for j in (0, 1):
                        ri, rj = pl.ds(i * HALF, HALF), pl.ds((1 - i) * HALF, HALF)
                        ci, cj = pl.ds(j * HALF, HALF), pl.ds((1 - j) * HALF, HALF)
                        y = (
                            spectrum[0, ri, ci] * wave[ri, ci]
                            + spectrum[1, ri, ci] * wave[rj, ci]
                            + spectrum[2, ri, ci] * wave[ri, cj]
                            + spectrum[3, ri, ci] * wave[rj, cj]
                        )
                        to = pl.ds(a * TILE + i * HALF, HALF), pl.ds(b * TILE + j * HALF, HALF)
                        y_hi[to], y_lo[to] = split(y)
        for a in range(row_windows):
            low, high = row_spans[a]
            for b in range(col_windows):
                cells = triple(y_hi, y_lo, pl.ds(a * TILE, TILE), pl.ds(b * TILE, TILE), 0)
                u = dot32(row_inv[a, low:high, :], cells)
                to = pl.ds(a * HALF + low, high - low), pl.ds(b * TILE, TILE)
                u_hi[to], u_lo[to] = split(u)
        for a in range(tile_rows):
            for b in range(tile_cols):
                at = pl.ds(a * TILE, TILE), pl.ds(b * TILE, TILE)
                t_hi[at], t_lo[at] = split(dot32(left[a, b], triple(w_hi, w_lo, *at, 0)))
        square = jnp.zeros((8, LANES), jnp.float32)
        for a in range(tile_rows):
            ra = pl.ds(a * TILE, TILE)
            parts = []
            for b in range(col_windows):
                lhs = triple(u_hi, u_lo, ra, pl.ds(b * TILE, TILE), 1)
                rhs = col_inv[b]
                if b % 2 == 0:
                    lhs = jnp.concatenate([lhs, triple(t_hi, t_lo, ra, pl.ds(b // 2 * TILE, TILE), 1)], 1)
                    rhs = jnp.concatenate([rhs, right[a, b // 2]], 0)
                parts.append(dot32(lhs, rhs))
            for j in range(cols // HALF):
                pieces = [parts[b][:, (j - b) * HALF : (j - b + 1) * HALF] for b in range(col_windows) if b <= j <= b + 1]
                cj = pl.ds(j * HALF, HALF)
                residual = keep * state[ra, cj] - take * functools.reduce(jnp.add, pieces)
                state[ra, cj] = residual
                total[ra, cj] = total[ra, cj] + relax_step * residual
                w_hi[ra, cj], w_lo[ra, cj] = split(residual)
                square = square + jnp.sum((residual * residual).reshape(TILE // 8, 8, LANES), 0)
        squares[k] = square
        return carry

    lax.fori_loop(0, ITERS, step, 0)
    own_row = pl.multiple_of(here_x * block_rows, block_rows)
    own_col = pl.multiple_of((here_y * 2 + here_c) * block_cols, block_cols)
    out[...] = total[pl.ds(own_row, block_rows), pl.ds(own_col, block_cols)]


def swap(value, axis, bit):
    return lax.ppermute(value, axis, [(i, i ^ bit) for i in range(lax.axis_size(axis))])


def doubled(value, axis, bits):
    for bit in bits:
        value = jnp.concatenate([value, swap(value, axis, bit)], 0)
    return value


def bit_places(bits):
    places = [0]
    for bit in bits:
        places = places + [p | bit for p in places]
    return places


def replicated(source, coeffs, row_factor, col_factor, tile_mask):
    block_rows, block_cols = source.shape
    rows, cols = col_factor.shape[0], row_factor.shape[1]
    band_width = (coeffs.shape[0] - 1) // 2
    hx_size, hy_size = lax.axis_size("hx"), lax.axis_size("hy")
    index_x, index_y = lax.axis_index("hx"), lax.axis_index("hy")
    down = [1 << i for i in reversed(range(hx_size.bit_length() - 1))]
    turned = down[:-2] + down[-2:][::-1]
    y_bits = [1 << i for i in range(1, hy_size.bit_length() - 1)]
    s_part = doubled(source[None], "hy", y_bits)
    c_part = doubled(col_factor[None], "hy", y_bits)
    r_half = lax.dynamic_slice_in_dim(row_factor, (index_y % 2) * (cols // 2), cols // 2, 1)
    r_part = r_half.reshape(block_rows, -1, LANES).swapaxes(0, 1)
    s_count = s_part.shape[0]
    both = jnp.concatenate([s_part, r_part], 0)[None]
    both = doubled(both, "hx", down[:-2])
    s_all = doubled(both[:, :s_count], "hx", down[-2:])
    r_all = doubled(both[:, s_count:], "hx", turned[-2:])
    far = [swap(v, "hy", 1) for v in (s_all, r_all, c_part)]
    spectrum = tap_spectrum(coeffs)
    mats, row_spans = window_mats(rows, band_width)
    col_mats, _ = window_mats(cols, band_width)
    weights = [jnp.asarray(m) for m in (mats[0], col_mats[1], mats[2], col_mats[3])]
    place = jnp.stack([index_x, index_y // 2, index_y % 2])
    row_windows, col_windows = rows // HALF - 1, cols // HALF - 1
    vmem = pl.BlockSpec(memory_space=pltpu.VMEM)
    smem = pl.BlockSpec(memory_space=pltpu.SMEM)
    f32, bf16 = jnp.float32, jnp.bfloat16
    shapes = [((rows, cols), f32)] * 2 + [((rows, cols), bf16)] * 2 + [((rows, col_windows * TILE), bf16)] * 2
    shapes += [((row_windows * TILE, col_windows * TILE), bf16)] * 2 + [((rows, col_windows * TILE), bf16)] * 2
    shapes += [((rows, cols), bf16)] * 2 + [((TILE, TILE), f32)]
    tiles = (rows // TILE, cols // TILE)
    shapes += [(tiles + (TILE, 3 * TILE), bf16), (tiles + (3 * TILE, TILE), bf16)]
    result, squares = pl.pallas_call(
        functools.partial(replicated_kernel, row_spans, (bit_places(down), bit_places(turned)), None),
        out_shape=(
            jax.ShapeDtypeStruct((block_rows, block_cols), f32),
            jax.ShapeDtypeStruct((ITERS, 8, LANES), f32),
        ),
        in_specs=[smem, smem] + [vmem] * 11,
        out_specs=(vmem, vmem),
        scratch_shapes=[pltpu.VMEM(*s) for s in shapes],
        compiler_params=pltpu.CompilerParams(vmem_limit_bytes=40 * 1024 * 1024),
        name="replicated_steps",
    )(place, tile_mask, s_all, far[0], r_all, far[1], c_part, far[2], spectrum, *weights)
    norm_values = jnp.sqrt(jnp.sum(squares, (1, 2)) / (rows * cols) + tiny_square)
    return result, norm_values


def fits(rows, cols, block_rows, block_cols, band_width, hx_size, hy_size):
    powers = all(n & (n - 1) == 0 for n in (hx_size, hy_size))
    whole = rows % TILE == 0 and cols % TILE == 0 and rows > TILE and cols > TILE
    aligned = TILE % block_rows == 0 and block_rows % 16 == 0 and block_cols == LANES and cols % (2 * LANES) == 0
    small = rows * cols * 4 <= GRID_BYTES and 4 * band_width <= TILE
    return powers and whole and aligned and small and hx_size >= 4 and hy_size >= 2


def local(source, coeffs, row_factor, col_factor, tile_mask):
    rows, cols = col_factor.shape[0], row_factor.shape[1]
    band_width = (coeffs.shape[0] - 1) // 2
    sizes = lax.axis_size("hx"), lax.axis_size("hy")
    if fits(rows, cols, *source.shape, band_width, *sizes):
        return replicated(source, coeffs, row_factor, col_factor, tile_mask)
    return distributed(source, coeffs, row_factor, col_factor, tile_mask)


def solution(mesh):
    in_specs = (P("hx", "hy"), P(), P("hx", None), P(None, "hy"), P())
    out_specs = (P("hx", "hy"), P())
    return jax.shard_map(local, mesh=mesh, in_specs=in_specs, out_specs=out_specs, check_vma=False)
```

profile of v0, /device:TPU:0, one launch (start us, length us, event | category | flops | bytes accessed | tf_op | source)
XLA Modules:
  0.0 75.5 jit_solution(3849462294083345113)
XLA Ops:
  0.6 0.0 copy-start
  0.6 0.0 copy-start.6
  0.7 0.0 copy-start.9
  0.7 3.1 %collective-permute-start = (f32[1,64,128]{2,1,0:T(8,128)}, f32[1,64,128]{2,1,0:T(8,128)S(1)}, u32[]{:S(2)}, u32[]{:S(2)}) collective-permute-start(f32[1,64,128]{2,1,0:T(8,128)} %bitcast.28), channel_id=1, source_target_pairs={{0,2},{1,3},{2,0},{3,1},{4,6},{5,7},{6,4},{7,5},{8,10},{9,11},{10,... | collective-permute-start | bytes 98312 | tf_op jit(solution)/shard_map/ppermute | solution.py:304
  3.7 0.0 copy-done
  3.7 0.0 copy-start.8
  3.8 2.1 %collective-permute-done = f32[1,64,128]{2,1,0:T(8,128)S(1)} collective-permute-done((f32[1,64,128]{2,1,0:T(8,128)}, f32[1,64,128]{2,1,0:T(8,128)S(1)}, u32[]{:S(2)}, u32[]{:S(2)}) %collective-permute-start) | collective-permute-done | bytes 32800 | tf_op jit(solution)/shard_map/ppermute | solution.py:304
  5.8 0.8 %maximum_bitcast_fusion = f32[1,4,64,128]{3,2,1,0:T(8,128)S(1)} fusion(f32[2,64,128]{2,1,0:T(8,128)S(1)} %bitcast_bitcast_fusion, f32[1,64,128]{2,1,0:T(8,128)S(1)} %collective-permute-done, f32[1,64,128]{2,1,0:T(8,128)} %bitcast.29), kind=kLoop, calls=%fused_computation.17 | loop fusion | flops 65536 | bytes 262144 | tf_op jit(solution)/shard_map/broadcast_in_dim | solution.py:334
  6.6 3.2 %collective-permute-start.1 = (f32[1,4,64,128]{3,2,1,0:T(8,128)S(1)}, f32[1,4,64,128]{3,2,1,0:T(8,128)S(1)}, u32[]{:S(2)}, u32[]{:S(2)}) collective-permute-start(f32[1,4,64,128]{3,2,1,0:T(8,128)S(1)} %maximum_bitcast_fusion), channel_id=1, source_target_pairs={{0,16},{4,20},{8,24},{12,28},{16,0},{20,4},{24,8},{28,12},{1,17},{... | collective-permute-start | bytes 393224 | tf_op jit(solution)/shard_map/ppermute | solution.py:304
  9.8 5.2 %collective-permute-done.1 = f32[1,4,64,128]{3,2,1,0:T(8,128)S(1)} collective-permute-done((f32[1,4,64,128]{3,2,1,0:T(8,128)S(1)}, f32[1,4,64,128]{3,2,1,0:T(8,128)S(1)}, u32[]{:S(2)}, u32[]{:S(2)}) %collective-permute-start.1) | collective-permute-done | bytes 131104 | tf_op jit(solution)/shard_map/ppermute | solution.py:304
  14.9 1.6 %collective-permute-start.5 = (f32[2,2,64,128]{3,2,1,0:T(8,128)S(1)}, f32[2,2,64,128]{3,2,1,0:T(8,128)S(1)}, u32[]{:S(2)}, u32[]{:S(2)}) collective-permute-start(f32[2,2,64,128]{3,2,1,0:T(8,128)S(1)} %get-tuple-element.12), channel_id=1, source_target_pairs={{0,4},{4,0},{8,12},{12,8},{16,20},{20,16},{24,28},{28,24},{1,5},{5... | collective-permute-start | bytes 393224 | tf_op jit(solution)/shard_map/ppermute | solution.py:304
  16.5 0.7 collective-permute-start.2
  17.2 1.5 %collective-permute-start.8 = (f32[1,512,128]{2,1,0:T(8,128)}, f32[1,512,128]{2,1,0:T(8,128)S(1)}, u32[]{:S(2)}, u32[]{:S(2)}) collective-permute-start(f32[1,512,128]{2,1,0:T(8,128)} %bitcast.26), channel_id=1, source_target_pairs={{0,2},{1,3},{2,0},{3,1},{4,6},{5,7},{6,4},{7,5},{8,10},{9,11},{10,... | collective-permute-start | bytes 786440 | tf_op jit(solution)/shard_map/ppermute | solution.py:304
  18.7 1.2 %collective-permute-done.5 = f32[2,2,64,128]{3,2,1,0:T(8,128)S(1)} collective-permute-done((f32[2,2,64,128]{3,2,1,0:T(8,128)S(1)}, f32[2,2,64,128]{3,2,1,0:T(8,128)S(1)}, u32[]{:S(2)}, u32[]{:S(2)}) %collective-permute-start.5) | collective-permute-done | bytes 131104 | tf_op jit(solution)/shard_map/ppermute | solution.py:304
  20.0 0.8 %collective-permute-start.6 = (f32[4,2,64,128]{3,2,1,0:T(8,128)S(1)}, f32[4,2,64,128]{3,2,1,0:T(8,128)S(1)}, u32[]{:S(2)}, u32[]{:S(2)}) collective-permute-start(f32[4,2,64,128]{3,2,1,0:T(8,128)S(1)} %pad_maximum_fusion.5), channel_id=1, source_target_pairs={{0,8},{4,12},{8,0},{12,4},{16,24},{20,28},{24,16},{28,20},{1,9},{5... | collective-permute-start | bytes 786440 | tf_op jit(solution)/shard_map/ppermute | solution.py:304
  20.8 2.1 %collective-permute-done.2 = f32[2,2,64,128]{3,2,1,0:T(8,128)S(1)} collective-permute-done((f32[2,2,64,128]{3,2,1,0:T(8,128)S(1)}, f32[2,2,64,128]{3,2,1,0:T(8,128)S(1)}, u32[]{:S(2)}, u32[]{:S(2)}) %collective-permute-start.2) | collective-permute-done | bytes 131104 | tf_op jit(solution)/shard_map/ppermute | solution.py:304
  22.9 0.1 collective-permute-start.3
  23.0 0.0 copy-done.6
  23.0 0.0 copy-done.9
  23.0 0.4 fusion.4
  23.4 0.8 %collective-permute-done.8 = f32[1,512,128]{2,1,0:T(8,128)S(1)} collective-permute-done((f32[1,512,128]{2,1,0:T(8,128)}, f32[1,512,128]{2,1,0:T(8,128)S(1)}, u32[]{:S(2)}, u32[]{:S(2)}) %collective-permute-start.8) | collective-permute-done | bytes 262176 | tf_op jit(solution)/shard_map/ppermute | solution.py:304
  24.2 0.0 copy-done.8
  24.3 0.0 copy-start.7
  24.3 0.1 collective-permute-start.9
  24.3 2.4 %collective-permute-done.6 = f32[4,2,64,128]{3,2,1,0:T(8,128)S(1)} collective-permute-done((f32[4,2,64,128]{3,2,1,0:T(8,128)S(1)}, f32[4,2,64,128]{3,2,1,0:T(8,128)S(1)}, u32[]{:S(2)}, u32[]{:S(2)}) %collective-permute-start.6) | collective-permute-done | bytes 262176 | tf_op jit(solution)/shard_map/ppermute | solution.py:304
  26.8 0.0 copy-start.10
  26.8 0.1 collective-permute-start.7
  26.9 2.5 %collective-permute-done.3 = f32[4,2,64,128]{3,2,1,0:T(8,128)S(1)} collective-permute-done((f32[4,2,64,128]{3,2,1,0:T(8,128)S(1)}, f32[4,2,64,128]{3,2,1,0:T(8,128)S(1)}, u32[]{:S(2)}, u32[]{:S(2)}) %collective-permute-start.3) | collective-permute-done | bytes 262176 | tf_op jit(solution)/shard_map/ppermute | solution.py:304
  29.4 0.1 collective-permute-start.4
  29.5 0.0 copy-done.7
  29.5 0.0 copy-start.4
  29.5 2.0 %fusion.5 = f32[512,512]{1,0:T(8,128)} fusion(f32[512,65]{1,0:T(8,128)S(1)} %fusion.4, f32[512,65]{1,0:T(8,128)S(1)} %copy-done.7), kind=kOutput, calls=%fused_computation.23 | convolution fusion | flops 204472320 | bytes 1314816 | tf_op jit(solution)/shard_map/dot_general | solution.py:168
  31.5 0.1 pad_add_fusion.place
  31.6 0.0 copy-done.10
  31.6 0.0 copy-start.2
  31.6 0.0 copy-start.3
  31.6 1.5 %slice_bitcast_fusion = (f32[1,256,256]{2,1,0:T(8,128)S(1)}, f32[1,256,256]{2,1,0:T(8,128)S(1)}, f32[1,256,256]{2,1,0:T(8,128)S(1)}, f32[1,256,256]{2,1,0:T(8,128)S(1)}) fusion(f32[512,512]{1,0:T(8,128)} %fusion.5, f32[256,256]{1,0:T(8,128)} %constant.66.clone, f32[256]{0:T(256)S(1)} %copy-done.10), kind=kLoop, calls=%fused_computation.10 | loop fusion | flops 196608 | bytes 2361344 | tf_op jit(solution)/shard_map/stack | solution.py:171
  33.1 0.0 copy-start.1
  33.1 0.0 copy-start.5
  33.1 0.1 pad_maximum_fusion.spectrum
  33.2 0.0 collective-permute-done.9.c_far
  33.2 0.0 collective-permute-done.7.r_far
  33.2 0.0 collective-permute-done.4.s_far
  33.3 0.0 copy-done.4
  33.3 0.0 copy-done.2
  33.3 0.3 copy-done.3
  33.6 0.9 %copy-done.1 = bf16[3,256,768]{2,1,0:T(8,128)(2,1)S(1)} copy-done((bf16[3,256,768]{2,1,0:T(8,128)(2,1)S(1)}, bf16[3,256,768]{2,1,0:T(8,128)(2,1)}, u32[]{:S(2)}) %copy-start.1) | copy-done | bytes 1179672
  34.5 0.0 copy-done.5
  34.5 40.4 %replicated_steps.1 = (f32[64,128]{1,0:T(8,128)}, f32[8,8,128]{2,1,0:T(8,128)S(1)}) custom-call(s32[3]{0:T(128)S(1)} %pad_add_fusion.place, s32[2,2]{1,0:T(2,128)S(1)} %copy-done.5, f32[8,2,64,128]{3,2,1,0:T(8,128)S(1)} %pad_maximum_fusion.1.s_own, f32[8,2,64,128]{3,2,1,0:T(8,128)} %collective-permute-done.4.s_far, ...), custom_call_target="tpu_custom_call" | custom-call | tf_op jit(solution)/shard_map/replicated_steps/pallas_call | solution.py:353
  74.9 0.1 reduce_sum.9
  75.0 0.5 add_sqrt_fusion
  (7 shorter events, 0.2 us)
Async XLA Ops:
  0.6 3.1 %copy-start = (f32[64,512]{1,0:T(8,128)S(1)}, f32[64,512]{1,0:T(8,128)}, u32[]{:S(2)}) copy-start(f32[64,512]{1,0:T(8,128)} %param.15) | copy-start | bytes 393220
  0.6 22.4 %copy-start.6 = (f32[512,65]{1,0:T(8,128)S(1)}, f32[512,65]{1,0:T(8,128)}, u32[]{:S(2)}) copy-start(f32[512,65]{1,0:T(8,128)} %constant.63.clone) | copy-start | bytes 399364
  0.7 22.4 %copy-start.9 = (f32[65,65]{1,0:T(8,128)S(1)}, f32[65,65]{1,0:T(8,128)}, u32[]{:S(2)}) copy-start(f32[65,65]{1,0:T(8,128)} %param.14) | copy-start | bytes 50704
  0.7 5.2 %collective-permute-start = (f32[1,64,128]{2,1,0:T(8,128)}, f32[1,64,128]{2,1,0:T(8,128)S(1)}, u32[]{:S(2)}, u32[]{:S(2)}) collective-permute-start(f32[1,64,128]{2,1,0:T(8,128)} %bitcast.28), channel_id=1, source_target_pairs={{0,2},{1,3},{2,0},{3,1},{4,6},{5,7},{6,4},{7,5},{8,10},{9,11},{10,... | collective-permute-start | bytes 98312 | tf_op jit(solution)/shard_map/ppermute | solution.py:304
  3.7 20.5 %copy-start.8 = (f32[512,128]{1,0:T(8,128)S(1)}, f32[512,128]{1,0:T(8,128)}, u32[]{:S(2)}) copy-start(f32[512,128]{1,0:T(8,128)} %param.16) | copy-start | bytes 786436
  6.6 8.3 %collective-permute-start.1 = (f32[1,4,64,128]{3,2,1,0:T(8,128)S(1)}, f32[1,4,64,128]{3,2,1,0:T(8,128)S(1)}, u32[]{:S(2)}, u32[]{:S(2)}) collective-permute-start(f32[1,4,64,128]{3,2,1,0:T(8,128)S(1)} %maximum_bitcast_fusion), channel_id=1, source_target_pairs={{0,16},{4,20},{8,24},{12,28},{16,0},{20,4},{24,8},{28,12},{1,17},{... | collective-permute-start | bytes 393224 | tf_op jit(solution)/shard_map/ppermute | solution.py:304
  14.9 5.0 %collective-permute-start.5 = (f32[2,2,64,128]{3,2,1,0:T(8,128)S(1)}, f32[2,2,64,128]{3,2,1,0:T(8,128)S(1)}, u32[]{:S(2)}, u32[]{:S(2)}) collective-permute-start(f32[2,2,64,128]{3,2,1,0:T(8,128)S(1)} %get-tuple-element.12), channel_id=1, source_target_pairs={{0,4},{4,0},{8,12},{12,8},{16,20},{20,16},{24,28},{28,24},{1,5},{5... | collective-permute-start | bytes 393224 | tf_op jit(solution)/shard_map/ppermute | solution.py:304
  16.5 6.4 %collective-permute-start.2 = (f32[2,2,64,128]{3,2,1,0:T(8,128)S(1)}, f32[2,2,64,128]{3,2,1,0:T(8,128)S(1)}, u32[]{:S(2)}, u32[]{:S(2)}) collective-permute-start(f32[2,2,64,128]{3,2,1,0:T(8,128)S(1)} %get-tuple-element.13), channel_id=1, source_target_pairs={{0,8},{4,12},{8,0},{12,4},{16,24},{20,28},{24,16},{28,20},{1,9},{5... | collective-permute-start | bytes 393224 | tf_op jit(solution)/shard_map/ppermute | solution.py:304
  17.2 7.0 %collective-permute-start.8 = (f32[1,512,128]{2,1,0:T(8,128)}, f32[1,512,128]{2,1,0:T(8,128)S(1)}, u32[]{:S(2)}, u32[]{:S(2)}) collective-permute-start(f32[1,512,128]{2,1,0:T(8,128)} %bitcast.26), channel_id=1, source_target_pairs={{0,2},{1,3},{2,0},{3,1},{4,6},{5,7},{6,4},{7,5},{8,10},{9,11},{10,... | collective-permute-start | bytes 786440 | tf_op jit(solution)/shard_map/ppermute | solution.py:304
  20.0 6.7 %collective-permute-start.6 = (f32[4,2,64,128]{3,2,1,0:T(8,128)S(1)}, f32[4,2,64,128]{3,2,1,0:T(8,128)S(1)}, u32[]{:S(2)}, u32[]{:S(2)}) collective-permute-start(f32[4,2,64,128]{3,2,1,0:T(8,128)S(1)} %pad_maximum_fusion.5), channel_id=1, source_target_pairs={{0,8},{4,12},{8,0},{12,4},{16,24},{20,28},{24,16},{28,20},{1,9},{5... | collective-permute-start | bytes 786440 | tf_op jit(solution)/shard_map/ppermute | solution.py:304
  22.9 6.4 %collective-permute-start.3 = (f32[4,2,64,128]{3,2,1,0:T(8,128)S(1)}, f32[4,2,64,128]{3,2,1,0:T(8,128)S(1)}, u32[]{:S(2)}, u32[]{:S(2)}) collective-permute-start(f32[4,2,64,128]{3,2,1,0:T(8,128)S(1)} %pad_maximum_fusion.4), channel_id=1, source_target_pairs={{0,4},{4,0},{8,12},{12,8},{16,20},{20,16},{24,28},{28,24},{1,5},{5... | collective-permute-start | bytes 786440 | tf_op jit(solution)/shard_map/ppermute | solution.py:304
  24.3 5.2 %copy-start.7 = (f32[512,65]{1,0:T(8,128)S(1)}, f32[512,65]{1,0:T(8,128)}, u32[]{:S(2)}) copy-start(f32[512,65]{1,0:T(8,128)} %constant.63.clone) | copy-start | bytes 399364
  24.3 9.0 %collective-permute-start.9 = (f32[2,512,128]{2,1,0:T(8,128)S(1)}, f32[2,512,128]{2,1,0:T(8,128)S(1)}, u32[]{:S(2)}, u32[]{:S(2)}) collective-permute-start(f32[2,512,128]{2,1,0:T(8,128)S(1)} %pad_maximum_fusion.3.c_own), channel_id=1, source_target_pairs={{0,1},{1,0},{2,3},{3,2},{4,5},{5,4},{6,7},{7,6},{8,9},{9,8},{10,11... | collective-permute-start | bytes 1572872 | tf_op jit(solution)/shard_map/ppermute | solution.py:304
  26.8 4.8 %copy-start.10 = (f32[256]{0:T(256)S(1)}, f32[256]{0:T(256)}, u32[]{:S(2)}) copy-start(f32[256]{0:T(256)} %constant.71) | copy-start | bytes 3076
  26.8 6.4 %collective-permute-start.7 = (f32[8,2,64,128]{3,2,1,0:T(8,128)S(1)}, f32[8,2,64,128]{3,2,1,0:T(8,128)}, u32[]{:S(2)}, u32[]{:S(2)}) collective-permute-start(f32[8,2,64,128]{3,2,1,0:T(8,128)S(1)} %pad_maximum_fusion.2.r_own), channel_id=1, source_target_pairs={{0,1},{1,0},{2,3},{3,2},{4,5},{5,4},{6,7},{7,6},{8,9},{9,8},{10,11... | collective-permute-start | bytes 1572872 | tf_op jit(solution)/shard_map/ppermute | solution.py:304
  29.4 3.8 %collective-permute-start.4 = (f32[8,2,64,128]{3,2,1,0:T(8,128)S(1)}, f32[8,2,64,128]{3,2,1,0:T(8,128)}, u32[]{:S(2)}, u32[]{:S(2)}) collective-permute-start(f32[8,2,64,128]{3,2,1,0:T(8,128)S(1)} %pad_maximum_fusion.1.s_own), channel_id=1, source_target_pairs={{0,1},{1,0},{2,3},{3,2},{4,5},{5,4},{6,7},{7,6},{8,9},{9,8},{10,11... | collective-permute-start | bytes 1572872 | tf_op jit(solution)/shard_map/ppermute | solution.py:304
  29.5 3.8 %copy-start.4 = (bf16[3,768,256]{2,1,0:T(8,128)(2,1)S(1)}, bf16[3,768,256]{2,1,0:T(8,128)(2,1)}, u32[]{:S(2)}) copy-start(bf16[3,768,256]{2,1,0:T(8,128)(2,1)} %constant.70.clone.col_inv) | copy-start | bytes 3538948
  31.6 1.7 %copy-start.2 = (bf16[3,768,256]{2,1,0:T(8,128)(2,1)S(1)}, bf16[3,768,256]{2,1,0:T(8,128)(2,1)}, u32[]{:S(2)}) copy-start(bf16[3,768,256]{2,1,0:T(8,128)(2,1)} %constant.68.clone.col_fwd) | copy-start | bytes 3538948
  31.6 2.0 %copy-start.3 = (bf16[3,256,768]{2,1,0:T(8,128)(2,1)S(1)}, bf16[3,256,768]{2,1,0:T(8,128)(2,1)}, u32[]{:S(2)}) copy-start(bf16[3,256,768]{2,1,0:T(8,128)(2,1)} %constant.69.clone.row_inv) | copy-start | bytes 3538948
  33.1 1.4 %copy-start.1 = (bf16[3,256,768]{2,1,0:T(8,128)(2,1)S(1)}, bf16[3,256,768]{2,1,0:T(8,128)(2,1)}, u32[]{:S(2)}) copy-start(bf16[3,256,768]{2,1,0:T(8,128)(2,1)} %constant.67.clone.row_fwd) | copy-start | bytes 3538948
  33.1 1.4 %copy-start.5 = (s32[2,2]{1,0:T(2,128)S(1)}, s32[2,2]{1,0:T(2,128)}, u32[]{:S(2)}) copy-start(s32[2,2]{1,0:T(2,128)} %mask.1) | copy-start | bytes 52
where the time goes:
time: 75.8 us; the launch traced here: 75.5 us
  Pallas kernels  40.4 us (53%)
  waiting for transfers between devices  16.3 us (22%)
  starting transfers between devices  11.1 us (15%)
  other arithmetic  3.28 us (4%)
  matrix products  2.33 us (3%)
  local copies, waits for them, and re-layouts  1.29 us (2%)
  between operations  0.87 us (1%)
    pallas_call x1, Pallas kernels, replicated(): pl.pallas_call(functools.partial(replicated_kernel, row_spans, (bit_place...  40.4 us
    ppermute x10, waiting for transfers between devices, swap(): lax.ppermute(value, axis, [(i, i ^ bit) for i in range(lax.axis_size(axis...  16.3 us
    ppermute x10, starting transfers between devices, swap(): lax.ppermute(value, axis, [(i, i ^ bit) for i in range(lax.axis_size(axis...  11.1 us
    dot_general x1, matrix products, tap_spectrum(): jnp.dot(jnp.dot(waves, coeffs, precision=highest), waves.T, precision=hig...  1.98 us
    another operation x2, other arithmetic, tap_spectrum(): jnp.stack([quarter[0][0], quarter[1][0] * sign[:, None], quarter[0][1] *...  1.61 us
  transfers between devices with their start and end apart: 10, of which 7 were waited for; matrix products, arithmetic and copies ran while one was open for 6% of the time, Pallas kernels for 0%

commit v1 on v0

--- a/solution.py
+++ b/solution.py
@@ -113,69 +113,115 @@
     return (solution, norm_values)
 
 
-def packed_dft():
-    place = np.arange(TILE)
-    freq = np.arange(HALF)
-    phase = 2 * np.pi * ((freq[:, None] * place[None, :]) % TILE) / TILE
-    forward = np.concatenate([np.cos(phase), np.sin(phase)], 0)
-    forward[HALF] = np.cos(np.pi * place)
-    weight = np.full((TILE, 1), 2.0 / TILE)
-    weight[0] = weight[HALF] = 1.0 / TILE
-    return forward, (forward * weight).T
-
-
-def tap_waves(band_width):
-    offset = np.arange(-band_width, band_width + 1)
-    freq = np.concatenate([np.arange(HALF), np.arange(HALF)])
-    freq[HALF] = HALF
-    phase = 2 * np.pi * ((freq[:, None] * offset[None, :]) % TILE) / TILE
-    return np.concatenate([np.cos(phase), np.sin(phase)], 0).astype(np.float32)
-
-
 def split_np(value):
     high = value.astype(jnp.bfloat16)
     return high, (value - high.astype(np.float64)).astype(jnp.bfloat16)
 
 
-def window_mats(length, band_width):
-    forward, inverse = packed_dft()
-    count = length // HALF - 1
-    mats = [[], [], [], []]
-    spans = []
+def packed_freqs(length):
+    half = length // 2
+    freq = np.concatenate([np.arange(half), np.arange(half)])
+    freq[half] = half
+    return freq
+
+
+def cyclic_mats(length):
+    half = length // 2
+    phase = 2 * np.pi * ((packed_freqs(length)[:, None] * np.arange(length)[None, :]) % length) / length
+    forward = np.concatenate([np.cos(phase[: half + 1]), np.sin(phase[half + 1 :])], 0)
+    weight = np.full((length, 1), 2.0 / length)
+    weight[0] = weight[half] = 1.0 / length
+    return forward, (forward * weight).T
+
+
+def negacyclic_mats(length):
+    half = length // 2
+    odd = 2 * np.arange(half) + 1
+    phase = 2 * np.pi * ((odd[:, None] * np.arange(length)[None, :]) % (2 * length)) / (2 * length)
+    forward = np.concatenate([np.cos(phase), np.sin(phase)], 0)
+    return forward, (forward * (2.0 / length)).T
+
+
+def row_mats(band_width):
+    half = (TILE + 2 * band_width) // 2
+    fwd, inv = [], []
+    for forward, inverse in (cyclic_mats(half), negacyclic_mats(half)):
+        fh, fl = split_np(forward)
+        gh, gl = split_np(inverse * 0.5)
+        fwd.append(np.concatenate([fh, fh, fl], 1))
+        inv.append(np.concatenate([gh, gh, gl], 1))
+    return np.stack(fwd), np.stack(inv)
+
+
+def col_mats():
+    forward, inverse = cyclic_mats(TILE)
+    return np.stack(split_np(forward.T) + split_np(inverse.T))
+
+
+def tap_waves(band_width):
+    offset = np.arange(-band_width, band_width + 1)
+    half = (TILE + 2 * band_width) // 2
+    odd = 2 * np.arange(half // 2) + 1
+    row_freq = np.concatenate([2 * packed_freqs(half), odd, odd])
+    row_phase = 2 * np.pi * ((row_freq[:, None] * offset[None, :]) % (2 * half)) / (2 * half)
+    col_phase = 2 * np.pi * ((packed_freqs(TILE)[:, None] * offset[None, :]) % TILE) / TILE
+    rows = np.stack([np.cos(row_phase), np.sin(row_phase)]).astype(np.float32)
+    cols = np.stack([np.cos(col_phase).T, np.sin(col_phase).T]).astype(np.float32)
+    return rows, cols
+
+
+def setup_kernel(coeffs, row_waves, col_waves, col_base, spectrum, col_fwd, col_inv):
+    half = spectrum.shape[2]
+    band_width = (coeffs.shape[0] - 1) // 2
+    for j in (0, 1):
+        cols = jnp.dot(coeffs[...], col_waves[j], precision=highest, preferred_element_type=jnp.float32)
+        lane = lax.broadcasted_iota(jnp.int32, (1, TILE), 1)
+        if j:
+            cols = jnp.where(lane < HALF, -cols, cols)
+        for i in (0, 1):
+            mixed = jnp.dot(row_waves[i], cols, precision=highest, preferred_element_type=jnp.float32)
+            if i:
+                place = lax.broadcasted_iota(jnp.int32, (2 * half, 1), 0) % half
+                mixed = jnp.where(place < half // 2, -mixed, mixed)
+            for part in (0, 1):
+                spectrum[part, 2 * j + i] = mixed[part * half : (part + 1) * half]
+    count = col_fwd.shape[0]
+    none = jnp.zeros((TILE, TILE), jnp.bfloat16)
     for w in range(count):
         first, last = w == 0, w == count - 1
-        taken = np.ones(TILE)
-        if first:
-            taken[TILE - band_width :] = 0
-        if last:
-            taken[:band_width] = 0
-        low = 0 if first else HALF // 2
-        high = TILE if last else TILE - HALF // 2
-        spans.append((low, high))
-        kept = np.zeros(TILE)
-        kept[low:high] = 1
-        fh, fl = split_np(forward * taken[None, :])
-        gh, gl = split_np(inverse * kept[:, None])
-        mats[0].append(np.concatenate([fh, fh, fl], 1))
-        mats[1].append(np.concatenate([fh.T, fh.T, fl.T], 0))
-        mats[2].append(np.concatenate([gh, gh, gl], 1))
-        mats[3].append(np.concatenate([gh.T, gh.T, gl.T], 0))
-    return [np.stack(m) for m in mats], spans
-
-
-def tap_spectrum(coeffs):
-    waves = jnp.asarray(tap_waves((coeffs.shape[0] - 1) // 2))
-    mixed = jnp.dot(jnp.dot(waves, coeffs, precision=highest), waves.T, precision=highest)
-    sign = np.where(np.arange(TILE) < HALF, -1.0, 1.0).astype(np.float32)
-    quarter = [[mixed[i * TILE : (i + 1) * TILE, j * TILE : (j + 1) * TILE] for j in (0, 1)] for i in (0, 1)]
-    return jnp.stack(
-        [
-            quarter[0][0],
-            quarter[1][0] * sign[:, None],
-            quarter[0][1] * sign[None, :],
-            quarter[1][1] * (sign[:, None] * sign[None, :]),
-        ]
-    )
+        for third, part in enumerate((0, 0, 1)):
+            rows = pl.ds(third * TILE, TILE)
+            col_fwd[w, rows, :] = col_base[part]
+            if first:
+                col_fwd[w, pl.ds(third * TILE + TILE - band_width, band_width), :] = none[:band_width]
+            if last:
+                col_fwd[w, pl.ds(third * TILE, band_width), :] = none[:band_width]
+            inverse = col_base[2 + part].astype(jnp.float32)
+            lane = lax.broadcasted_iota(jnp.int32, inverse.shape, 1)
+            if not first:
+                inverse = jnp.where(lane >= HALF // 2, inverse, 0.0)
+            if not last:
+                inverse = jnp.where(lane < TILE - HALF // 2, inverse, 0.0)
+            col_inv[w, rows, :] = inverse.astype(jnp.bfloat16)
+
+
+def setup(coeffs, cols):
+    band_width = (coeffs.shape[0] - 1) // 2
+    windows = cols // HALF - 1
+    waves = [jnp.asarray(v) for v in tap_waves(band_width)]
+    vmem = pl.BlockSpec(memory_space=pltpu.VMEM)
+    return pl.pallas_call(
+        setup_kernel,
+        out_shape=(
+            jax.ShapeDtypeStruct((2, 4, HALF + band_width, TILE), jnp.float32),
+            jax.ShapeDtypeStruct((windows, 3 * TILE, TILE), jnp.bfloat16),
+            jax.ShapeDtypeStruct((windows, 3 * TILE, TILE), jnp.bfloat16),
+        ),
+        in_specs=[vmem] * 4,
+        out_specs=(vmem,) * 3,
+        compiler_params=pltpu.CompilerParams(vmem_limit_bytes=16 * 1024 * 1024),
+        name="setup",
+    )(coeffs, *waves, jnp.asarray(col_mats()))
 
 
 def split(value):
@@ -187,52 +233,58 @@
     return jnp.dot(left, right, preferred_element_type=jnp.float32)
 
 
-def replicated_kernel(
-    row_spans, hx_bits, col_places, place, mask, s_own, s_far, r_own, r_far, c_own, c_far, spectrum,
-    row_fwd, col_fwd, row_inv, col_inv, out, squares,
-    state, total, w_hi, w_lo, z_hi, z_lo, y_hi, y_lo, u_hi, u_lo, t_hi, t_lo, wave, left, right,
-):
+def replicated_kernel(hx_bits, place, mask, *refs):
+    s_near, s_turn, s_far, s_both, r_near, r_turn, r_far, r_both, c_near, c_turn, c_far, c_both = refs[:12]
+    spectrum, row_fwd, col_fwd, row_inv, col_inv, out, norms = refs[12:19]
+    state, total, w_hi, w_lo, z, y_hi, y_lo, u_hi, u_lo, t_hi, t_lo, wave, left, right = refs[19:]
     rows, cols = state.shape
-    row_windows, col_windows = row_fwd.shape[0], col_fwd.shape[0]
+    col_windows = col_fwd.shape[0]
+    half = row_fwd.shape[1]
+    quarter = half // 2
+    band_width = half - HALF
     tile_rows, tile_cols = rows // TILE, cols // TILE
-    block_rows, block_cols = s_own.shape[-2:]
+    block_rows, block_cols = s_near.shape[-2:]
+    near_count = s_near.shape[0]
     here_x, here_y, here_c = place[0], place[1], place[2]
-    for pos in range(s_own.shape[0]):
+    for pos in range(2 * near_count):
         s_row = (here_x ^ hx_bits[0][pos]) * block_rows
         s_row = pl.multiple_of(s_row, block_rows)
-        for far, ref in ((0, s_own), (1, s_far)):
-            for k in range(s_own.shape[1]):
+        for far, ref in enumerate((s_near, s_far) if pos < near_count else (s_turn, s_both)):
+            for k in range(ref.shape[1]):
                 s_col = ((here_y ^ k) * 2 + (here_c ^ far)) * block_cols
                 s_col = pl.multiple_of(s_col, block_cols)
-                value = ref[pos, k]
+                value = ref[pos % near_count, k]
                 state[pl.ds(s_row, block_rows), pl.ds(s_col, block_cols)] = value
                 total[pl.ds(s_row, block_rows), pl.ds(s_col, block_cols)] = value
                 high, low = split(value)
                 w_hi[pl.ds(s_row, block_rows), pl.ds(s_col, block_cols)] = high
                 w_lo[pl.ds(s_row, block_rows), pl.ds(s_col, block_cols)] = low
     share = TILE // block_rows
-    for pos in range(r_own.shape[0]):
+    for pos in range(2 * near_count):
         index = here_x ^ hx_bits[1][pos]
         a = index // share
         sub = pl.multiple_of((index % share) * block_rows, block_rows)
-        for far, ref in ((0, r_own), (1, r_far)):
+        for far, ref in enumerate((r_near, r_far) if pos < near_count else (r_turn, r_both)):
             side = here_c ^ far
-            for k in range(r_own.shape[1]):
+            for k in range(ref.shape[1]):
                 lane = side * (cols // 2) + k * LANES
                 b = lane // TILE
                 at = pl.multiple_of(lane % TILE, LANES)
-                high, low = split(ref[pos, k] * mask[a, b].astype(jnp.float32))
+                high, low = split(ref[pos % near_count, k] * mask[a, b].astype(jnp.float32))
                 for third, part in enumerate((high, high, low)):
                     left[a, b, pl.ds(sub, block_rows), pl.ds(pl.multiple_of(at + third * TILE, LANES), LANES)] = part
-    for k in range(c_own.shape[0]):
-        for far, ref in ((0, c_own), (1, c_far)):
+    for k in range(2 * c_near.shape[0]):
+        for far, ref in enumerate((c_near, c_far) if k < c_near.shape[0] else (c_turn, c_both)):
             lane = ((here_y ^ k) * 2 + (here_c ^ far)) * block_cols
             b = lane // TILE
             at = pl.multiple_of(lane % TILE, block_cols)
             for a in range(tile_rows):
-                high, low = split(ref[k, pl.ds(a * TILE, TILE), :])
+                high, low = split(ref[k % c_near.shape[0], pl.ds(a * TILE, TILE), :])
                 for third, part in enumerate((high, high, low)):
                     right[a, b, pl.ds(third * TILE, TILE), pl.ds(at, block_cols)] = part
+
+    for edge in (0, rows + band_width):
+        z[pl.ds(edge, band_width), :] = jnp.zeros((band_width, z.shape[1]), jnp.float32)
 
     def triple(hi_ref, lo_ref, row_at, col_at, axis):
         high = hi_ref[row_at, col_at]
@@ -243,31 +295,38 @@
         take = jnp.where(k == 0, 1.0, relax_step)
         every = pl.ds(0, rows)
         for b in range(col_windows):
-            z = dot32(triple(w_hi, w_lo, every, pl.ds(b * HALF, TILE), 1), col_fwd[b])
-            z_hi[:, pl.ds(b * TILE, TILE)], z_lo[:, pl.ds(b * TILE, TILE)] = split(z)
-        for a in range(row_windows):
+            at = pl.ds(b * TILE, TILE)
+            z[pl.ds(band_width, rows), at] = dot32(triple(w_hi, w_lo, every, pl.ds(b * HALF, TILE), 1), col_fwd[b])
+        for a in range(tile_rows):
             for b in range(col_windows):
-                cells = triple(z_hi, z_lo, pl.ds(a * HALF, TILE), pl.ds(b * TILE, TILE), 0)
-                wave[...] = dot32(row_fwd[a], cells)
-                for i in (0, 1):
-                    for j in (0, 1):
-                        ri, rj = pl.ds(i * HALF, HALF), pl.ds((1 - i) * HALF, HALF)
-                        ci, cj = pl.ds(j * HALF, HALF), pl.ds((1 - j) * HALF, HALF)
-                        y = (
-                            spectrum[0, ri, ci] * wave[ri, ci]
-                            + spectrum[1, ri, ci] * wave[rj, ci]
-                            + spectrum[2, ri, ci] * wave[ri, cj]
-                            + spectrum[3, ri, ci] * wave[rj, cj]
-                        )
-                        to = pl.ds(a * TILE + i * HALF, HALF), pl.ds(b * TILE + j * HALF, HALF)
-                        y_hi[to], y_lo[to] = split(y)
-        for a in range(row_windows):
-            low, high = row_spans[a]
+                cb = pl.ds(b * TILE, TILE)
+                upper = z[pl.ds(a * TILE, half), cb]
+                lower = z[pl.ds(a * TILE + half, half), cb]
+                for part, cells in enumerate((upper + lower, upper - lower)):
+                    high, low = split(cells)
+                    wave[part] = dot32(row_fwd[part], jnp.concatenate([high, low, high], 0))
+                    for i in (0, 1):
+                        for j in (0, 1):
+                            ri, rj = pl.ds(i * quarter, quarter), pl.ds((1 - i) * quarter, quarter)
+                            ci, cj = pl.ds(j * HALF, HALF), pl.ds((1 - j) * HALF, HALF)
+                            y = (
+                                spectrum[part, 0, ri, ci] * wave[part, ri, ci]
+                                + spectrum[part, 1, ri, ci] * wave[part, rj, ci]
+                                + spectrum[part, 2, ri, ci] * wave[part, ri, cj]
+                                + spectrum[part, 3, ri, ci] * wave[part, rj, cj]
+                            )
+                            to = pl.ds((2 * a + part) * half + i * quarter, quarter), pl.ds(b * TILE + j * HALF, HALF)
+                            y_hi[to], y_lo[to] = split(y)
+        for a in range(tile_rows):
             for b in range(col_windows):
-                cells = triple(y_hi, y_lo, pl.ds(a * TILE, TILE), pl.ds(b * TILE, TILE), 0)
-                u = dot32(row_inv[a, low:high, :], cells)
-                to = pl.ds(a * HALF + low, high - low), pl.ds(b * TILE, TILE)
-                u_hi[to], u_lo[to] = split(u)
+                cb = pl.ds(b * TILE, TILE)
+                sums, diffs = (
+                    dot32(row_inv[part], triple(y_hi, y_lo, pl.ds((2 * a + part) * half, half), cb, 0)) for part in (0, 1)
+                )
+                upper = sums[band_width:] + diffs[band_width:]
+                lower = sums[: half - band_width] - diffs[: half - band_width]
+                u_hi[pl.ds(a * TILE, HALF), cb], u_lo[pl.ds(a * TILE, HALF), cb] = split(upper)
+                u_hi[pl.ds(a * TILE + HALF, HALF), cb], u_lo[pl.ds(a * TILE + HALF, HALF), cb] = split(lower)
         for a in range(tile_rows):
             for b in range(tile_cols):
                 at = pl.ds(a * TILE, TILE), pl.ds(b * TILE, TILE)
@@ -291,10 +350,11 @@
                 total[ra, cj] = total[ra, cj] + relax_step * residual
                 w_hi[ra, cj], w_lo[ra, cj] = split(residual)
                 square = square + jnp.sum((residual * residual).reshape(TILE // 8, 8, LANES), 0)
-        squares[k] = square
-        return carry
-
-    lax.fori_loop(0, ITERS, step, 0)
+        return jnp.where(norm_lane == k, jnp.sum(square), carry)
+
+    norm_lane = lax.broadcasted_iota(jnp.int32, norms.shape, 1)
+    summed = lax.fori_loop(0, ITERS, step, jnp.zeros(norms.shape, jnp.float32))
+    norms[...] = jnp.sqrt(summed / (rows * cols) + tiny_square)
     own_row = pl.multiple_of(here_x * block_rows, block_rows)
     own_col = pl.multiple_of((here_y * 2 + here_c) * block_cols, block_cols)
     out[...] = total[pl.ds(own_row, block_rows), pl.ds(own_col, block_cols)]
@@ -327,51 +387,52 @@
     turned = down[:-2] + down[-2:][::-1]
     y_bits = [1 << i for i in range(1, hy_size.bit_length() - 1)]
     s_part = doubled(source[None], "hy", y_bits)
-    c_part = doubled(col_factor[None], "hy", y_bits)
     r_half = lax.dynamic_slice_in_dim(row_factor, (index_y % 2) * (cols // 2), cols // 2, 1)
-    r_part = r_half.reshape(block_rows, -1, LANES).swapaxes(0, 1)
-    s_count = s_part.shape[0]
-    both = jnp.concatenate([s_part, r_part], 0)[None]
-    both = doubled(both, "hx", down[:-2])
-    s_all = doubled(both[:, :s_count], "hx", down[-2:])
-    r_all = doubled(both[:, s_count:], "hx", turned[-2:])
-    far = [swap(v, "hy", 1) for v in (s_all, r_all, c_part)]
-    spectrum = tap_spectrum(coeffs)
-    mats, row_spans = window_mats(rows, band_width)
-    col_mats, _ = window_mats(cols, band_width)
-    weights = [jnp.asarray(m) for m in (mats[0], col_mats[1], mats[2], col_mats[3])]
+    r_near = doubled(r_half.reshape(block_rows, -1, LANES).swapaxes(0, 1)[None], "hx", turned[:-1])
+    s_near = doubled(s_part[None], "hx", down[:-2])
+    s_near = doubled(s_near, "hx", down[-2:-1])
+    s_near, coeffs = lax.optimization_barrier((s_near, coeffs))
+    ready = setup(coeffs, cols)
+    c_near = doubled(col_factor[None], "hy", y_bits[:-1])
+    turns = [swap(s_near, "hx", down[-1]), swap(r_near, "hx", turned[-1]), swap(c_near, "hy", y_bits[-1])]
+    s_held, *ready = lax.optimization_barrier((s_near, *ready))
+    pieces = []
+    for near, held, turn in zip((s_near, r_near, c_near), (s_held, r_near, c_near), turns):
+        pieces += [near, turn, swap(held, "hy", 1), swap(turn, "hy", 1)]
+    spectrum, col_fwd, col_inv = ready
+    row_fwd, row_inv = (jnp.asarray(m) for m in row_mats(band_width))
     place = jnp.stack([index_x, index_y // 2, index_y % 2])
-    row_windows, col_windows = rows // HALF - 1, cols // HALF - 1
+    half, col_windows = HALF + band_width, cols // HALF - 1
     vmem = pl.BlockSpec(memory_space=pltpu.VMEM)
     smem = pl.BlockSpec(memory_space=pltpu.SMEM)
     f32, bf16 = jnp.float32, jnp.bfloat16
-    shapes = [((rows, cols), f32)] * 2 + [((rows, cols), bf16)] * 2 + [((rows, col_windows * TILE), bf16)] * 2
-    shapes += [((row_windows * TILE, col_windows * TILE), bf16)] * 2 + [((rows, col_windows * TILE), bf16)] * 2
-    shapes += [((rows, cols), bf16)] * 2 + [((TILE, TILE), f32)]
     tiles = (rows // TILE, cols // TILE)
+    shapes = [((rows, cols), f32)] * 2 + [((rows, cols), bf16)] * 2
+    shapes += [((rows + 2 * band_width, col_windows * TILE), f32)]
+    shapes += [((2 * half * tiles[0], col_windows * TILE), bf16)] * 2 + [((rows, col_windows * TILE), bf16)] * 2
+    shapes += [((rows, cols), bf16)] * 2 + [((2, half, TILE), f32)]
     shapes += [(tiles + (TILE, 3 * TILE), bf16), (tiles + (3 * TILE, TILE), bf16)]
-    result, squares = pl.pallas_call(
-        functools.partial(replicated_kernel, row_spans, (bit_places(down), bit_places(turned)), None),
+    result, norms = pl.pallas_call(
+        functools.partial(replicated_kernel, (bit_places(down), bit_places(turned))),
         out_shape=(
             jax.ShapeDtypeStruct((block_rows, block_cols), f32),
-            jax.ShapeDtypeStruct((ITERS, 8, LANES), f32),
+            jax.ShapeDtypeStruct((1, ITERS), f32),
         ),
-        in_specs=[smem, smem] + [vmem] * 11,
+        in_specs=[smem, smem] + [vmem] * 17,
         out_specs=(vmem, vmem),
         scratch_shapes=[pltpu.VMEM(*s) for s in shapes],
-        compiler_params=pltpu.CompilerParams(vmem_limit_bytes=40 * 1024 * 1024),
+        compiler_params=pltpu.CompilerParams(vmem_limit_bytes=50 * 1024 * 1024),
         name="replicated_steps",
-    )(place, tile_mask, s_all, far[0], r_all, far[1], c_part, far[2], spectrum, *weights)
-    norm_values = jnp.sqrt(jnp.sum(squares, (1, 2)) / (rows * cols) + tiny_square)
-    return result, norm_values
+    )(place, tile_mask, *pieces, spectrum, row_fwd, col_fwd, row_inv, col_inv)
+    return result, norms[0]
 
 
 def fits(rows, cols, block_rows, block_cols, band_width, hx_size, hy_size):
     powers = all(n & (n - 1) == 0 for n in (hx_size, hy_size))
     whole = rows % TILE == 0 and cols % TILE == 0 and rows > TILE and cols > TILE
     aligned = TILE % block_rows == 0 and block_rows % 16 == 0 and block_cols == LANES and cols % (2 * LANES) == 0
-    small = rows * cols * 4 <= GRID_BYTES and 4 * band_width <= TILE
-    return powers and whole and aligned and small and hx_size >= 4 and hy_size >= 2
+    small = rows * cols * 4 <= GRID_BYTES and 4 * band_width <= TILE and band_width % 32 == 0
+    return powers and whole and aligned and small and hx_size >= 4 and hy_size >= 4
 
 
 def local(source, coeffs, row_factor, col_factor, tile_mask):

time: 75.8 us -> 65.3 us (0.86); the launches traced: 75.5 us -> 64.2 us
  waiting for transfers between devices: 16.3 us -> 3.72 us
  starting transfers between devices: 11.1 us -> 16.5 us
  other arithmetic: 3.28 us -> 0.9 us
  matrix products: 2.33 us -> 0 us
  local copies, waits for them, and re-layouts: 1.29 us -> 3.16 us
  Pallas kernels: 40.4 us -> 39.2 us
    ppermute x10 -> x14, waiting for transfers between devices: 16.3 us -> 3.72 us  [swap(): lax.ppermute(value, axis, [(i, i ^ bit) for i in range(lax.axis_size(axis...]
    ppermute x10 -> x14, starting transfers between devices: 11.1 us -> 16.5 us  [swap(): lax.ppermute(value, axis, [(i, i ^ bit) for i in range(lax.axis_size(axis...]
    dot_general x2 -> x0, matrix products: 2.33 us -> none  [the longest x1 1.98 us: tap_spectrum(): jnp.dot(jnp.dot(waves, coeffs, precision=highest), waves.T, precision=hig...]
    unnamed x22 -> x24, local copies, waits for them, and re-layouts: 1.29 us -> 3.16 us
    another operation x2 -> x0, other arithmetic: 1.61 us -> none  [tap_spectrum(): jnp.stack([quarter[0][0], quarter[1][0] * sign[:, None], quarter[0][1] *...]
    pallas_call x1 -> x2, Pallas kernels: 40.4 us -> 39.2 us  [the longest x1 37.3 us: replicated(): pl.pallas_call(functools.partial(replicated_kernel, (bit_places(down), bi...]
  transfers between devices with their start and end apart: 10 -> 14, of which waited for: 7 -> 6; matrix products, arithmetic and copies ran while one was open for 6% -> 1% of each run, Pallas kernels for 0% -> 3%
where the time goes in v1:
time: 65.3 us; the launch traced here: 64.2 us
  Pallas kernels  39.2 us (60%)
  starting transfers between devices  16.5 us (25%)
  waiting for transfers between devices  3.72 us (6%)
  local copies, waits for them, and re-layouts  3.16 us (5%)
  other arithmetic  0.9 us (1%)
  between operations  0.78 us (1%)
    pallas_call x1, Pallas kernels, replicated(): pl.pallas_call(functools.partial(replicated_kernel, (bit_places(down), bi...  37.3 us
    ppermute x14, starting transfers between devices, swap(): lax.ppermute(value, axis, [(i, i ^ bit) for i in range(lax.axis_size(axis...  16.5 us
    ppermute x14, waiting for transfers between devices, swap(): lax.ppermute(value, axis, [(i, i ^ bit) for i in range(lax.axis_size(axis...  3.72 us
    unnamed x24, local copies, waits for them, and re-layouts  3.16 us
    pallas_call x1, Pallas kernels, setup(): pl.pallas_call(setup_kernel, out_shape=(jax.ShapeDtypeStruct((2, 4, HALF...  1.85 us
  transfers between devices with their start and end apart: 14, of which 6 were waited for; matrix products, arithmetic and copies ran while one was open for 1% of the time, Pallas kernels for 3%

profile of v1, /device:TPU:0, one launch (start us, length us, event | category | flops | bytes accessed | tf_op | source)
XLA Modules:
  0.0 64.2 jit_solution(10585105616051097742)
XLA Ops:
  0.6 0.0 copy-start
  0.6 0.0 copy-start.4
  0.7 0.0 copy-start.7
  0.7 0.0 copy-start.10
  0.7 3.1 %collective-permute-start = (f32[1,64,128]{2,1,0:T(8,128)}, f32[1,64,128]{2,1,0:T(8,128)S(1)}, u32[]{:S(2)}, u32[]{:S(2)}) collective-permute-start(f32[1,64,128]{2,1,0:T(8,128)} %bitcast.20), channel_id=1, source_target_pairs={{0,2},{1,3},{2,0},{3,1},{4,6},{5,7},{6,4},{7,5},{8,10},{9,11},{10,... | collective-permute-start | bytes 98312 | tf_op jit(solution)/shard_map/ppermute | solution.py:364
  3.7 0.0 copy-done
  3.7 0.0 copy-start.9
  3.8 2.7 %collective-permute-start.6 = (f32[1,2,64,128]{3,2,1,0:T(8,128)S(1)}, f32[1,2,64,128]{3,2,1,0:T(8,128)S(1)}, u32[]{:S(2)}, u32[]{:S(2)}) collective-permute-start(f32[1,2,64,128]{3,2,1,0:T(8,128)S(1)} %bitcast_bitcast_fusion), channel_id=1, source_target_pairs={{0,16},{4,20},{8,24},{12,28},{16,0},{20,4},{24,8},{28,12},{1,17},{... | collective-permute-start | bytes 196616 | tf_op jit(solution)/shard_map/ppermute | solution.py:364
  6.4 0.0 collective-permute-done
  6.4 0.8 %maximum_bitcast_fusion = f32[1,2,64,128]{3,2,1,0:T(8,128)S(1)} fusion(f32[1,64,128]{2,1,0:T(8,128)S(1)} %collective-permute-done, f32[1,64,128]{2,1,0:T(8,128)} %bitcast.21), kind=kLoop, calls=%fused_computation.5 | loop fusion | flops 16384 | bytes 131072 | tf_op jit(solution)/shard_map/broadcast_in_dim | solution.py:392
  7.2 2.5 %collective-permute-start.1 = (f32[1,2,64,128]{3,2,1,0:T(8,128)S(1)}, f32[1,2,64,128]{3,2,1,0:T(8,128)S(1)}, u32[]{:S(2)}, u32[]{:S(2)}) collective-permute-start(f32[1,2,64,128]{3,2,1,0:T(8,128)S(1)} %maximum_bitcast_fusion), channel_id=1, source_target_pairs={{0,16},{4,20},{8,24},{12,28},{16,0},{20,4},{24,8},{28,12},{1,17},{... | collective-permute-start | bytes 196616 | tf_op jit(solution)/shard_map/ppermute | solution.py:364
  9.7 0.0 collective-permute-done.6
  9.7 0.0 copy-start.5
  9.7 0.0 copy-start.6
  9.7 0.0 copy-start.8
  9.8 0.0 copy-start.11
  9.8 1.6 %collective-permute-start.7 = (f32[2,2,64,128]{3,2,1,0:T(8,128)S(1)}, f32[2,2,64,128]{3,2,1,0:T(8,128)S(1)}, u32[]{:S(2)}, u32[]{:S(2)}) collective-permute-start(f32[2,2,64,128]{3,2,1,0:T(8,128)S(1)} %pad_maximum_fusion.3), channel_id=1, source_target_pairs={{0,4},{4,0},{8,12},{12,8},{16,20},{20,16},{24,28},{28,24},{1,5},{5... | collective-permute-start | bytes 393224 | tf_op jit(solution)/shard_map/ppermute | solution.py:364
  11.3 1.0 %collective-permute-done.1 = f32[1,2,64,128]{3,2,1,0:T(8,128)S(1)} collective-permute-done((f32[1,2,64,128]{3,2,1,0:T(8,128)S(1)}, f32[1,2,64,128]{3,2,1,0:T(8,128)S(1)}, u32[]{:S(2)}, u32[]{:S(2)}) %collective-permute-start.1) | collective-permute-done | bytes 65568 | tf_op jit(solution)/shard_map/ppermute | solution.py:364
  12.4 1.6 %collective-permute-start.2 = (f32[2,2,64,128]{3,2,1,0:T(8,128)S(1)}, f32[2,2,64,128]{3,2,1,0:T(8,128)S(1)}, u32[]{:S(2)}, u32[]{:S(2)}) collective-permute-start(f32[2,2,64,128]{3,2,1,0:T(8,128)S(1)} %pad_maximum_fusion.2), channel_id=1, source_target_pairs={{0,8},{4,12},{8,0},{12,4},{16,24},{20,28},{24,16},{28,20},{1,9},{5... | collective-permute-start | bytes 393224 | tf_op jit(solution)/shard_map/ppermute | solution.py:364
  14.0 0.0 collective-permute-start.12
  14.0 1.5 %collective-permute-start.11 = (f32[1,512,128]{2,1,0:T(8,128)}, f32[1,512,128]{2,1,0:T(8,128)S(1)}, u32[]{:S(2)}, u32[]{:S(2)}) collective-permute-start(f32[1,512,128]{2,1,0:T(8,128)} %bitcast.18), channel_id=1, source_target_pairs={{0,2},{1,3},{2,0},{3,1},{4,6},{5,7},{6,4},{7,5},{8,10},{9,11},{10,... | collective-permute-start | bytes 786440 | tf_op jit(solution)/shard_map/ppermute | solution.py:364
  15.5 0.0 collective-permute-done.7
  15.5 1.0 %collective-permute-start.8 = (f32[4,2,64,128]{3,2,1,0:T(8,128)S(1)}, f32[4,2,64,128]{3,2,1,0:T(8,128)S(1)}, u32[]{:S(2)}, u32[]{:S(2)}) collective-permute-start(f32[4,2,64,128]{3,2,1,0:T(8,128)S(1)} %pad_maximum_fusion.1.refs_4_), channel_id=1, source_target_pairs={{0,8},{4,12},{8,0},{12,4},{16,24},{20,28},{24,16},{28,20},{1,9},{5... | collective-permute-start | bytes 786440 | tf_op jit(solution)/shard_map/ppermute | solution.py:364
  16.5 0.9 %collective-permute-done.2 = f32[2,2,64,128]{3,2,1,0:T(8,128)S(1)} collective-permute-done((f32[2,2,64,128]{3,2,1,0:T(8,128)S(1)}, f32[2,2,64,128]{3,2,1,0:T(8,128)S(1)}, u32[]{:S(2)}, u32[]{:S(2)}) %collective-permute-start.2) | collective-permute-done | bytes 131104 | tf_op jit(solution)/shard_map/ppermute | solution.py:364
  17.4 1.6 %collective-permute-start.3 = (f32[4,2,64,128]{3,2,1,0:T(8,128)S(1)}, f32[4,2,64,128]{3,2,1,0:T(8,128)S(1)}, u32[]{:S(2)}, u32[]{:S(2)}) collective-permute-start(f32[4,2,64,128]{3,2,1,0:T(8,128)S(1)} %pad_maximum_fusion.refs_0_), channel_id=1, source_target_pairs={{0,4},{4,0},{8,12},{12,8},{16,20},{20,16},{24,28},{28,24},{1,5},{5... | collective-permute-start | bytes 786440 | tf_op jit(solution)/shard_map/ppermute | solution.py:364
  19.0 0.0 collective-permute-start.9
  19.0 0.0 copy-done.4
  19.0 0.0 copy-done.7
  19.0 0.0 copy-done.10
  19.0 0.0 copy-done.9
  19.0 1.8 %setup.1 = (f32[2,4,160,256]{3,2,1,0:T(8,128)S(1)}, bf16[3,768,256]{2,1,0:T(8,128)(2,1)S(1)}, bf16[3,768,256]{2,1,0:T(8,128)(2,1)S(1)}) custom-call(f32[65,65]{1,0:T(8,128)S(1)} %copy-done.10, f32[2,320,65]{2,1,0:T(8,128)S(1)} %copy-done.7, f32[2,65,256]{2,1,0:T(8,128)S(1)} %copy-done.9, bf16[4,256,256]{2,1,0:T(8,128)(2,1)S(1)} %copy-done.4), custom_call_target="tpu_custom_call" | custom-call | tf_op jit(solution)/shard_map/setup/pallas_call | solution.py:213
  20.9 0.0 copy-start.1
  20.9 1.1 %copy-done.1 = f32[2,4,160,256]{3,2,1,0:T(8,128)} copy-done((f32[2,4,160,256]{3,2,1,0:T(8,128)}, f32[2,4,160,256]{3,2,1,0:T(8,128)S(1)}, u32[]{:S(2)}) %copy-start.1) | copy-done | bytes 1310744
  21.9 0.0 copy-start.2
  21.9 1.0 %copy-done.2 = bf16[3,768,256]{2,1,0:T(8,128)(2,1)} copy-done((bf16[3,768,256]{2,1,0:T(8,128)(2,1)}, bf16[3,768,256]{2,1,0:T(8,128)(2,1)S(1)}, u32[]{:S(2)}) %copy-start.2) | copy-done | bytes 1179672
  23.0 0.0 copy-start.3
  23.0 1.0 %copy-done.3 = bf16[3,768,256]{2,1,0:T(8,128)(2,1)} copy-done((bf16[3,768,256]{2,1,0:T(8,128)(2,1)}, bf16[3,768,256]{2,1,0:T(8,128)(2,1)S(1)}, u32[]{:S(2)}) %copy-start.3) | copy-done | bytes 1179672
  24.0 0.0 collective-permute-done.12.refs_10_
  24.0 0.5 collective-permute-start.4
  24.5 0.0 collective-permute-done.11.refs_9_
  24.5 0.1 collective-permute-start.13
  24.6 0.0 collective-permute-done.8.refs_5_
  24.6 0.4 collective-permute-start.10
  25.0 0.0 collective-permute-done.3.refs_1_
  25.0 0.1 collective-permute-start.5
  25.1 0.1 pad_add_fusion.place
  25.1 0.0 collective-permute-done.9.refs_6_
  25.1 0.5 collective-permute-done.4.refs_2_
  25.6 0.4 collective-permute-done.13.refs_11_
  26.0 0.4 collective-permute-done.10.refs_7_
  26.4 0.5 collective-permute-done.5.refs_3_
  26.9 0.0 copy-done.5
  26.9 0.0 copy-done.6
  26.9 0.0 copy-done.8
  26.9 0.0 copy-done.11
  26.9 37.3 %replicated_steps.1 = (f32[64,128]{1,0:T(8,128)}, f32[1,8]{1,0:T(1,128)}) custom-call(s32[3]{0:T(128)S(1)} %pad_add_fusion.place, s32[2,2]{1,0:T(2,128)S(1)} %copy-done.11, f32[4,2,64,128]{3,2,1,0:T(8,128)S(1)} %pad_maximum_fusion.refs_0_, f32[4,2,64,128]{3,2,1,0:T(8,128)S(1)} %collective-permute-done.3.refs_1_, ...), custom_call_target="tpu_custom_call" | custom-call | tf_op jit(solution)/shard_map/replicated_steps/pallas_call | solution.py:415
  (5 shorter events, 0.1 us)
Async XLA Ops:
  0.6 3.1 %copy-start = (f32[64,512]{1,0:T(8,128)S(1)}, f32[64,512]{1,0:T(8,128)}, u32[]{:S(2)}) copy-start(f32[64,512]{1,0:T(8,128)} %param.12) | copy-start | bytes 393220
  0.6 18.3 %copy-start.4 = (bf16[4,256,256]{2,1,0:T(8,128)(2,1)S(1)}, bf16[4,256,256]{2,1,0:T(8,128)(2,1)}, u32[]{:S(2)}) copy-start(bf16[4,256,256]{2,1,0:T(8,128)(2,1)} %constant.52.clone.col_base) | copy-start | bytes 1572868
  0.7 18.3 %copy-start.7 = (f32[2,320,65]{2,1,0:T(8,128)S(1)}, f32[2,320,65]{2,1,0:T(8,128)}, u32[]{:S(2)}) copy-start(f32[2,320,65]{2,1,0:T(8,128)} %constant.50.clone.row_waves) | copy-start | bytes 499204
  0.7 18.3 %copy-start.10 = (f32[65,65]{1,0:T(8,128)S(1)}, f32[65,65]{1,0:T(8,128)}, u32[]{:S(2)}) copy-start(f32[65,65]{1,0:T(8,128)} %coeffs) | copy-start | bytes 50704
  0.7 5.7 %collective-permute-start = (f32[1,64,128]{2,1,0:T(8,128)}, f32[1,64,128]{2,1,0:T(8,128)S(1)}, u32[]{:S(2)}, u32[]{:S(2)}) collective-permute-start(f32[1,64,128]{2,1,0:T(8,128)} %bitcast.20), channel_id=1, source_target_pairs={{0,2},{1,3},{2,0},{3,1},{4,6},{5,7},{6,4},{7,5},{8,10},{9,11},{10,... | collective-permute-start | bytes 98312 | tf_op jit(solution)/shard_map/ppermute | solution.py:364
  3.7 15.3 %copy-start.9 = (f32[2,65,256]{2,1,0:T(8,128)S(1)}, f32[2,65,256]{2,1,0:T(8,128)}, u32[]{:S(2)}) copy-start(f32[2,65,256]{2,1,0:T(8,128)} %constant.51.clone.col_waves) | copy-start | bytes 399364
  3.8 5.9 %collective-permute-start.6 = (f32[1,2,64,128]{3,2,1,0:T(8,128)S(1)}, f32[1,2,64,128]{3,2,1,0:T(8,128)S(1)}, u32[]{:S(2)}, u32[]{:S(2)}) collective-permute-start(f32[1,2,64,128]{3,2,1,0:T(8,128)S(1)} %bitcast_bitcast_fusion), channel_id=1, source_target_pairs={{0,16},{4,20},{8,24},{12,28},{16,0},{20,4},{24,8},{28,12},{1,17},{... | collective-permute-start | bytes 196616 | tf_op jit(solution)/shard_map/ppermute | solution.py:364
  7.2 5.2 %collective-permute-start.1 = (f32[1,2,64,128]{3,2,1,0:T(8,128)S(1)}, f32[1,2,64,128]{3,2,1,0:T(8,128)S(1)}, u32[]{:S(2)}, u32[]{:S(2)}) collective-permute-start(f32[1,2,64,128]{3,2,1,0:T(8,128)S(1)} %maximum_bitcast_fusion), channel_id=1, source_target_pairs={{0,16},{4,20},{8,24},{12,28},{16,0},{20,4},{24,8},{28,12},{1,17},{... | collective-permute-start | bytes 196616 | tf_op jit(solution)/shard_map/ppermute | solution.py:364
  9.7 17.2 %copy-start.5 = (bf16[2,160,480]{2,1,0:T(8,128)(2,1)S(1)}, bf16[2,160,480]{2,1,0:T(8,128)(2,1)}, u32[]{:S(2)}) copy-start(bf16[2,160,480]{2,1,0:T(8,128)(2,1)} %constant.54.clone.refs_15_) | copy-start | bytes 921604
  9.7 17.2 %copy-start.6 = (bf16[2,160,480]{2,1,0:T(8,128)(2,1)S(1)}, bf16[2,160,480]{2,1,0:T(8,128)(2,1)}, u32[]{:S(2)}) copy-start(bf16[2,160,480]{2,1,0:T(8,128)(2,1)} %constant.53.clone.refs_13_) | copy-start | bytes 921604
  9.7 17.2 %copy-start.8 = (f32[512,128]{1,0:T(8,128)S(1)}, f32[512,128]{1,0:T(8,128)}, u32[]{:S(2)}) copy-start(f32[512,128]{1,0:T(8,128)} %param.13) | copy-start | bytes 786436
  9.8 17.2 %copy-start.11 = (s32[2,2]{1,0:T(2,128)S(1)}, s32[2,2]{1,0:T(2,128)}, u32[]{:S(2)}) copy-start(s32[2,2]{1,0:T(2,128)} %mask.1) | copy-start | bytes 52
  9.8 5.7 %collective-permute-start.7 = (f32[2,2,64,128]{3,2,1,0:T(8,128)S(1)}, f32[2,2,64,128]{3,2,1,0:T(8,128)S(1)}, u32[]{:S(2)}, u32[]{:S(2)}) collective-permute-start(f32[2,2,64,128]{3,2,1,0:T(8,128)S(1)} %pad_maximum_fusion.3), channel_id=1, source_target_pairs={{0,4},{4,0},{8,12},{12,8},{16,20},{20,16},{24,28},{28,24},{1,5},{5... | collective-permute-start | bytes 393224 | tf_op jit(solution)/shard_map/ppermute | solution.py:364
  12.4 5.0 %collective-permute-start.2 = (f32[2,2,64,128]{3,2,1,0:T(8,128)S(1)}, f32[2,2,64,128]{3,2,1,0:T(8,128)S(1)}, u32[]{:S(2)}, u32[]{:S(2)}) collective-permute-start(f32[2,2,64,128]{3,2,1,0:T(8,128)S(1)} %pad_maximum_fusion.2), channel_id=1, source_target_pairs={{0,8},{4,12},{8,0},{12,4},{16,24},{20,28},{24,16},{28,20},{1,9},{5... | collective-permute-start | bytes 393224 | tf_op jit(solution)/shard_map/ppermute | solution.py:364
  14.0 10.0 %collective-permute-start.12 = (f32[1,512,128]{2,1,0:T(8,128)}, f32[1,512,128]{2,1,0:T(8,128)S(1)}, u32[]{:S(2)}, u32[]{:S(2)}) collective-permute-start(f32[1,512,128]{2,1,0:T(8,128)} %bitcast.17), channel_id=1, source_target_pairs={{0,1},{1,0},{2,3},{3,2},{4,5},{5,4},{6,7},{7,6},{8,9},{9,8},{10,11... | collective-permute-start | bytes 786440 | tf_op jit(solution)/shard_map/ppermute | solution.py:364
  14.0 10.5 %collective-permute-start.11 = (f32[1,512,128]{2,1,0:T(8,128)}, f32[1,512,128]{2,1,0:T(8,128)S(1)}, u32[]{:S(2)}, u32[]{:S(2)}) collective-permute-start(f32[1,512,128]{2,1,0:T(8,128)} %bitcast.18), channel_id=1, source_target_pairs={{0,2},{1,3},{2,0},{3,1},{4,6},{5,7},{6,4},{7,5},{8,10},{9,11},{10,... | collective-permute-start | bytes 786440 | tf_op jit(solution)/shard_map/ppermute | solution.py:364
  15.5 9.1 %collective-permute-start.8 = (f32[4,2,64,128]{3,2,1,0:T(8,128)S(1)}, f32[4,2,64,128]{3,2,1,0:T(8,128)S(1)}, u32[]{:S(2)}, u32[]{:S(2)}) collective-permute-start(f32[4,2,64,128]{3,2,1,0:T(8,128)S(1)} %pad_maximum_fusion.1.refs_4_), channel_id=1, source_target_pairs={{0,8},{4,12},{8,0},{12,4},{16,24},{20,28},{24,16},{28,20},{1,9},{5... | collective-permute-start | bytes 786440 | tf_op jit(solution)/shard_map/ppermute | solution.py:364
  17.4 7.6 %collective-permute-start.3 = (f32[4,2,64,128]{3,2,1,0:T(8,128)S(1)}, f32[4,2,64,128]{3,2,1,0:T(8,128)S(1)}, u32[]{:S(2)}, u32[]{:S(2)}) collective-permute-start(f32[4,2,64,128]{3,2,1,0:T(8,128)S(1)} %pad_maximum_fusion.refs_0_), channel_id=1, source_target_pairs={{0,4},{4,0},{8,12},{12,8},{16,20},{20,16},{24,28},{28,24},{1,5},{5... | collective-permute-start | bytes 786440 | tf_op jit(solution)/shard_map/ppermute | solution.py:364
  19.0 6.2 %collective-permute-start.9 = (f32[4,2,64,128]{3,2,1,0:T(8,128)S(1)}, f32[4,2,64,128]{3,2,1,0:T(8,128)}, u32[]{:S(2)}, u32[]{:S(2)}) collective-permute-start(f32[4,2,64,128]{3,2,1,0:T(8,128)S(1)} %pad_maximum_fusion.1.refs_4_), channel_id=1, source_target_pairs={{0,1},{1,0},{2,3},{3,2},{4,5},{5,4},{6,7},{7,6},{8,9},{9,8},{10,11... | collective-permute-start | bytes 786440 | tf_op jit(solution)/shard_map/ppermute | solution.py:364
  20.9 1.1 %copy-start.1 = (f32[2,4,160,256]{3,2,1,0:T(8,128)}, f32[2,4,160,256]{3,2,1,0:T(8,128)S(1)}, u32[]{:S(2)}) copy-start(f32[2,4,160,256]{3,2,1,0:T(8,128)S(1)} %get-tuple-element.19.refs_12_) | copy-start | bytes 3932164
  21.9 1.0 %copy-start.2 = (bf16[3,768,256]{2,1,0:T(8,128)(2,1)}, bf16[3,768,256]{2,1,0:T(8,128)(2,1)S(1)}, u32[]{:S(2)}) copy-start(bf16[3,768,256]{2,1,0:T(8,128)(2,1)S(1)} %get-tuple-element.20.refs_14_) | copy-start | bytes 3538948
  23.0 1.0 %copy-start.3 = (bf16[3,768,256]{2,1,0:T(8,128)(2,1)}, bf16[3,768,256]{2,1,0:T(8,128)(2,1)S(1)}, u32[]{:S(2)}) copy-start(bf16[3,768,256]{2,1,0:T(8,128)(2,1)S(1)} %get-tuple-element.21.refs_16_) | copy-start | bytes 3538948
  24.0 1.7 %collective-permute-start.4 = (f32[4,2,64,128]{3,2,1,0:T(8,128)S(1)}, f32[4,2,64,128]{3,2,1,0:T(8,128)S(1)}, u32[]{:S(2)}, u32[]{:S(2)}) collective-permute-start(f32[4,2,64,128]{3,2,1,0:T(8,128)S(1)} %pad_maximum_fusion.refs_0_), channel_id=1, source_target_pairs={{0,1},{1,0},{2,3},{3,2},{4,5},{5,4},{6,7},{7,6},{8,9},{9,8},{10,11... | collective-permute-start | bytes 786440 | tf_op jit(solution)/shard_map/ppermute | solution.py:364
  24.5 1.5 %collective-permute-start.13 = (f32[1,512,128]{2,1,0:T(8,128)S(1)}, f32[1,512,128]{2,1,0:T(8,128)S(1)}, u32[]{:S(2)}, u32[]{:S(2)}) collective-permute-start(f32[1,512,128]{2,1,0:T(8,128)S(1)} %collective-permute-done.11.refs_9_), channel_id=1, source_target_pairs={{0,1},{1,0},{2,3},{3,2},{4,5},{5,4},{6,7},{7,6},{8,9},{9,8},{10,11... | collective-permute-start | bytes 786440 | tf_op jit(solution)/shard_map/ppermute | solution.py:364
  24.6 1.8 %collective-permute-start.10 = (f32[4,2,64,128]{3,2,1,0:T(8,128)S(1)}, f32[4,2,64,128]{3,2,1,0:T(8,128)S(1)}, u32[]{:S(2)}, u32[]{:S(2)}) collective-permute-start(f32[4,2,64,128]{3,2,1,0:T(8,128)S(1)} %collective-permute-done.8.refs_5_), channel_id=1, source_target_pairs={{0,1},{1,0},{2,3},{3,2},{4,5},{5,4},{6,7},{7,6},{8,9},{9,8},{10,11... | collective-permute-start | bytes 786440 | tf_op jit(solution)/shard_map/ppermute | solution.py:364
  25.0 1.9 %collective-permute-start.5 = (f32[4,2,64,128]{3,2,1,0:T(8,128)S(1)}, f32[4,2,64,128]{3,2,1,0:T(8,128)}, u32[]{:S(2)}, u32[]{:S(2)}) collective-permute-start(f32[4,2,64,128]{3,2,1,0:T(8,128)S(1)} %collective-permute-done.3.refs_1_), channel_id=1, source_target_pairs={{0,1},{1,0},{2,3},{3,2},{4,5},{5,4},{6,7},{7,6},{8,9},{9,8},{10,11... | collective-permute-start | bytes 786440 | tf_op jit(solution)/shard_map/ppermute | solution.py:364

commit v2 on v1

--- a/solution.py
+++ b/solution.py
@@ -12,6 +12,9 @@
 HALF = TILE // 2
 LANES = 128
 GRID_BYTES = 2 * 1024 * 1024
+LEFT_SCALE, RIGHT_SCALE, VECTOR_SCALE = 16.0, 8.0, 256.0
+BACK_SCALE = LEFT_SCALE * RIGHT_SCALE
+small = jnp.float8_e5m2
 
 
 relax_step = 0.25
@@ -155,7 +158,7 @@
 
 def col_mats():
     forward, inverse = cyclic_mats(TILE)
-    return np.stack(split_np(forward.T) + split_np(inverse.T))
+    return np.stack(split_np(forward.T) + split_np(inverse.T * BACK_SCALE))
 
 
 def tap_waves(band_width):
@@ -170,7 +173,7 @@
     return rows, cols
 
 
-def setup_kernel(coeffs, row_waves, col_waves, col_base, spectrum, col_fwd, col_inv):
+def setup_kernel(coeffs, row_waves, col_waves, col_base, spectrum, col_main, col_small):
     half = spectrum.shape[2]
     band_width = (coeffs.shape[0] - 1) // 2
     for j in (0, 1):
@@ -185,24 +188,20 @@
                 mixed = jnp.where(place < half // 2, -mixed, mixed)
             for part in (0, 1):
                 spectrum[part, 2 * j + i] = mixed[part * half : (part + 1) * half]
-    count = col_fwd.shape[0]
-    none = jnp.zeros((TILE, TILE), jnp.bfloat16)
+    count = col_main.shape[1]
     for w in range(count):
-        first, last = w == 0, w == count - 1
-        for third, part in enumerate((0, 0, 1)):
-            rows = pl.ds(third * TILE, TILE)
-            col_fwd[w, rows, :] = col_base[part]
-            if first:
-                col_fwd[w, pl.ds(third * TILE + TILE - band_width, band_width), :] = none[:band_width]
-            if last:
-                col_fwd[w, pl.ds(third * TILE, band_width), :] = none[:band_width]
-            inverse = col_base[2 + part].astype(jnp.float32)
-            lane = lax.broadcasted_iota(jnp.int32, inverse.shape, 1)
-            if not first:
-                inverse = jnp.where(lane >= HALF // 2, inverse, 0.0)
-            if not last:
-                inverse = jnp.where(lane < TILE - HALF // 2, inverse, 0.0)
-            col_inv[w, rows, :] = inverse.astype(jnp.bfloat16)
+        for way in (0, 1):
+            for part in (0, 1):
+                cells = col_base[2 * way + part].astype(jnp.float32)
+                place = lax.broadcasted_iota(jnp.int32, cells.shape, way)
+                margin = HALF // 2 if way else band_width
+                if (w > 0) if way else (w == count - 1):
+                    cells = jnp.where(place >= margin, cells, 0.0)
+                if (w < count - 1) if way else (w == 0):
+                    cells = jnp.where(place < TILE - margin, cells, 0.0)
+                if part == 0:
+                    col_main[way, w] = cells.astype(jnp.bfloat16)
+                col_small[way, w, part * TILE : (part + 1) * TILE] = cells.astype(small)
 
 
 def setup(coeffs, cols):
@@ -214,8 +213,8 @@
         setup_kernel,
         out_shape=(
             jax.ShapeDtypeStruct((2, 4, HALF + band_width, TILE), jnp.float32),
-            jax.ShapeDtypeStruct((windows, 3 * TILE, TILE), jnp.bfloat16),
-            jax.ShapeDtypeStruct((windows, 3 * TILE, TILE), jnp.bfloat16),
+            jax.ShapeDtypeStruct((2, windows, TILE, TILE), jnp.bfloat16),
+            jax.ShapeDtypeStruct((2, windows, 2 * TILE, TILE), small),
         ),
         in_specs=[vmem] * 4,
         out_specs=(vmem,) * 3,
@@ -229,16 +228,25 @@
     return high, (value - high.astype(jnp.float32)).astype(jnp.bfloat16)
 
 
+def split_small(value):
+    high = value.astype(jnp.bfloat16)
+    low = (value - high.astype(jnp.float32)).astype(jnp.bfloat16)
+    most = jnp.asarray(jnp.finfo(small).max, jnp.bfloat16)
+    return high, jnp.clip(low, -most, most).astype(small), jnp.clip(high, -most, most).astype(small)
+
+
 def dot32(left, right):
     return jnp.dot(left, right, preferred_element_type=jnp.float32)
 
 
 def replicated_kernel(hx_bits, place, mask, *refs):
     s_near, s_turn, s_far, s_both, r_near, r_turn, r_far, r_both, c_near, c_turn, c_far, c_both = refs[:12]
-    spectrum, row_fwd, col_fwd, row_inv, col_inv, out, norms = refs[12:19]
-    state, total, w_hi, w_lo, z, y_hi, y_lo, u_hi, u_lo, t_hi, t_lo, wave, left, right = refs[19:]
+    spectrum, row_fwd, row_inv, col_main, col_small, out, norms = refs[12:19]
+    state, total, z, y_hi, y_lo, w_main, w_rest, w_same, u_main, u_rest, u_same, t_main, t_rest, t_same = refs[19:33]
+    left_main, left_small, right_main, right_small, scale = refs[33:]
+    w, u, t = (w_main, w_rest, w_same), (u_main, u_rest, u_same), (t_main, t_rest, t_same)
     rows, cols = state.shape
-    col_windows = col_fwd.shape[0]
+    col_windows = col_main.shape[1]
     half = row_fwd.shape[1]
     quarter = half // 2
     band_width = half - HALF
@@ -246,6 +254,7 @@
     block_rows, block_cols = s_near.shape[-2:]
     near_count = s_near.shape[0]
     here_x, here_y, here_c = place[0], place[1], place[2]
+    square = jnp.zeros((8, LANES), jnp.float32)
     for pos in range(2 * near_count):
         s_row = (here_x ^ hx_bits[0][pos]) * block_rows
         s_row = pl.multiple_of(s_row, block_rows)
@@ -256,9 +265,7 @@
                 value = ref[pos % near_count, k]
                 state[pl.ds(s_row, block_rows), pl.ds(s_col, block_cols)] = value
                 total[pl.ds(s_row, block_rows), pl.ds(s_col, block_cols)] = value
-                high, low = split(value)
-                w_hi[pl.ds(s_row, block_rows), pl.ds(s_col, block_cols)] = high
-                w_lo[pl.ds(s_row, block_rows), pl.ds(s_col, block_cols)] = low
+                square = square + jnp.sum((value * value).reshape(block_rows // 8, 8, block_cols), 0)
     share = TILE // block_rows
     for pos in range(2 * near_count):
         index = here_x ^ hx_bits[1][pos]
@@ -270,18 +277,21 @@
                 lane = side * (cols // 2) + k * LANES
                 b = lane // TILE
                 at = pl.multiple_of(lane % TILE, LANES)
-                high, low = split(ref[pos % near_count, k] * mask[a, b].astype(jnp.float32))
-                for third, part in enumerate((high, high, low)):
-                    left[a, b, pl.ds(sub, block_rows), pl.ds(pl.multiple_of(at + third * TILE, LANES), LANES)] = part
+                cells = ref[pos % near_count, k] * (LEFT_SCALE * mask[a, b].astype(jnp.float32))
+                high, rest, same = split_small(cells)
+                left_main[a, b, pl.ds(sub, block_rows), pl.ds(at, LANES)] = high
+                left_small[a, b, pl.ds(sub, block_rows), pl.ds(at, LANES)] = same
+                left_small[a, b, pl.ds(sub, block_rows), pl.ds(pl.multiple_of(at + TILE, LANES), LANES)] = rest
     for k in range(2 * c_near.shape[0]):
         for far, ref in enumerate((c_near, c_far) if k < c_near.shape[0] else (c_turn, c_both)):
             lane = ((here_y ^ k) * 2 + (here_c ^ far)) * block_cols
             b = lane // TILE
             at = pl.multiple_of(lane % TILE, block_cols)
             for a in range(tile_rows):
-                high, low = split(ref[k % c_near.shape[0], pl.ds(a * TILE, TILE), :])
-                for third, part in enumerate((high, high, low)):
-                    right[a, b, pl.ds(third * TILE, TILE), pl.ds(at, block_cols)] = part
+                high, rest, same = split_small(ref[k % c_near.shape[0], pl.ds(a * TILE, TILE), :] * RIGHT_SCALE)
+                right_main[a, b, :, pl.ds(at, block_cols)] = high
+                right_small[a, b, pl.ds(0, TILE), pl.ds(at, block_cols)] = same
+                right_small[a, b, pl.ds(TILE, TILE), pl.ds(at, block_cols)] = rest
 
     for edge in (0, rows + band_width):
         z[pl.ds(edge, band_width), :] = jnp.zeros((band_width, z.shape[1]), jnp.float32)
@@ -290,70 +300,117 @@
         high = hi_ref[row_at, col_at]
         return jnp.concatenate([high, lo_ref[row_at, col_at], high], axis)
 
+    def put(refs, at, value):
+        for ref, part in zip(refs, split_small(value)):
+            ref[at] = part
+
+    def scaled_by(sum_square):
+        return VECTOR_SCALE * lax.rsqrt(jnp.maximum(jnp.full((8, LANES), sum_square), 1e-30))
+
+    def times(cells, factor):
+        return (cells.reshape(-1, 8, LANES) * factor).reshape(cells.shape)
+
+    def columns(b):
+        at = slice(None), pl.ds(b * HALF, TILE)
+        rest_same = jnp.concatenate([w_rest[at], w_same[at]], 1)
+        z[pl.ds(band_width, rows), pl.ds(b * TILE, TILE)] = dot32(w_main[at], col_main[0, b]) + dot32(
+            rest_same, col_small[0, b]
+        )
+
+    def spectral(a, b, part):
+        cb = pl.ds(b * TILE, TILE)
+        upper = z[pl.ds(a * TILE, half), cb]
+        lower = z[pl.ds(a * TILE + half, half), cb]
+        high, low = split(upper - lower if part else upper + lower)
+        wave = dot32(row_fwd[part], jnp.concatenate([high, low, high], 0))
+        for i in (0, 1):
+            for j in (0, 1):
+                ri, rj = slice(i * quarter, (i + 1) * quarter), slice((1 - i) * quarter, (2 - i) * quarter)
+                ci, cj = slice(j * HALF, (j + 1) * HALF), slice((1 - j) * HALF, (2 - j) * HALF)
+                y = (
+                    spectrum[part, 0, ri, ci] * wave[ri, ci]
+                    + spectrum[part, 1, ri, ci] * wave[rj, ci]
+                    + spectrum[part, 2, ri, ci] * wave[ri, cj]
+                    + spectrum[part, 3, ri, ci] * wave[rj, cj]
+                )
+                to = pl.ds((2 * a + part) * half + i * quarter, quarter), pl.ds(b * TILE + j * HALF, HALF)
+                y_hi[to], y_lo[to] = split(y)
+
+    def back_rows(a, b):
+        cb = pl.ds(b * TILE, TILE)
+        sums, diffs = (
+            dot32(row_inv[part], triple(y_hi, y_lo, pl.ds((2 * a + part) * half, half), cb, 0)) for part in (0, 1)
+        )
+        upper = sums[band_width:] + diffs[band_width:]
+        lower = sums[: half - band_width] - diffs[: half - band_width]
+        put(u, (pl.ds(a * TILE, HALF), cb), upper)
+        put(u, (pl.ds(a * TILE + HALF, HALF), cb), lower)
+
+    def tile_left(a, b):
+        at = pl.ds(a * TILE, TILE), pl.ds(b * TILE, TILE)
+        rest_same = jnp.concatenate([w_rest[at], w_same[at]], 0)
+        put(t, at, dot32(left_main[a, b], w_main[at]) + dot32(left_small[a, b], rest_same))
+
+    def update(a, keep, take, factor):
+        ra = pl.ds(a * TILE, TILE)
+        square = jnp.zeros((8, LANES), jnp.float32)
+        parts = []
+        for b in range(col_windows):
+            at = ra, pl.ds(b * TILE, TILE)
+            lhs, lhs_small, rhs, rhs_small = [u_main[at]], [u_rest[at], u_same[at]], [col_main[1, b]], [col_small[1, b]]
+            if b % 2 == 0:
+                at = ra, pl.ds(b // 2 * TILE, TILE)
+                lhs, lhs_small = lhs + [t_main[at]], lhs_small + [t_rest[at], t_same[at]]
+                rhs, rhs_small = rhs + [right_main[a, b // 2]], rhs_small + [right_small[a, b // 2]]
+            parts.append(
+                dot32(jnp.concatenate(lhs, 1), jnp.concatenate(rhs, 0))
+                + dot32(jnp.concatenate(lhs_small, 1), jnp.concatenate(rhs_small, 0))
+            )
+        for j in range(cols // HALF):
+            pieces = [parts[b][:, (j - b) * HALF : (j - b + 1) * HALF] for b in range(col_windows) if b <= j <= b + 1]
+            cj = pl.ds(j * HALF, HALF)
+            residual = keep * state[ra, cj] - times(functools.reduce(jnp.add, pieces), take)
+            state[ra, cj] = residual
+            total[ra, cj] = total[ra, cj] + relax_step * residual
+            put(w, (ra, cj), times(residual, factor))
+            square = square + jnp.sum((residual * residual).reshape(TILE // 8, 8, LANES), 0)
+        return square
+
     def step(k, carry):
+        sums, last = carry
         keep = jnp.where(k == 0, 0.0, 1.0 - relax_step)
-        take = jnp.where(k == 0, 1.0, relax_step)
-        every = pl.ds(0, rows)
+        take = jnp.where(k == 0, 1.0, relax_step) / (BACK_SCALE * scale[...])
+        factor = scaled_by(last)
+        tiles = [(a, b) for a in range(tile_rows) for b in range(tile_cols)]
         for b in range(col_windows):
-            at = pl.ds(b * TILE, TILE)
-            z[pl.ds(band_width, rows), at] = dot32(triple(w_hi, w_lo, every, pl.ds(b * HALF, TILE), 1), col_fwd[b])
+            columns(b)
+        for b in range(col_windows):
+            for a in range(tile_rows):
+                spectral(a, b, 0)
+                spectral(a, b, 1)
+                if tiles:
+                    tile_left(*tiles.pop(0))
+                if b:
+                    back_rows(a, b - 1)
+        for at in tiles:
+            tile_left(*at)
         for a in range(tile_rows):
-            for b in range(col_windows):
-                cb = pl.ds(b * TILE, TILE)
-                upper = z[pl.ds(a * TILE, half), cb]
-                lower = z[pl.ds(a * TILE + half, half), cb]
-                for part, cells in enumerate((upper + lower, upper - lower)):
-                    high, low = split(cells)
-                    wave[part] = dot32(row_fwd[part], jnp.concatenate([high, low, high], 0))
-                    for i in (0, 1):
-                        for j in (0, 1):
-                            ri, rj = pl.ds(i * quarter, quarter), pl.ds((1 - i) * quarter, quarter)
-                            ci, cj = pl.ds(j * HALF, HALF), pl.ds((1 - j) * HALF, HALF)
-                            y = (
-                                spectrum[part, 0, ri, ci] * wave[part, ri, ci]
-                                + spectrum[part, 1, ri, ci] * wave[part, rj, ci]
-                                + spectrum[part, 2, ri, ci] * wave[part, ri, cj]
-                                + spectrum[part, 3, ri, ci] * wave[part, rj, cj]
-                            )
-                            to = pl.ds((2 * a + part) * half + i * quarter, quarter), pl.ds(b * TILE + j * HALF, HALF)
-                            y_hi[to], y_lo[to] = split(y)
-        for a in range(tile_rows):
-            for b in range(col_windows):
-                cb = pl.ds(b * TILE, TILE)
-                sums, diffs = (
-                    dot32(row_inv[part], triple(y_hi, y_lo, pl.ds((2 * a + part) * half, half), cb, 0)) for part in (0, 1)
-                )
-                upper = sums[band_width:] + diffs[band_width:]
-                lower = sums[: half - band_width] - diffs[: half - band_width]
-                u_hi[pl.ds(a * TILE, HALF), cb], u_lo[pl.ds(a * TILE, HALF), cb] = split(upper)
-                u_hi[pl.ds(a * TILE + HALF, HALF), cb], u_lo[pl.ds(a * TILE + HALF, HALF), cb] = split(lower)
-        for a in range(tile_rows):
-            for b in range(tile_cols):
-                at = pl.ds(a * TILE, TILE), pl.ds(b * TILE, TILE)
-                t_hi[at], t_lo[at] = split(dot32(left[a, b], triple(w_hi, w_lo, *at, 0)))
+            back_rows(a, col_windows - 1)
         square = jnp.zeros((8, LANES), jnp.float32)
         for a in range(tile_rows):
-            ra = pl.ds(a * TILE, TILE)
-            parts = []
-            for b in range(col_windows):
-                lhs = triple(u_hi, u_lo, ra, pl.ds(b * TILE, TILE), 1)
-                rhs = col_inv[b]
-                if b % 2 == 0:
-                    lhs = jnp.concatenate([lhs, triple(t_hi, t_lo, ra, pl.ds(b // 2 * TILE, TILE), 1)], 1)
-                    rhs = jnp.concatenate([rhs, right[a, b // 2]], 0)
-                parts.append(dot32(lhs, rhs))
-            for j in range(cols // HALF):
-                pieces = [parts[b][:, (j - b) * HALF : (j - b + 1) * HALF] for b in range(col_windows) if b <= j <= b + 1]
-                cj = pl.ds(j * HALF, HALF)
-                residual = keep * state[ra, cj] - take * functools.reduce(jnp.add, pieces)
-                state[ra, cj] = residual
-                total[ra, cj] = total[ra, cj] + relax_step * residual
-                w_hi[ra, cj], w_lo[ra, cj] = split(residual)
-                square = square + jnp.sum((residual * residual).reshape(TILE // 8, 8, LANES), 0)
-        return jnp.where(norm_lane == k, jnp.sum(square), carry)
-
+            square = square + update(a, keep, take, factor)
+        scale[...] = factor
+        sum_square = jnp.sum(square)
+        return jnp.where(norm_lane == k, sum_square, sums), sum_square
+
+    sum_square = jnp.sum(square)
+    scale[...] = scaled_by(sum_square)
+    for i in range(0, rows, TILE):
+        for j in range(0, cols, LANES):
+            at = pl.ds(i, TILE), pl.ds(j, LANES)
+            put(w, at, times(state[at], scale[...]))
     norm_lane = lax.broadcasted_iota(jnp.int32, norms.shape, 1)
-    summed = lax.fori_loop(0, ITERS, step, jnp.zeros(norms.shape, jnp.float32))
+    summed, _ = lax.fori_loop(0, ITERS, step, (jnp.zeros(norms.shape, jnp.float32), sum_square))
     norms[...] = jnp.sqrt(summed / (rows * cols) + tiny_square)
     own_row = pl.multiple_of(here_x * block_rows, block_rows)
     own_col = pl.multiple_of((here_y * 2 + here_c) * block_cols, block_cols)
@@ -399,7 +456,7 @@
     pieces = []
     for near, held, turn in zip((s_near, r_near, c_near), (s_held, r_near, c_near), turns):
         pieces += [near, turn, swap(held, "hy", 1), swap(turn, "hy", 1)]
-    spectrum, col_fwd, col_inv = ready
+    spectrum, col_main, col_small = ready
     row_fwd, row_inv = (jnp.asarray(m) for m in row_mats(band_width))
     place = jnp.stack([index_x, index_y // 2, index_y % 2])
     half, col_windows = HALF + band_width, cols // HALF - 1
@@ -407,11 +464,13 @@
     smem = pl.BlockSpec(memory_space=pltpu.SMEM)
     f32, bf16 = jnp.float32, jnp.bfloat16
     tiles = (rows // TILE, cols // TILE)
-    shapes = [((rows, cols), f32)] * 2 + [((rows, cols), bf16)] * 2
-    shapes += [((rows + 2 * band_width, col_windows * TILE), f32)]
-    shapes += [((2 * half * tiles[0], col_windows * TILE), bf16)] * 2 + [((rows, col_windows * TILE), bf16)] * 2
-    shapes += [((rows, cols), bf16)] * 2 + [((2, half, TILE), f32)]
-    shapes += [(tiles + (TILE, 3 * TILE), bf16), (tiles + (3 * TILE, TILE), bf16)]
+    wide = col_windows * TILE
+    shapes = [((rows, cols), f32)] * 2 + [((rows + 2 * band_width, wide), f32)]
+    shapes += [((2 * half * tiles[0], wide), bf16)] * 2
+    for shape in ((rows, cols), (rows, wide), (rows, cols)):
+        shapes += [(shape, bf16), (shape, small), (shape, small)]
+    shapes += [(tiles + (TILE, TILE), bf16), (tiles + (TILE, 2 * TILE), small)]
+    shapes += [(tiles + (TILE, TILE), bf16), (tiles + (2 * TILE, TILE), small), ((8, LANES), f32)]
     result, norms = pl.pallas_call(
         functools.partial(replicated_kernel, (bit_places(down), bit_places(turned))),
         out_shape=(
@@ -423,7 +482,7 @@
         scratch_shapes=[pltpu.VMEM(*s) for s in shapes],
         compiler_params=pltpu.CompilerParams(vmem_limit_bytes=50 * 1024 * 1024),
         name="replicated_steps",
-    )(place, tile_mask, *pieces, spectrum, row_fwd, col_fwd, row_inv, col_inv)
+    )(place, tile_mask, *pieces, spectrum, row_fwd, row_inv, col_main, col_small)
     return result, norms[0]
 
 

time: 65.3 us -> 58.7 us (0.90)
  Pallas kernels: 39.2 us -> 32.8 us
    pallas_call x1, Pallas kernels: 37.3 us -> 30.9 us  [replicated(): pl.pallas_call(functools.partial(replicated_kernel, (bit_places(down), bi...]
  transfers between devices with their start and end apart: 14 -> 14, of which waited for: 6 -> 6; matrix products, arithmetic and copies ran while one was open for 1% -> 2% of each run, Pallas kernels for 3% -> 3%
where the time goes in v2:
time: 58.7 us; the launch traced here: 57.7 us
  Pallas kernels  32.8 us (56%)
  starting transfers between devices  16.5 us (28%)
  waiting for transfers between devices  3.85 us (7%)
  local copies, waits for them, and re-layouts  2.87 us (5%)
  other arithmetic  0.9 us (2%)
  between operations  0.76 us (1%)
    pallas_call x1, Pallas kernels, replicated(): pl.pallas_call(functools.partial(replicated_kernel, (bit_places(down), bi...  30.9 us
    ppermute x14, starting transfers between devices, swap(): lax.ppermute(value, axis, [(i, i ^ bit) for i in range(lax.axis_size(axis...  16.5 us
    ppermute x14, waiting for transfers between devices, swap(): lax.ppermute(value, axis, [(i, i ^ bit) for i in range(lax.axis_size(axis...  3.85 us
    unnamed x24, local copies, waits for them, and re-layouts  2.86 us
    pallas_call x1, Pallas kernels, setup(): pl.pallas_call(setup_kernel, out_shape=(jax.ShapeDtypeStruct((2, 4, HALF...  1.88 us
  transfers between devices with their start and end apart: 14, of which 6 were waited for; matrix products, arithmetic and copies ran while one was open for 2% of the time, Pallas kernels for 3%

profile of v2, /device:TPU:0, one launch (start us, length us, event | category | flops | bytes accessed | tf_op | source)
XLA Modules:
  0.0 57.7 jit_solution(4737661026313244923)
XLA Ops:
  0.6 0.0 copy-start
  0.6 0.0 copy-start.4
  0.7 0.0 copy-start.7
  0.7 0.0 copy-start.10
  0.7 3.1 %collective-permute-start = (f32[1,64,128]{2,1,0:T(8,128)}, f32[1,64,128]{2,1,0:T(8,128)S(1)}, u32[]{:S(2)}, u32[]{:S(2)}) collective-permute-start(f32[1,64,128]{2,1,0:T(8,128)} %bitcast.20), channel_id=1, source_target_pairs={{0,2},{1,3},{2,0},{3,1},{4,6},{5,7},{6,4},{7,5},{8,10},{9,11},{10,... | collective-permute-start | bytes 98312 | tf_op jit(solution)/shard_map/ppermute | solution.py:421
  3.7 0.0 copy-done
  3.7 0.0 copy-start.9
  3.8 2.7 %collective-permute-start.6 = (f32[1,2,64,128]{3,2,1,0:T(8,128)S(1)}, f32[1,2,64,128]{3,2,1,0:T(8,128)S(1)}, u32[]{:S(2)}, u32[]{:S(2)}) collective-permute-start(f32[1,2,64,128]{3,2,1,0:T(8,128)S(1)} %bitcast_bitcast_fusion), channel_id=1, source_target_pairs={{0,16},{4,20},{8,24},{12,28},{16,0},{20,4},{24,8},{28,12},{1,17},{... | collective-permute-start | bytes 196616 | tf_op jit(solution)/shard_map/ppermute | solution.py:421
  6.4 0.0 collective-permute-done
  6.4 0.8 %maximum_bitcast_fusion = f32[1,2,64,128]{3,2,1,0:T(8,128)S(1)} fusion(f32[1,64,128]{2,1,0:T(8,128)S(1)} %collective-permute-done, f32[1,64,128]{2,1,0:T(8,128)} %bitcast.21), kind=kLoop, calls=%fused_computation.5 | loop fusion | flops 16384 | bytes 131072 | tf_op jit(solution)/shard_map/broadcast_in_dim | solution.py:449
  7.2 0.0 copy-start.5
  7.2 0.0 copy-start.6
  7.2 0.0 copy-start.8
  7.2 0.0 copy-start.11
  7.2 2.6 %collective-permute-start.1 = (f32[1,2,64,128]{3,2,1,0:T(8,128)S(1)}, f32[1,2,64,128]{3,2,1,0:T(8,128)S(1)}, u32[]{:S(2)}, u32[]{:S(2)}) collective-permute-start(f32[1,2,64,128]{3,2,1,0:T(8,128)S(1)} %maximum_bitcast_fusion), channel_id=1, source_target_pairs={{0,16},{4,20},{8,24},{12,28},{16,0},{20,4},{24,8},{28,12},{1,17},{... | collective-permute-start | bytes 196616 | tf_op jit(solution)/shard_map/ppermute | solution.py:421
  9.8 0.0 collective-permute-done.6
  9.8 1.6 %collective-permute-start.7 = (f32[2,2,64,128]{3,2,1,0:T(8,128)S(1)}, f32[2,2,64,128]{3,2,1,0:T(8,128)S(1)}, u32[]{:S(2)}, u32[]{:S(2)}) collective-permute-start(f32[2,2,64,128]{3,2,1,0:T(8,128)S(1)} %pad_maximum_fusion.3), channel_id=1, source_target_pairs={{0,4},{4,0},{8,12},{12,8},{16,20},{20,16},{24,28},{28,24},{1,5},{5... | collective-permute-start | bytes 393224 | tf_op jit(solution)/shard_map/ppermute | solution.py:421
  11.4 1.1 %collective-permute-done.1 = f32[1,2,64,128]{3,2,1,0:T(8,128)S(1)} collective-permute-done((f32[1,2,64,128]{3,2,1,0:T(8,128)S(1)}, f32[1,2,64,128]{3,2,1,0:T(8,128)S(1)}, u32[]{:S(2)}, u32[]{:S(2)}) %collective-permute-start.1) | collective-permute-done | bytes 65568 | tf_op jit(solution)/shard_map/ppermute | solution.py:421
  12.5 1.6 %collective-permute-start.2 = (f32[2,2,64,128]{3,2,1,0:T(8,128)S(1)}, f32[2,2,64,128]{3,2,1,0:T(8,128)S(1)}, u32[]{:S(2)}, u32[]{:S(2)}) collective-permute-start(f32[2,2,64,128]{3,2,1,0:T(8,128)S(1)} %pad_maximum_fusion.2), channel_id=1, source_target_pairs={{0,8},{4,12},{8,0},{12,4},{16,24},{20,28},{24,16},{28,20},{1,9},{5... | collective-permute-start | bytes 393224 | tf_op jit(solution)/shard_map/ppermute | solution.py:421
  14.1 0.0 collective-permute-start.12
  14.1 1.5 %collective-permute-start.11 = (f32[1,512,128]{2,1,0:T(8,128)}, f32[1,512,128]{2,1,0:T(8,128)S(1)}, u32[]{:S(2)}, u32[]{:S(2)}) collective-permute-start(f32[1,512,128]{2,1,0:T(8,128)} %bitcast.18), channel_id=1, source_target_pairs={{0,2},{1,3},{2,0},{3,1},{4,6},{5,7},{6,4},{7,5},{8,10},{9,11},{10,... | collective-permute-start | bytes 786440 | tf_op jit(solution)/shard_map/ppermute | solution.py:421
  15.6 0.0 collective-permute-done.7
  15.6 0.9 %collective-permute-start.8 = (f32[4,2,64,128]{3,2,1,0:T(8,128)S(1)}, f32[4,2,64,128]{3,2,1,0:T(8,128)S(1)}, u32[]{:S(2)}, u32[]{:S(2)}) collective-permute-start(f32[4,2,64,128]{3,2,1,0:T(8,128)S(1)} %pad_maximum_fusion.1.refs_4_), channel_id=1, source_target_pairs={{0,8},{4,12},{8,0},{12,4},{16,24},{20,28},{24,16},{28,20},{1,9},{5... | collective-permute-start | bytes 786440 | tf_op jit(solution)/shard_map/ppermute | solution.py:421
  16.5 1.0 %collective-permute-done.2 = f32[2,2,64,128]{3,2,1,0:T(8,128)S(1)} collective-permute-done((f32[2,2,64,128]{3,2,1,0:T(8,128)S(1)}, f32[2,2,64,128]{3,2,1,0:T(8,128)S(1)}, u32[]{:S(2)}, u32[]{:S(2)}) %collective-permute-start.2) | collective-permute-done | bytes 131104 | tf_op jit(solution)/shard_map/ppermute | solution.py:421
  17.5 1.6 %collective-permute-start.3 = (f32[4,2,64,128]{3,2,1,0:T(8,128)S(1)}, f32[4,2,64,128]{3,2,1,0:T(8,128)S(1)}, u32[]{:S(2)}, u32[]{:S(2)}) collective-permute-start(f32[4,2,64,128]{3,2,1,0:T(8,128)S(1)} %pad_maximum_fusion.refs_0_), channel_id=1, source_target_pairs={{0,4},{4,0},{8,12},{12,8},{16,20},{20,16},{24,28},{28,24},{1,5},{5... | collective-permute-start | bytes 786440 | tf_op jit(solution)/shard_map/ppermute | solution.py:421
  19.1 0.0 collective-permute-start.9
  19.1 0.0 copy-done.4
  19.1 0.0 copy-done.7
  19.1 0.0 copy-done.10
  19.1 0.0 copy-done.9
  19.1 1.9 %setup.1 = (f32[2,4,160,256]{3,2,1,0:T(8,128)S(1)}, bf16[2,3,256,256]{3,2,1,0:T(8,128)(2,1)S(1)}, f8e5m2[2,3,512,256]{3,2,1,0:T(32,128)(4,1)S(1)}) custom-call(f32[65,65]{1,0:T(8,128)S(1)} %copy-done.10, f32[2,320,65]{2,1,0:T(8,128)S(1)} %copy-done.7, f32[2,65,256]{2,1,0:T(8,128)S(1)} %copy-done.9, bf16[4,256,256]{2,1,0:T(8,128)(2,1)S(1)} %copy-done.4), custom_call_target="tpu_custom_call" | custom-call | tf_op jit(solution)/shard_map/setup/pallas_call | solution.py:212
  21.0 0.0 copy-start.1
  21.0 1.1 %copy-done.1 = f32[2,4,160,256]{3,2,1,0:T(8,128)} copy-done((f32[2,4,160,256]{3,2,1,0:T(8,128)}, f32[2,4,160,256]{3,2,1,0:T(8,128)S(1)}, u32[]{:S(2)}) %copy-start.1) | copy-done | bytes 1310744
  22.1 0.0 copy-start.2
  22.1 0.9 %copy-done.2 = bf16[2,3,256,256]{3,2,1,0:T(8,128)(2,1)} copy-done((bf16[2,3,256,256]{3,2,1,0:T(8,128)(2,1)}, bf16[2,3,256,256]{3,2,1,0:T(8,128)(2,1)S(1)}, u32[]{:S(2)}) %copy-start.2) | copy-done | bytes 786456
  22.9 0.0 copy-start.3
  22.9 0.9 %copy-done.3 = f8e5m2[2,3,512,256]{3,2,1,0:T(32,128)(4,1)} copy-done((f8e5m2[2,3,512,256]{3,2,1,0:T(32,128)(4,1)}, f8e5m2[2,3,512,256]{3,2,1,0:T(32,128)(4,1)S(1)}, u32[]{:S(2)}) %copy-start.3) | copy-done | bytes 786456
  23.8 0.0 collective-permute-done.12.refs_10_
  23.8 0.5 collective-permute-start.4
  24.3 0.0 collective-permute-done.11.refs_9_
  24.3 0.1 collective-permute-start.13
  24.4 0.0 collective-permute-done.8.refs_5_
  24.4 0.4 collective-permute-start.10
  24.8 0.0 collective-permute-done.3.refs_1_
  24.8 0.1 collective-permute-start.5
  24.9 0.1 pad_add_fusion.place
  25.0 0.0 collective-permute-done.9.refs_6_
  25.0 0.5 collective-permute-done.4.refs_2_
  25.5 0.4 collective-permute-done.13.refs_11_
  25.9 0.4 collective-permute-done.10.refs_7_
  26.2 0.5 collective-permute-done.5.refs_3_
  26.7 0.0 copy-done.5
  26.7 0.0 copy-done.6
  26.8 0.0 copy-done.8
  26.8 0.0 copy-done.11
  26.8 30.9 %replicated_steps.1 = (f32[64,128]{1,0:T(8,128)}, f32[1,8]{1,0:T(1,128)}) custom-call(s32[3]{0:T(128)S(1)} %pad_add_fusion.place, s32[2,2]{1,0:T(2,128)S(1)} %copy-done.11, f32[4,2,64,128]{3,2,1,0:T(8,128)S(1)} %pad_maximum_fusion.refs_0_, f32[4,2,64,128]{3,2,1,0:T(8,128)S(1)} %collective-permute-done.3.refs_1_, ...), custom_call_target="tpu_custom_call" | custom-call | tf_op jit(solution)/shard_map/replicated_steps/pallas_call | solution.py:474
  (5 shorter events, 0.1 us)
Async XLA Ops:
  0.6 3.1 %copy-start = (f32[64,512]{1,0:T(8,128)S(1)}, f32[64,512]{1,0:T(8,128)}, u32[]{:S(2)}) copy-start(f32[64,512]{1,0:T(8,128)} %param.12) | copy-start | bytes 393220
  0.6 18.4 %copy-start.4 = (bf16[4,256,256]{2,1,0:T(8,128)(2,1)S(1)}, bf16[4,256,256]{2,1,0:T(8,128)(2,1)}, u32[]{:S(2)}) copy-start(bf16[4,256,256]{2,1,0:T(8,128)(2,1)} %constant.52.clone.col_base) | copy-start | bytes 1572868
  0.7 18.4 %copy-start.7 = (f32[2,320,65]{2,1,0:T(8,128)S(1)}, f32[2,320,65]{2,1,0:T(8,128)}, u32[]{:S(2)}) copy-start(f32[2,320,65]{2,1,0:T(8,128)} %constant.50.clone.row_waves) | copy-start | bytes 499204
  0.7 18.4 %copy-start.10 = (f32[65,65]{1,0:T(8,128)S(1)}, f32[65,65]{1,0:T(8,128)}, u32[]{:S(2)}) copy-start(f32[65,65]{1,0:T(8,128)} %coeffs) | copy-start | bytes 50704
  0.7 5.7 %collective-permute-start = (f32[1,64,128]{2,1,0:T(8,128)}, f32[1,64,128]{2,1,0:T(8,128)S(1)}, u32[]{:S(2)}, u32[]{:S(2)}) collective-permute-start(f32[1,64,128]{2,1,0:T(8,128)} %bitcast.20), channel_id=1, source_target_pairs={{0,2},{1,3},{2,0},{3,1},{4,6},{5,7},{6,4},{7,5},{8,10},{9,11},{10,... | collective-permute-start | bytes 98312 | tf_op jit(solution)/shard_map/ppermute | solution.py:421
  3.7 15.4 %copy-start.9 = (f32[2,65,256]{2,1,0:T(8,128)S(1)}, f32[2,65,256]{2,1,0:T(8,128)}, u32[]{:S(2)}) copy-start(f32[2,65,256]{2,1,0:T(8,128)} %constant.51.clone.col_waves) | copy-start | bytes 399364
  3.8 6.0 %collective-permute-start.6 = (f32[1,2,64,128]{3,2,1,0:T(8,128)S(1)}, f32[1,2,64,128]{3,2,1,0:T(8,128)S(1)}, u32[]{:S(2)}, u32[]{:S(2)}) collective-permute-start(f32[1,2,64,128]{3,2,1,0:T(8,128)S(1)} %bitcast_bitcast_fusion), channel_id=1, source_target_pairs={{0,16},{4,20},{8,24},{12,28},{16,0},{20,4},{24,8},{28,12},{1,17},{... | collective-permute-start | bytes 196616 | tf_op jit(solution)/shard_map/ppermute | solution.py:421
  7.2 19.6 %copy-start.5 = (bf16[2,160,480]{2,1,0:T(8,128)(2,1)S(1)}, bf16[2,160,480]{2,1,0:T(8,128)(2,1)}, u32[]{:S(2)}) copy-start(bf16[2,160,480]{2,1,0:T(8,128)(2,1)} %constant.54.clone.refs_14_) | copy-start | bytes 921604
  7.2 19.6 %copy-start.6 = (bf16[2,160,480]{2,1,0:T(8,128)(2,1)S(1)}, bf16[2,160,480]{2,1,0:T(8,128)(2,1)}, u32[]{:S(2)}) copy-start(bf16[2,160,480]{2,1,0:T(8,128)(2,1)} %constant.53.clone.refs_13_) | copy-start | bytes 921604
  7.2 19.6 %copy-start.8 = (f32[512,128]{1,0:T(8,128)S(1)}, f32[512,128]{1,0:T(8,128)}, u32[]{:S(2)}) copy-start(f32[512,128]{1,0:T(8,128)} %param.13) | copy-start | bytes 786436
  7.2 19.6 %copy-start.11 = (s32[2,2]{1,0:T(2,128)S(1)}, s32[2,2]{1,0:T(2,128)}, u32[]{:S(2)}) copy-start(s32[2,2]{1,0:T(2,128)} %mask.1) | copy-start | bytes 52
  7.2 5.2 %collective-permute-start.1 = (f32[1,2,64,128]{3,2,1,0:T(8,128)S(1)}, f32[1,2,64,128]{3,2,1,0:T(8,128)S(1)}, u32[]{:S(2)}, u32[]{:S(2)}) collective-permute-start(f32[1,2,64,128]{3,2,1,0:T(8,128)S(1)} %maximum_bitcast_fusion), channel_id=1, source_target_pairs={{0,16},{4,20},{8,24},{12,28},{16,0},{20,4},{24,8},{28,12},{1,17},{... | collective-permute-start | bytes 196616 | tf_op jit(solution)/shard_map/ppermute | solution.py:421
  9.8 5.7 %collective-permute-start.7 = (f32[2,2,64,128]{3,2,1,0:T(8,128)S(1)}, f32[2,2,64,128]{3,2,1,0:T(8,128)S(1)}, u32[]{:S(2)}, u32[]{:S(2)}) collective-permute-start(f32[2,2,64,128]{3,2,1,0:T(8,128)S(1)} %pad_maximum_fusion.3), channel_id=1, source_target_pairs={{0,4},{4,0},{8,12},{12,8},{16,20},{20,16},{24,28},{28,24},{1,5},{5... | collective-permute-start | bytes 393224 | tf_op jit(solution)/shard_map/ppermute | solution.py:421
  12.5 5.0 %collective-permute-start.2 = (f32[2,2,64,128]{3,2,1,0:T(8,128)S(1)}, f32[2,2,64,128]{3,2,1,0:T(8,128)S(1)}, u32[]{:S(2)}, u32[]{:S(2)}) collective-permute-start(f32[2,2,64,128]{3,2,1,0:T(8,128)S(1)} %pad_maximum_fusion.2), channel_id=1, source_target_pairs={{0,8},{4,12},{8,0},{12,4},{16,24},{20,28},{24,16},{28,20},{1,9},{5... | collective-permute-start | bytes 393224 | tf_op jit(solution)/shard_map/ppermute | solution.py:421
  14.1 9.7 %collective-permute-start.12 = (f32[1,512,128]{2,1,0:T(8,128)}, f32[1,512,128]{2,1,0:T(8,128)S(1)}, u32[]{:S(2)}, u32[]{:S(2)}) collective-permute-start(f32[1,512,128]{2,1,0:T(8,128)} %bitcast.17), channel_id=1, source_target_pairs={{0,1},{1,0},{2,3},{3,2},{4,5},{5,4},{6,7},{7,6},{8,9},{9,8},{10,11... | collective-permute-start | bytes 786440 | tf_op jit(solution)/shard_map/ppermute | solution.py:421
  14.1 10.2 %collective-permute-start.11 = (f32[1,512,128]{2,1,0:T(8,128)}, f32[1,512,128]{2,1,0:T(8,128)S(1)}, u32[]{:S(2)}, u32[]{:S(2)}) collective-permute-start(f32[1,512,128]{2,1,0:T(8,128)} %bitcast.18), channel_id=1, source_target_pairs={{0,2},{1,3},{2,0},{3,1},{4,6},{5,7},{6,4},{7,5},{8,10},{9,11},{10,... | collective-permute-start | bytes 786440 | tf_op jit(solution)/shard_map/ppermute | solution.py:421
  15.6 8.8 %collective-permute-start.8 = (f32[4,2,64,128]{3,2,1,0:T(8,128)S(1)}, f32[4,2,64,128]{3,2,1,0:T(8,128)S(1)}, u32[]{:S(2)}, u32[]{:S(2)}) collective-permute-start(f32[4,2,64,128]{3,2,1,0:T(8,128)S(1)} %pad_maximum_fusion.1.refs_4_), channel_id=1, source_target_pairs={{0,8},{4,12},{8,0},{12,4},{16,24},{20,28},{24,16},{28,20},{1,9},{5... | collective-permute-start | bytes 786440 | tf_op jit(solution)/shard_map/ppermute | solution.py:421
  17.5 7.3 %collective-permute-start.3 = (f32[4,2,64,128]{3,2,1,0:T(8,128)S(1)}, f32[4,2,64,128]{3,2,1,0:T(8,128)S(1)}, u32[]{:S(2)}, u32[]{:S(2)}) collective-permute-start(f32[4,2,64,128]{3,2,1,0:T(8,128)S(1)} %pad_maximum_fusion.refs_0_), channel_id=1, source_target_pairs={{0,4},{4,0},{8,12},{12,8},{16,20},{20,16},{24,28},{28,24},{1,5},{5... | collective-permute-start | bytes 786440 | tf_op jit(solution)/shard_map/ppermute | solution.py:421
  19.1 5.9 %collective-permute-start.9 = (f32[4,2,64,128]{3,2,1,0:T(8,128)S(1)}, f32[4,2,64,128]{3,2,1,0:T(8,128)}, u32[]{:S(2)}, u32[]{:S(2)}) collective-permute-start(f32[4,2,64,128]{3,2,1,0:T(8,128)S(1)} %pad_maximum_fusion.1.refs_4_), channel_id=1, source_target_pairs={{0,1},{1,0},{2,3},{3,2},{4,5},{5,4},{6,7},{7,6},{8,9},{9,8},{10,11... | collective-permute-start | bytes 786440 | tf_op jit(solution)/shard_map/ppermute | solution.py:421
  21.0 1.1 %copy-start.1 = (f32[2,4,160,256]{3,2,1,0:T(8,128)}, f32[2,4,160,256]{3,2,1,0:T(8,128)S(1)}, u32[]{:S(2)}) copy-start(f32[2,4,160,256]{3,2,1,0:T(8,128)S(1)} %get-tuple-element.19.refs_12_) | copy-start | bytes 3932164
  22.1 0.9 %copy-start.2 = (bf16[2,3,256,256]{3,2,1,0:T(8,128)(2,1)}, bf16[2,3,256,256]{3,2,1,0:T(8,128)(2,1)S(1)}, u32[]{:S(2)}) copy-start(bf16[2,3,256,256]{3,2,1,0:T(8,128)(2,1)S(1)} %get-tuple-element.20.refs_15_) | copy-start | bytes 2359300
  22.9 0.9 %copy-start.3 = (f8e5m2[2,3,512,256]{3,2,1,0:T(32,128)(4,1)}, f8e5m2[2,3,512,256]{3,2,1,0:T(32,128)(4,1)S(1)}, u32[]{:S(2)}) copy-start(f8e5m2[2,3,512,256]{3,2,1,0:T(32,128)(4,1)S(1)} %get-tuple-element.21.refs_16_) | copy-start | bytes 2359300
  23.8 1.7 %collective-permute-start.4 = (f32[4,2,64,128]{3,2,1,0:T(8,128)S(1)}, f32[4,2,64,128]{3,2,1,0:T(8,128)S(1)}, u32[]{:S(2)}, u32[]{:S(2)}) collective-permute-start(f32[4,2,64,128]{3,2,1,0:T(8,128)S(1)} %pad_maximum_fusion.refs_0_), channel_id=1, source_target_pairs={{0,1},{1,0},{2,3},{3,2},{4,5},{5,4},{6,7},{7,6},{8,9},{9,8},{10,11... | collective-permute-start | bytes 786440 | tf_op jit(solution)/shard_map/ppermute | solution.py:421
  24.3 1.5 %collective-permute-start.13 = (f32[1,512,128]{2,1,0:T(8,128)S(1)}, f32[1,512,128]{2,1,0:T(8,128)S(1)}, u32[]{:S(2)}, u32[]{:S(2)}) collective-permute-start(f32[1,512,128]{2,1,0:T(8,128)S(1)} %collective-permute-done.11.refs_9_), channel_id=1, source_target_pairs={{0,1},{1,0},{2,3},{3,2},{4,5},{5,4},{6,7},{7,6},{8,9},{9,8},{10,11... | collective-permute-start | bytes 786440 | tf_op jit(solution)/shard_map/ppermute | solution.py:421
  24.4 1.8 %collective-permute-start.10 = (f32[4,2,64,128]{3,2,1,0:T(8,128)S(1)}, f32[4,2,64,128]{3,2,1,0:T(8,128)S(1)}, u32[]{:S(2)}, u32[]{:S(2)}) collective-permute-start(f32[4,2,64,128]{3,2,1,0:T(8,128)S(1)} %collective-permute-done.8.refs_5_), channel_id=1, source_target_pairs={{0,1},{1,0},{2,3},{3,2},{4,5},{5,4},{6,7},{7,6},{8,9},{9,8},{10,11... | collective-permute-start | bytes 786440 | tf_op jit(solution)/shard_map/ppermute | solution.py:421
  24.8 1.9 %collective-permute-start.5 = (f32[4,2,64,128]{3,2,1,0:T(8,128)S(1)}, f32[4,2,64,128]{3,2,1,0:T(8,128)}, u32[]{:S(2)}, u32[]{:S(2)}) collective-permute-start(f32[4,2,64,128]{3,2,1,0:T(8,128)S(1)} %collective-permute-done.3.refs_1_), channel_id=1, source_target_pairs={{0,1},{1,0},{2,3},{3,2},{4,5},{5,4},{6,7},{7,6},{8,9},{9,8},{10,11... | collective-permute-start | bytes 786440 | tf_op jit(solution)/shard_map/ppermute | solution.py:421

commit v3 on v2

--- a/solution.py
+++ b/solution.py
@@ -240,10 +240,14 @@
 
 
 def replicated_kernel(hx_bits, place, mask, *refs):
-    s_near, s_turn, s_far, s_both, r_near, r_turn, r_far, r_both, c_near, c_turn, c_far, c_both = refs[:12]
-    spectrum, row_fwd, row_inv, col_main, col_small, out, norms = refs[12:19]
+    sources, (out, norms), held = refs[:17], refs[17:19], refs[38:55]
+    loads = [pltpu.make_async_copy(a, b, refs[55].at[i]) for i, (a, b) in enumerate(zip(sources, held))]
+    for load in loads:
+        load.start()
+    s_near, s_turn, s_far, s_both, r_near, r_turn, r_far, r_both, c_near, c_turn, c_far, c_both = held[:12]
+    spectrum, row_fwd, row_inv, col_main, col_small = held[12:]
     state, total, z, y_hi, y_lo, w_main, w_rest, w_same, u_main, u_rest, u_same, t_main, t_rest, t_same = refs[19:33]
-    left_main, left_small, right_main, right_small, scale = refs[33:]
+    left_main, left_small, right_main, right_small, scale = refs[33:38]
     w, u, t = (w_main, w_rest, w_same), (u_main, u_rest, u_same), (t_main, t_rest, t_same)
     rows, cols = state.shape
     col_windows = col_main.shape[1]
@@ -255,6 +259,8 @@
     near_count = s_near.shape[0]
     here_x, here_y, here_c = place[0], place[1], place[2]
     square = jnp.zeros((8, LANES), jnp.float32)
+    for load in loads[:4]:
+        load.wait()
     for pos in range(2 * near_count):
         s_row = (here_x ^ hx_bits[0][pos]) * block_rows
         s_row = pl.multiple_of(s_row, block_rows)
@@ -266,6 +272,8 @@
                 state[pl.ds(s_row, block_rows), pl.ds(s_col, block_cols)] = value
                 total[pl.ds(s_row, block_rows), pl.ds(s_col, block_cols)] = value
                 square = square + jnp.sum((value * value).reshape(block_rows // 8, 8, block_cols), 0)
+    for load in loads[4:8]:
+        load.wait()
     share = TILE // block_rows
     for pos in range(2 * near_count):
         index = here_x ^ hx_bits[1][pos]
@@ -282,6 +290,8 @@
                 left_main[a, b, pl.ds(sub, block_rows), pl.ds(at, LANES)] = high
                 left_small[a, b, pl.ds(sub, block_rows), pl.ds(at, LANES)] = same
                 left_small[a, b, pl.ds(sub, block_rows), pl.ds(pl.multiple_of(at + TILE, LANES), LANES)] = rest
+    for load in loads[8:12]:
+        load.wait()
     for k in range(2 * c_near.shape[0]):
         for far, ref in enumerate((c_near, c_far) if k < c_near.shape[0] else (c_turn, c_both)):
             lane = ((here_y ^ k) * 2 + (here_c ^ far)) * block_cols
@@ -410,7 +420,12 @@
             at = pl.ds(i, TILE), pl.ds(j, LANES)
             put(w, at, times(state[at], scale[...]))
     norm_lane = lax.broadcasted_iota(jnp.int32, norms.shape, 1)
-    summed, _ = lax.fori_loop(0, ITERS, step, (jnp.zeros(norms.shape, jnp.float32), sum_square))
+    for load in loads[12:]:
+        load.wait()
+    def two_steps(k, carry):
+        return step(2 * k + 1, step(2 * k, carry))
+
+    summed, _ = lax.fori_loop(0, ITERS // 2, two_steps, (jnp.zeros(norms.shape, jnp.float32), sum_square))
     norms[...] = jnp.sqrt(summed / (rows * cols) + tiny_square)
     own_row = pl.multiple_of(here_x * block_rows, block_rows)
     own_col = pl.multiple_of((here_y * 2 + here_c) * block_cols, block_cols)
@@ -471,18 +486,20 @@
         shapes += [(shape, bf16), (shape, small), (shape, small)]
     shapes += [(tiles + (TILE, TILE), bf16), (tiles + (TILE, 2 * TILE), small)]
     shapes += [(tiles + (TILE, TILE), bf16), (tiles + (2 * TILE, TILE), small), ((8, LANES), f32)]
+    operands = (*pieces, spectrum, row_fwd, row_inv, col_main, col_small)
+    shapes += [(v.shape, v.dtype) for v in operands]
     result, norms = pl.pallas_call(
         functools.partial(replicated_kernel, (bit_places(down), bit_places(turned))),
         out_shape=(
             jax.ShapeDtypeStruct((block_rows, block_cols), f32),
             jax.ShapeDtypeStruct((1, ITERS), f32),
         ),
-        in_specs=[smem, smem] + [vmem] * 17,
+        in_specs=[smem, smem] + [pl.BlockSpec(memory_space=pl.ANY)] * 17,
         out_specs=(vmem, vmem),
-        scratch_shapes=[pltpu.VMEM(*s) for s in shapes],
+        scratch_shapes=[pltpu.VMEM(*s) for s in shapes] + [pltpu.SemaphoreType.DMA((len(operands),))],
         compiler_params=pltpu.CompilerParams(vmem_limit_bytes=50 * 1024 * 1024),
         name="replicated_steps",
-    )(place, tile_mask, *pieces, spectrum, row_fwd, row_inv, col_main, col_small)
+    )(place, tile_mask, *operands)
     return result, norms[0]
 
 

time: 58.7 us -> 57.4 us (0.978)
  Pallas kernels: 32.8 us -> 31.5 us
    pallas_call x1, Pallas kernels: 30.9 us -> 29.6 us  [replicated(): pl.pallas_call(functools.partial(replicated_kernel, (bit_places(down), bi...]
where the time goes in v3:
time: 57.4 us; the launch traced here: 56.4 us
  Pallas kernels  31.5 us (55%)
  starting transfers between devices  16.5 us (29%)
  waiting for transfers between devices  3.85 us (7%)
  local copies, waits for them, and re-layouts  2.87 us (5%)
  other arithmetic  0.9 us (2%)
  between operations  0.76 us (1%)
    pallas_call x1, Pallas kernels, replicated(): pl.pallas_call(functools.partial(replicated_kernel, (bit_places(down), bi...  29.6 us
    ppermute x14, starting transfers between devices, swap(): lax.ppermute(value, axis, [(i, i ^ bit) for i in range(lax.axis_size(axis...  16.5 us
    ppermute x14, waiting for transfers between devices, swap(): lax.ppermute(value, axis, [(i, i ^ bit) for i in range(lax.axis_size(axis...  3.85 us
    unnamed x24, local copies, waits for them, and re-layouts  2.86 us
    pallas_call x1, Pallas kernels, setup(): pl.pallas_call(setup_kernel, out_shape=(jax.ShapeDtypeStruct((2, 4, HALF...  1.88 us
  transfers between devices with their start and end apart: 14, of which 6 were waited for; matrix products, arithmetic and copies ran while one was open for 2% of the time, Pallas kernels for 3%

profile of v3, /device:TPU:0, one launch (start us, length us, event | category | flops | bytes accessed | tf_op | source)
XLA Modules:
  0.0 56.4 jit_solution(13012815413319644516)
XLA Ops:
  0.6 0.0 copy-start
  0.6 0.0 copy-start.4
  0.7 0.0 copy-start.7
  0.7 0.0 copy-start.10
  0.7 3.1 %collective-permute-start = (f32[1,64,128]{2,1,0:T(8,128)}, f32[1,64,128]{2,1,0:T(8,128)S(1)}, u32[]{:S(2)}, u32[]{:S(2)}) collective-permute-start(f32[1,64,128]{2,1,0:T(8,128)} %bitcast.20), channel_id=1, source_target_pairs={{0,2},{1,3},{2,0},{3,1},{4,6},{5,7},{6,4},{7,5},{8,10},{9,11},{10,... | collective-permute-start | bytes 98312 | tf_op jit(solution)/shard_map/ppermute | solution.py:436
  3.7 0.0 copy-done
  3.7 0.0 copy-start.9
  3.8 2.7 %collective-permute-start.6 = (f32[1,2,64,128]{3,2,1,0:T(8,128)S(1)}, f32[1,2,64,128]{3,2,1,0:T(8,128)S(1)}, u32[]{:S(2)}, u32[]{:S(2)}) collective-permute-start(f32[1,2,64,128]{3,2,1,0:T(8,128)S(1)} %bitcast_bitcast_fusion), channel_id=1, source_target_pairs={{0,16},{4,20},{8,24},{12,28},{16,0},{20,4},{24,8},{28,12},{1,17},{... | collective-permute-start | bytes 196616 | tf_op jit(solution)/shard_map/ppermute | solution.py:436
  6.4 0.0 collective-permute-done
  6.4 0.8 %maximum_bitcast_fusion = f32[1,2,64,128]{3,2,1,0:T(8,128)S(1)} fusion(f32[1,64,128]{2,1,0:T(8,128)S(1)} %collective-permute-done, f32[1,64,128]{2,1,0:T(8,128)} %bitcast.21), kind=kLoop, calls=%fused_computation.5 | loop fusion | flops 16384 | bytes 131072 | tf_op jit(solution)/shard_map/broadcast_in_dim | solution.py:464
  7.2 0.0 copy-start.5
  7.2 0.0 copy-start.6
  7.2 0.0 copy-start.8
  7.2 0.0 copy-start.11
  7.2 2.6 %collective-permute-start.1 = (f32[1,2,64,128]{3,2,1,0:T(8,128)S(1)}, f32[1,2,64,128]{3,2,1,0:T(8,128)S(1)}, u32[]{:S(2)}, u32[]{:S(2)}) collective-permute-start(f32[1,2,64,128]{3,2,1,0:T(8,128)S(1)} %maximum_bitcast_fusion), channel_id=1, source_target_pairs={{0,16},{4,20},{8,24},{12,28},{16,0},{20,4},{24,8},{28,12},{1,17},{... | collective-permute-start | bytes 196616 | tf_op jit(solution)/shard_map/ppermute | solution.py:436
  9.8 0.0 collective-permute-done.6
  9.8 1.6 %collective-permute-start.7 = (f32[2,2,64,128]{3,2,1,0:T(8,128)S(1)}, f32[2,2,64,128]{3,2,1,0:T(8,128)S(1)}, u32[]{:S(2)}, u32[]{:S(2)}) collective-permute-start(f32[2,2,64,128]{3,2,1,0:T(8,128)S(1)} %pad_maximum_fusion.3), channel_id=1, source_target_pairs={{0,4},{4,0},{8,12},{12,8},{16,20},{20,16},{24,28},{28,24},{1,5},{5... | collective-permute-start | bytes 393224 | tf_op jit(solution)/shard_map/ppermute | solution.py:436
  11.4 1.1 %collective-permute-done.1 = f32[1,2,64,128]{3,2,1,0:T(8,128)S(1)} collective-permute-done((f32[1,2,64,128]{3,2,1,0:T(8,128)S(1)}, f32[1,2,64,128]{3,2,1,0:T(8,128)S(1)}, u32[]{:S(2)}, u32[]{:S(2)}) %collective-permute-start.1) | collective-permute-done | bytes 65568 | tf_op jit(solution)/shard_map/ppermute | solution.py:436
  12.5 1.6 %collective-permute-start.2 = (f32[2,2,64,128]{3,2,1,0:T(8,128)S(1)}, f32[2,2,64,128]{3,2,1,0:T(8,128)S(1)}, u32[]{:S(2)}, u32[]{:S(2)}) collective-permute-start(f32[2,2,64,128]{3,2,1,0:T(8,128)S(1)} %pad_maximum_fusion.2), channel_id=1, source_target_pairs={{0,8},{4,12},{8,0},{12,4},{16,24},{20,28},{24,16},{28,20},{1,9},{5... | collective-permute-start | bytes 393224 | tf_op jit(solution)/shard_map/ppermute | solution.py:436
  14.1 0.0 collective-permute-start.12
  14.1 1.5 %collective-permute-start.11 = (f32[1,512,128]{2,1,0:T(8,128)}, f32[1,512,128]{2,1,0:T(8,128)S(1)}, u32[]{:S(2)}, u32[]{:S(2)}) collective-permute-start(f32[1,512,128]{2,1,0:T(8,128)} %bitcast.18), channel_id=1, source_target_pairs={{0,2},{1,3},{2,0},{3,1},{4,6},{5,7},{6,4},{7,5},{8,10},{9,11},{10,... | collective-permute-start | bytes 786440 | tf_op jit(solution)/shard_map/ppermute | solution.py:436
  15.6 0.0 collective-permute-done.7
  15.6 0.9 %collective-permute-start.8 = (f32[4,2,64,128]{3,2,1,0:T(8,128)S(1)}, f32[4,2,64,128]{3,2,1,0:T(8,128)S(1)}, u32[]{:S(2)}, u32[]{:S(2)}) collective-permute-start(f32[4,2,64,128]{3,2,1,0:T(8,128)S(1)} %pad_maximum_fusion.1.refs_4_), channel_id=1, source_target_pairs={{0,8},{4,12},{8,0},{12,4},{16,24},{20,28},{24,16},{28,20},{1,9},{5... | collective-permute-start | bytes 786440 | tf_op jit(solution)/shard_map/ppermute | solution.py:436
  16.5 1.0 %collective-permute-done.2 = f32[2,2,64,128]{3,2,1,0:T(8,128)S(1)} collective-permute-done((f32[2,2,64,128]{3,2,1,0:T(8,128)S(1)}, f32[2,2,64,128]{3,2,1,0:T(8,128)S(1)}, u32[]{:S(2)}, u32[]{:S(2)}) %collective-permute-start.2) | collective-permute-done | bytes 131104 | tf_op jit(solution)/shard_map/ppermute | solution.py:436
  17.5 1.6 %collective-permute-start.3 = (f32[4,2,64,128]{3,2,1,0:T(8,128)S(1)}, f32[4,2,64,128]{3,2,1,0:T(8,128)S(1)}, u32[]{:S(2)}, u32[]{:S(2)}) collective-permute-start(f32[4,2,64,128]{3,2,1,0:T(8,128)S(1)} %pad_maximum_fusion.refs_0_), channel_id=1, source_target_pairs={{0,4},{4,0},{8,12},{12,8},{16,20},{20,16},{24,28},{28,24},{1,5},{5... | collective-permute-start | bytes 786440 | tf_op jit(solution)/shard_map/ppermute | solution.py:436
  19.1 0.0 collective-permute-start.9
  19.1 0.0 copy-done.4
  19.1 0.0 copy-done.7
  19.1 0.0 copy-done.10
  19.1 0.0 copy-done.9
  19.1 1.9 %setup.1 = (f32[2,4,160,256]{3,2,1,0:T(8,128)S(1)}, bf16[2,3,256,256]{3,2,1,0:T(8,128)(2,1)S(1)}, f8e5m2[2,3,512,256]{3,2,1,0:T(32,128)(4,1)S(1)}) custom-call(f32[65,65]{1,0:T(8,128)S(1)} %copy-done.10, f32[2,320,65]{2,1,0:T(8,128)S(1)} %copy-done.7, f32[2,65,256]{2,1,0:T(8,128)S(1)} %copy-done.9, bf16[4,256,256]{2,1,0:T(8,128)(2,1)S(1)} %copy-done.4), custom_call_target="tpu_custom_call" | custom-call | tf_op jit(solution)/shard_map/setup/pallas_call | solution.py:212
  21.0 0.0 copy-start.1
  21.0 1.1 %copy-done.1 = f32[2,4,160,256]{3,2,1,0:T(8,128)} copy-done((f32[2,4,160,256]{3,2,1,0:T(8,128)}, f32[2,4,160,256]{3,2,1,0:T(8,128)S(1)}, u32[]{:S(2)}) %copy-start.1) | copy-done | bytes 1310744
  22.1 0.0 copy-start.2
  22.1 0.9 %copy-done.2 = bf16[2,3,256,256]{3,2,1,0:T(8,128)(2,1)} copy-done((bf16[2,3,256,256]{3,2,1,0:T(8,128)(2,1)}, bf16[2,3,256,256]{3,2,1,0:T(8,128)(2,1)S(1)}, u32[]{:S(2)}) %copy-start.2) | copy-done | bytes 786456
  22.9 0.0 copy-start.3
  22.9 0.9 %copy-done.3 = f8e5m2[2,3,512,256]{3,2,1,0:T(32,128)(4,1)} copy-done((f8e5m2[2,3,512,256]{3,2,1,0:T(32,128)(4,1)}, f8e5m2[2,3,512,256]{3,2,1,0:T(32,128)(4,1)S(1)}, u32[]{:S(2)}) %copy-start.3) | copy-done | bytes 786456
  23.8 0.0 collective-permute-done.12.refs_10_
  23.8 0.5 collective-permute-start.4
  24.3 0.0 collective-permute-done.11.refs_9_
  24.3 0.1 collective-permute-start.13
  24.4 0.0 collective-permute-done.8.refs_5_
  24.4 0.4 collective-permute-start.10
  24.8 0.0 collective-permute-done.3.refs_1_
  24.8 0.1 collective-permute-start.5
  24.9 0.1 pad_add_fusion.place
  25.0 0.0 collective-permute-done.9.refs_6_
  25.0 0.5 collective-permute-done.4.refs_2_
  25.5 0.4 collective-permute-done.13.refs_11_
  25.9 0.4 collective-permute-done.10.refs_7_
  26.2 0.5 collective-permute-done.5.refs_3_
  26.7 0.0 copy-done.5
  26.7 0.0 copy-done.6
  26.8 0.0 copy-done.8
  26.8 0.0 copy-done.11
  26.8 29.6 %replicated_steps.1 = (f32[64,128]{1,0:T(8,128)}, f32[1,8]{1,0:T(1,128)}) custom-call(s32[3]{0:T(128)S(1)} %pad_add_fusion.place, s32[2,2]{1,0:T(2,128)S(1)} %copy-done.11, f32[4,2,64,128]{3,2,1,0:T(8,128)S(1)} %pad_maximum_fusion.refs_0_, f32[4,2,64,128]{3,2,1,0:T(8,128)S(1)} %collective-permute-done.3.refs_1_, ...), custom_call_target="tpu_custom_call" | custom-call | tf_op jit(solution)/shard_map/replicated_steps/pallas_call | solution.py:491
  (5 shorter events, 0.1 us)
Async XLA Ops:
  0.6 3.1 %copy-start = (f32[64,512]{1,0:T(8,128)S(1)}, f32[64,512]{1,0:T(8,128)}, u32[]{:S(2)}) copy-start(f32[64,512]{1,0:T(8,128)} %param.12) | copy-start | bytes 393220
  0.6 18.4 %copy-start.4 = (bf16[4,256,256]{2,1,0:T(8,128)(2,1)S(1)}, bf16[4,256,256]{2,1,0:T(8,128)(2,1)}, u32[]{:S(2)}) copy-start(bf16[4,256,256]{2,1,0:T(8,128)(2,1)} %constant.52.clone.col_base) | copy-start | bytes 1572868
  0.7 18.4 %copy-start.7 = (f32[2,320,65]{2,1,0:T(8,128)S(1)}, f32[2,320,65]{2,1,0:T(8,128)}, u32[]{:S(2)}) copy-start(f32[2,320,65]{2,1,0:T(8,128)} %constant.50.clone.row_waves) | copy-start | bytes 499204
  0.7 18.4 %copy-start.10 = (f32[65,65]{1,0:T(8,128)S(1)}, f32[65,65]{1,0:T(8,128)}, u32[]{:S(2)}) copy-start(f32[65,65]{1,0:T(8,128)} %coeffs) | copy-start | bytes 50704
  0.7 5.7 %collective-permute-start = (f32[1,64,128]{2,1,0:T(8,128)}, f32[1,64,128]{2,1,0:T(8,128)S(1)}, u32[]{:S(2)}, u32[]{:S(2)}) collective-permute-start(f32[1,64,128]{2,1,0:T(8,128)} %bitcast.20), channel_id=1, source_target_pairs={{0,2},{1,3},{2,0},{3,1},{4,6},{5,7},{6,4},{7,5},{8,10},{9,11},{10,... | collective-permute-start | bytes 98312 | tf_op jit(solution)/shard_map/ppermute | solution.py:436
  3.7 15.4 %copy-start.9 = (f32[2,65,256]{2,1,0:T(8,128)S(1)}, f32[2,65,256]{2,1,0:T(8,128)}, u32[]{:S(2)}) copy-start(f32[2,65,256]{2,1,0:T(8,128)} %constant.51.clone.col_waves) | copy-start | bytes 399364
  3.8 6.0 %collective-permute-start.6 = (f32[1,2,64,128]{3,2,1,0:T(8,128)S(1)}, f32[1,2,64,128]{3,2,1,0:T(8,128)S(1)}, u32[]{:S(2)}, u32[]{:S(2)}) collective-permute-start(f32[1,2,64,128]{3,2,1,0:T(8,128)S(1)} %bitcast_bitcast_fusion), channel_id=1, source_target_pairs={{0,16},{4,20},{8,24},{12,28},{16,0},{20,4},{24,8},{28,12},{1,17},{... | collective-permute-start | bytes 196616 | tf_op jit(solution)/shard_map/ppermute | solution.py:436
  7.2 19.6 %copy-start.5 = (bf16[2,160,480]{2,1,0:T(8,128)(2,1)S(1)}, bf16[2,160,480]{2,1,0:T(8,128)(2,1)}, u32[]{:S(2)}) copy-start(bf16[2,160,480]{2,1,0:T(8,128)(2,1)} %constant.54.clone.refs_14_) | copy-start | bytes 921604
  7.2 19.6 %copy-start.6 = (bf16[2,160,480]{2,1,0:T(8,128)(2,1)S(1)}, bf16[2,160,480]{2,1,0:T(8,128)(2,1)}, u32[]{:S(2)}) copy-start(bf16[2,160,480]{2,1,0:T(8,128)(2,1)} %constant.53.clone.refs_13_) | copy-start | bytes 921604
  7.2 19.6 %copy-start.8 = (f32[512,128]{1,0:T(8,128)S(1)}, f32[512,128]{1,0:T(8,128)}, u32[]{:S(2)}) copy-start(f32[512,128]{1,0:T(8,128)} %param.13) | copy-start | bytes 786436
  7.2 19.6 %copy-start.11 = (s32[2,2]{1,0:T(2,128)S(1)}, s32[2,2]{1,0:T(2,128)}, u32[]{:S(2)}) copy-start(s32[2,2]{1,0:T(2,128)} %mask.1) | copy-start | bytes 52
  7.2 5.2 %collective-permute-start.1 = (f32[1,2,64,128]{3,2,1,0:T(8,128)S(1)}, f32[1,2,64,128]{3,2,1,0:T(8,128)S(1)}, u32[]{:S(2)}, u32[]{:S(2)}) collective-permute-start(f32[1,2,64,128]{3,2,1,0:T(8,128)S(1)} %maximum_bitcast_fusion), channel_id=1, source_target_pairs={{0,16},{4,20},{8,24},{12,28},{16,0},{20,4},{24,8},{28,12},{1,17},{... | collective-permute-start | bytes 196616 | tf_op jit(solution)/shard_map/ppermute | solution.py:436
  9.8 5.7 %collective-permute-start.7 = (f32[2,2,64,128]{3,2,1,0:T(8,128)S(1)}, f32[2,2,64,128]{3,2,1,0:T(8,128)S(1)}, u32[]{:S(2)}, u32[]{:S(2)}) collective-permute-start(f32[2,2,64,128]{3,2,1,0:T(8,128)S(1)} %pad_maximum_fusion.3), channel_id=1, source_target_pairs={{0,4},{4,0},{8,12},{12,8},{16,20},{20,16},{24,28},{28,24},{1,5},{5... | collective-permute-start | bytes 393224 | tf_op jit(solution)/shard_map/ppermute | solution.py:436
  12.5 5.0 %collective-permute-start.2 = (f32[2,2,64,128]{3,2,1,0:T(8,128)S(1)}, f32[2,2,64,128]{3,2,1,0:T(8,128)S(1)}, u32[]{:S(2)}, u32[]{:S(2)}) collective-permute-start(f32[2,2,64,128]{3,2,1,0:T(8,128)S(1)} %pad_maximum_fusion.2), channel_id=1, source_target_pairs={{0,8},{4,12},{8,0},{12,4},{16,24},{20,28},{24,16},{28,20},{1,9},{5... | collective-permute-start | bytes 393224 | tf_op jit(solution)/shard_map/ppermute | solution.py:436
  14.1 9.7 %collective-permute-start.12 = (f32[1,512,128]{2,1,0:T(8,128)}, f32[1,512,128]{2,1,0:T(8,128)S(1)}, u32[]{:S(2)}, u32[]{:S(2)}) collective-permute-start(f32[1,512,128]{2,1,0:T(8,128)} %bitcast.17), channel_id=1, source_target_pairs={{0,1},{1,0},{2,3},{3,2},{4,5},{5,4},{6,7},{7,6},{8,9},{9,8},{10,11... | collective-permute-start | bytes 786440 | tf_op jit(solution)/shard_map/ppermute | solution.py:436
  14.1 10.2 %collective-permute-start.11 = (f32[1,512,128]{2,1,0:T(8,128)}, f32[1,512,128]{2,1,0:T(8,128)S(1)}, u32[]{:S(2)}, u32[]{:S(2)}) collective-permute-start(f32[1,512,128]{2,1,0:T(8,128)} %bitcast.18), channel_id=1, source_target_pairs={{0,2},{1,3},{2,0},{3,1},{4,6},{5,7},{6,4},{7,5},{8,10},{9,11},{10,... | collective-permute-start | bytes 786440 | tf_op jit(solution)/shard_map/ppermute | solution.py:436
  15.6 8.8 %collective-permute-start.8 = (f32[4,2,64,128]{3,2,1,0:T(8,128)S(1)}, f32[4,2,64,128]{3,2,1,0:T(8,128)S(1)}, u32[]{:S(2)}, u32[]{:S(2)}) collective-permute-start(f32[4,2,64,128]{3,2,1,0:T(8,128)S(1)} %pad_maximum_fusion.1.refs_4_), channel_id=1, source_target_pairs={{0,8},{4,12},{8,0},{12,4},{16,24},{20,28},{24,16},{28,20},{1,9},{5... | collective-permute-start | bytes 786440 | tf_op jit(solution)/shard_map/ppermute | solution.py:436
  17.5 7.3 %collective-permute-start.3 = (f32[4,2,64,128]{3,2,1,0:T(8,128)S(1)}, f32[4,2,64,128]{3,2,1,0:T(8,128)S(1)}, u32[]{:S(2)}, u32[]{:S(2)}) collective-permute-start(f32[4,2,64,128]{3,2,1,0:T(8,128)S(1)} %pad_maximum_fusion.refs_0_), channel_id=1, source_target_pairs={{0,4},{4,0},{8,12},{12,8},{16,20},{20,16},{24,28},{28,24},{1,5},{5... | collective-permute-start | bytes 786440 | tf_op jit(solution)/shard_map/ppermute | solution.py:436
  19.1 5.9 %collective-permute-start.9 = (f32[4,2,64,128]{3,2,1,0:T(8,128)S(1)}, f32[4,2,64,128]{3,2,1,0:T(8,128)}, u32[]{:S(2)}, u32[]{:S(2)}) collective-permute-start(f32[4,2,64,128]{3,2,1,0:T(8,128)S(1)} %pad_maximum_fusion.1.refs_4_), channel_id=1, source_target_pairs={{0,1},{1,0},{2,3},{3,2},{4,5},{5,4},{6,7},{7,6},{8,9},{9,8},{10,11... | collective-permute-start | bytes 786440 | tf_op jit(solution)/shard_map/ppermute | solution.py:436
  21.0 1.1 %copy-start.1 = (f32[2,4,160,256]{3,2,1,0:T(8,128)}, f32[2,4,160,256]{3,2,1,0:T(8,128)S(1)}, u32[]{:S(2)}) copy-start(f32[2,4,160,256]{3,2,1,0:T(8,128)S(1)} %get-tuple-element.19.refs_12_) | copy-start | bytes 3932164
  22.1 0.9 %copy-start.2 = (bf16[2,3,256,256]{3,2,1,0:T(8,128)(2,1)}, bf16[2,3,256,256]{3,2,1,0:T(8,128)(2,1)S(1)}, u32[]{:S(2)}) copy-start(bf16[2,3,256,256]{3,2,1,0:T(8,128)(2,1)S(1)} %get-tuple-element.20.refs_15_) | copy-start | bytes 2359300
  22.9 0.9 %copy-start.3 = (f8e5m2[2,3,512,256]{3,2,1,0:T(32,128)(4,1)}, f8e5m2[2,3,512,256]{3,2,1,0:T(32,128)(4,1)S(1)}, u32[]{:S(2)}) copy-start(f8e5m2[2,3,512,256]{3,2,1,0:T(32,128)(4,1)S(1)} %get-tuple-element.21.refs_16_) | copy-start | bytes 2359300
  23.8 1.7 %collective-permute-start.4 = (f32[4,2,64,128]{3,2,1,0:T(8,128)S(1)}, f32[4,2,64,128]{3,2,1,0:T(8,128)S(1)}, u32[]{:S(2)}, u32[]{:S(2)}) collective-permute-start(f32[4,2,64,128]{3,2,1,0:T(8,128)S(1)} %pad_maximum_fusion.refs_0_), channel_id=1, source_target_pairs={{0,1},{1,0},{2,3},{3,2},{4,5},{5,4},{6,7},{7,6},{8,9},{9,8},{10,11... | collective-permute-start | bytes 786440 | tf_op jit(solution)/shard_map/ppermute | solution.py:436
  24.3 1.5 %collective-permute-start.13 = (f32[1,512,128]{2,1,0:T(8,128)S(1)}, f32[1,512,128]{2,1,0:T(8,128)S(1)}, u32[]{:S(2)}, u32[]{:S(2)}) collective-permute-start(f32[1,512,128]{2,1,0:T(8,128)S(1)} %collective-permute-done.11.refs_9_), channel_id=1, source_target_pairs={{0,1},{1,0},{2,3},{3,2},{4,5},{5,4},{6,7},{7,6},{8,9},{9,8},{10,11... | collective-permute-start | bytes 786440 | tf_op jit(solution)/shard_map/ppermute | solution.py:436
  24.4 1.8 %collective-permute-start.10 = (f32[4,2,64,128]{3,2,1,0:T(8,128)S(1)}, f32[4,2,64,128]{3,2,1,0:T(8,128)S(1)}, u32[]{:S(2)}, u32[]{:S(2)}) collective-permute-start(f32[4,2,64,128]{3,2,1,0:T(8,128)S(1)} %collective-permute-done.8.refs_5_), channel_id=1, source_target_pairs={{0,1},{1,0},{2,3},{3,2},{4,5},{5,4},{6,7},{7,6},{8,9},{9,8},{10,11... | collective-permute-start | bytes 786440 | tf_op jit(solution)/shard_map/ppermute | solution.py:436
  24.8 1.9 %collective-permute-start.5 = (f32[4,2,64,128]{3,2,1,0:T(8,128)S(1)}, f32[4,2,64,128]{3,2,1,0:T(8,128)}, u32[]{:S(2)}, u32[]{:S(2)}) collective-permute-start(f32[4,2,64,128]{3,2,1,0:T(8,128)S(1)} %collective-permute-done.3.refs_1_), channel_id=1, source_target_pairs={{0,1},{1,0},{2,3},{3,2},{4,5},{5,4},{6,7},{7,6},{8,9},{9,8},{10,11... | collective-permute-start | bytes 786440 | tf_op jit(solution)/shard_map/ppermute | solution.py:436

commit v4 on v3

--- a/solution.py
+++ b/solution.py
@@ -364,22 +364,23 @@
     def update(a, keep, take, factor):
         ra = pl.ds(a * TILE, TILE)
         square = jnp.zeros((8, LANES), jnp.float32)
-        parts = []
-        for b in range(col_windows):
-            at = ra, pl.ds(b * TILE, TILE)
-            lhs, lhs_small, rhs, rhs_small = [u_main[at]], [u_rest[at], u_same[at]], [col_main[1, b]], [col_small[1, b]]
-            if b % 2 == 0:
-                at = ra, pl.ds(b // 2 * TILE, TILE)
-                lhs, lhs_small = lhs + [t_main[at]], lhs_small + [t_rest[at], t_same[at]]
-                rhs, rhs_small = rhs + [right_main[a, b // 2]], rhs_small + [right_small[a, b // 2]]
-            parts.append(
-                dot32(jnp.concatenate(lhs, 1), jnp.concatenate(rhs, 0))
-                + dot32(jnp.concatenate(lhs_small, 1), jnp.concatenate(rhs_small, 0))
-            )
-        for j in range(cols // HALF):
-            pieces = [parts[b][:, (j - b) * HALF : (j - b + 1) * HALF] for b in range(col_windows) if b <= j <= b + 1]
-            cj = pl.ds(j * HALF, HALF)
-            residual = keep * state[ra, cj] - times(functools.reduce(jnp.add, pieces), take)
+        before = None
+        for b in range(col_windows + 1):
+            done = before
+            if b < col_windows:
+                at = ra, pl.ds(b * TILE, TILE)
+                lhs, lhs_small, rhs, rhs_small = [u_main[at]], [u_rest[at], u_same[at]], [col_main[1, b]], [col_small[1, b]]
+                if b % 2 == 0:
+                    at = ra, pl.ds(b // 2 * TILE, TILE)
+                    lhs, lhs_small = lhs + [t_main[at]], lhs_small + [t_rest[at], t_same[at]]
+                    rhs, rhs_small = rhs + [right_main[a, b // 2]], rhs_small + [right_small[a, b // 2]]
+                cells = dot32(jnp.concatenate(lhs, 1), jnp.concatenate(rhs, 0)) + dot32(
+                    jnp.concatenate(lhs_small, 1), jnp.concatenate(rhs_small, 0)
+                )
+                done = cells[:, :HALF] if before is None else before + cells[:, :HALF]
+                before = cells[:, HALF:]
+            cj = pl.ds(b * HALF, HALF)
+            residual = keep * state[ra, cj] - times(done, take)
             state[ra, cj] = residual
             total[ra, cj] = total[ra, cj] + relax_step * residual
             put(w, (ra, cj), times(residual, factor))
@@ -497,7 +498,7 @@
         in_specs=[smem, smem] + [pl.BlockSpec(memory_space=pl.ANY)] * 17,
         out_specs=(vmem, vmem),
         scratch_shapes=[pltpu.VMEM(*s) for s in shapes] + [pltpu.SemaphoreType.DMA((len(operands),))],
-        compiler_params=pltpu.CompilerParams(vmem_limit_bytes=50 * 1024 * 1024),
+        compiler_params=pltpu.CompilerParams(vmem_limit_bytes=50432 * 1024),
         name="replicated_steps",
     )(place, tile_mask, *operands)
     return result, norms[0]

time: 57.4 us -> 56.5 us (0.984); the launches traced: 56.4 us -> 56.1 us
  local copies, waits for them, and re-layouts: 2.87 us -> 1.99 us
  waiting for transfers between devices: 3.85 us -> 4.67 us
    unnamed x24 -> x22, local copies, waits for them, and re-layouts: 2.86 us -> 1.99 us
    ppermute x14, waiting for transfers between devices: 3.85 us -> 4.67 us  [swap(): lax.ppermute(value, axis, [(i, i ^ bit) for i in range(lax.axis_size(axis...]
  transfers between devices with their start and end apart: 14 -> 14, of which waited for: 6 -> 7; matrix products, arithmetic and copies ran while one was open for 2% -> 2% of each run, Pallas kernels for 3% -> 3%
where the time goes in v4:
time: 56.5 us; the launch traced here: 56.1 us
  Pallas kernels  31.5 us (56%)
  starting transfers between devices  16.3 us (29%)
  waiting for transfers between devices  4.67 us (8%)
  local copies, waits for them, and re-layouts  1.99 us (4%)
  other arithmetic  0.89 us (2%)
  between operations  0.77 us (1%)
    pallas_call x1, Pallas kernels, replicated(): pl.pallas_call(functools.partial(replicated_kernel, (bit_places(down), bi...  29.6 us
    ppermute x14, starting transfers between devices, swap(): lax.ppermute(value, axis, [(i, i ^ bit) for i in range(lax.axis_size(axis...  16.3 us
    ppermute x14, waiting for transfers between devices, swap(): lax.ppermute(value, axis, [(i, i ^ bit) for i in range(lax.axis_size(axis...  4.67 us
    unnamed x22, local copies, waits for them, and re-layouts  1.99 us
    pallas_call x1, Pallas kernels, setup(): pl.pallas_call(setup_kernel, out_shape=(jax.ShapeDtypeStruct((2, 4, HALF...  1.88 us
  transfers between devices with their start and end apart: 14, of which 7 were waited for; matrix products, arithmetic and copies ran while one was open for 2% of the time, Pallas kernels for 3%

profile of v4, /device:TPU:0, one launch (start us, length us, event | category | flops | bytes accessed | tf_op | source)
XLA Modules:
  0.0 56.1 jit_solution(3811178195787637245)
XLA Ops:
  0.6 0.0 copy-start
  0.6 0.0 copy-start.3
  0.7 0.0 copy-start.6
  0.7 0.0 copy-start.9
  0.7 3.1 %collective-permute-start = (f32[1,64,128]{2,1,0:T(8,128)}, f32[1,64,128]{2,1,0:T(8,128)S(1)}, u32[]{:S(2)}, u32[]{:S(2)}) collective-permute-start(f32[1,64,128]{2,1,0:T(8,128)} %bitcast.20), channel_id=1, source_target_pairs={{0,2},{1,3},{2,0},{3,1},{4,6},{5,7},{6,4},{7,5},{8,10},{9,11},{10,... | collective-permute-start | bytes 98312 | tf_op jit(solution)/shard_map/ppermute | solution.py:437
  3.7 0.0 copy-done
  3.7 0.0 copy-start.8
  3.8 2.7 %collective-permute-start.6 = (f32[1,2,64,128]{3,2,1,0:T(8,128)S(1)}, f32[1,2,64,128]{3,2,1,0:T(8,128)S(1)}, u32[]{:S(2)}, u32[]{:S(2)}) collective-permute-start(f32[1,2,64,128]{3,2,1,0:T(8,128)S(1)} %bitcast_bitcast_fusion), channel_id=1, source_target_pairs={{0,16},{4,20},{8,24},{12,28},{16,0},{20,4},{24,8},{28,12},{1,17},{... | collective-permute-start | bytes 196616 | tf_op jit(solution)/shard_map/ppermute | solution.py:437
  6.4 0.0 collective-permute-done
  6.4 0.8 %maximum_bitcast_fusion = f32[1,2,64,128]{3,2,1,0:T(8,128)S(1)} fusion(f32[1,64,128]{2,1,0:T(8,128)S(1)} %collective-permute-done, f32[1,64,128]{2,1,0:T(8,128)} %bitcast.21), kind=kLoop, calls=%fused_computation.5 | loop fusion | flops 16384 | bytes 131072 | tf_op jit(solution)/shard_map/broadcast_in_dim | solution.py:465
  7.2 0.0 copy-start.4
  7.2 0.0 copy-start.5
  7.2 0.0 copy-start.7
  7.2 0.0 copy-start.10
  7.2 2.6 %collective-permute-start.1 = (f32[1,2,64,128]{3,2,1,0:T(8,128)S(1)}, f32[1,2,64,128]{3,2,1,0:T(8,128)S(1)}, u32[]{:S(2)}, u32[]{:S(2)}) collective-permute-start(f32[1,2,64,128]{3,2,1,0:T(8,128)S(1)} %maximum_bitcast_fusion), channel_id=1, source_target_pairs={{0,16},{4,20},{8,24},{12,28},{16,0},{20,4},{24,8},{28,12},{1,17},{... | collective-permute-start | bytes 196616 | tf_op jit(solution)/shard_map/ppermute | solution.py:437
  9.8 0.0 collective-permute-done.6
  9.8 1.6 %collective-permute-start.7 = (f32[2,2,64,128]{3,2,1,0:T(8,128)S(1)}, f32[2,2,64,128]{3,2,1,0:T(8,128)S(1)}, u32[]{:S(2)}, u32[]{:S(2)}) collective-permute-start(f32[2,2,64,128]{3,2,1,0:T(8,128)S(1)} %pad_maximum_fusion.3), channel_id=1, source_target_pairs={{0,4},{4,0},{8,12},{12,8},{16,20},{20,16},{24,28},{28,24},{1,5},{5... | collective-permute-start | bytes 393224 | tf_op jit(solution)/shard_map/ppermute | solution.py:437
  11.4 1.1 %collective-permute-done.1 = f32[1,2,64,128]{3,2,1,0:T(8,128)S(1)} collective-permute-done((f32[1,2,64,128]{3,2,1,0:T(8,128)S(1)}, f32[1,2,64,128]{3,2,1,0:T(8,128)S(1)}, u32[]{:S(2)}, u32[]{:S(2)}) %collective-permute-start.1) | collective-permute-done | bytes 65568 | tf_op jit(solution)/shard_map/ppermute | solution.py:437
  12.5 1.6 %collective-permute-start.2 = (f32[2,2,64,128]{3,2,1,0:T(8,128)S(1)}, f32[2,2,64,128]{3,2,1,0:T(8,128)S(1)}, u32[]{:S(2)}, u32[]{:S(2)}) collective-permute-start(f32[2,2,64,128]{3,2,1,0:T(8,128)S(1)} %pad_maximum_fusion.2), channel_id=1, source_target_pairs={{0,8},{4,12},{8,0},{12,4},{16,24},{20,28},{24,16},{28,20},{1,9},{5... | collective-permute-start | bytes 393224 | tf_op jit(solution)/shard_map/ppermute | solution.py:437
  14.1 0.0 collective-permute-start.12
  14.1 1.5 %collective-permute-start.11 = (f32[1,512,128]{2,1,0:T(8,128)}, f32[1,512,128]{2,1,0:T(8,128)}, u32[]{:S(2)}, u32[]{:S(2)}) collective-permute-start(f32[1,512,128]{2,1,0:T(8,128)} %bitcast.18), channel_id=1, source_target_pairs={{0,2},{1,3},{2,0},{3,1},{4,6},{5,7},{6,4},{7,5},{8,10},{9,11},{10,... | collective-permute-start | bytes 786440 | tf_op jit(solution)/shard_map/ppermute | solution.py:437
  15.6 0.0 collective-permute-done.7
  15.6 0.9 %collective-permute-start.8 = (f32[4,2,64,128]{3,2,1,0:T(8,128)S(1)}, f32[4,2,64,128]{3,2,1,0:T(8,128)}, u32[]{:S(2)}, u32[]{:S(2)}) collective-permute-start(f32[4,2,64,128]{3,2,1,0:T(8,128)S(1)} %pad_maximum_fusion.1.refs_4_), channel_id=1, source_target_pairs={{0,8},{4,12},{8,0},{12,4},{16,24},{20,28},{24,16},{28,20},{1,9},{5... | collective-permute-start | bytes 786440 | tf_op jit(solution)/shard_map/ppermute | solution.py:437
  16.5 1.0 %collective-permute-done.2 = f32[2,2,64,128]{3,2,1,0:T(8,128)S(1)} collective-permute-done((f32[2,2,64,128]{3,2,1,0:T(8,128)S(1)}, f32[2,2,64,128]{3,2,1,0:T(8,128)S(1)}, u32[]{:S(2)}, u32[]{:S(2)}) %collective-permute-start.2) | collective-permute-done | bytes 131104 | tf_op jit(solution)/shard_map/ppermute | solution.py:437
  17.5 1.6 %collective-permute-start.3 = (f32[4,2,64,128]{3,2,1,0:T(8,128)S(1)}, f32[4,2,64,128]{3,2,1,0:T(8,128)}, u32[]{:S(2)}, u32[]{:S(2)}) collective-permute-start(f32[4,2,64,128]{3,2,1,0:T(8,128)S(1)} %pad_maximum_fusion.refs_0_), channel_id=1, source_target_pairs={{0,4},{4,0},{8,12},{12,8},{16,20},{20,16},{24,28},{28,24},{1,5},{5... | collective-permute-start | bytes 786440 | tf_op jit(solution)/shard_map/ppermute | solution.py:437
  19.1 0.0 collective-permute-start.9
  19.1 0.0 copy-done.3
  19.1 0.0 copy-done.6
  19.1 0.0 copy-done.9
  19.1 0.0 copy-done.8
  19.1 1.9 %setup.1 = (f32[2,4,160,256]{3,2,1,0:T(8,128)S(1)}, bf16[2,3,256,256]{3,2,1,0:T(8,128)(2,1)S(1)}, f8e5m2[2,3,512,256]{3,2,1,0:T(32,128)(4,1)S(1)}) custom-call(f32[65,65]{1,0:T(8,128)S(1)} %copy-done.9, f32[2,320,65]{2,1,0:T(8,128)S(1)} %copy-done.6, f32[2,65,256]{2,1,0:T(8,128)S(1)} %copy-done.8, bf16[4,256,256]{2,1,0:T(8,128)(2,1)S(1)} %copy-done.3), custom_call_target="tpu_custom_call" | custom-call | tf_op jit(solution)/shard_map/setup/pallas_call | solution.py:212
  21.0 0.0 copy-start.1
  21.0 1.1 %copy-done.1 = f32[2,4,160,256]{3,2,1,0:T(8,128)} copy-done((f32[2,4,160,256]{3,2,1,0:T(8,128)}, f32[2,4,160,256]{3,2,1,0:T(8,128)S(1)}, u32[]{:S(2)}) %copy-start.1) | copy-done | bytes 1310744
  22.1 0.0 copy-start.2
  22.1 0.9 %copy-done.2 = f8e5m2[2,3,512,256]{3,2,1,0:T(32,128)(4,1)} copy-done((f8e5m2[2,3,512,256]{3,2,1,0:T(32,128)(4,1)}, f8e5m2[2,3,512,256]{3,2,1,0:T(32,128)(4,1)S(1)}, u32[]{:S(2)}) %copy-start.2) | copy-done | bytes 786456
  22.9 0.0 collective-permute-done.12.refs_10_
  23.0 0.5 collective-permute-start.4
  23.4 0.0 collective-permute-done.11.refs_9_
  23.4 0.1 collective-permute-start.13
  23.5 0.7 %collective-permute-done.8.refs_5_ = f32[4,2,64,128]{3,2,1,0:T(8,128)} collective-permute-done((f32[4,2,64,128]{3,2,1,0:T(8,128)S(1)}, f32[4,2,64,128]{3,2,1,0:T(8,128)}, u32[]{:S(2)}, u32[]{:S(2)}) %collective-permute-start.8) | collective-permute-done | bytes 262176 | tf_op jit(solution)/shard_map/ppermute | solution.py:437
  24.2 0.0 collective-permute-start.10
  24.2 0.3 collective-permute-done.3.refs_1_
  24.4 0.3 collective-permute-start.5
  24.7 0.1 pad_add_fusion.place
  24.8 0.0 collective-permute-done.9.refs_6_
  24.8 0.0 collective-permute-done.4.refs_2_
  24.8 0.4 collective-permute-done.13.refs_11_
  25.2 0.7 %collective-permute-done.10.refs_7_ = f32[4,2,64,128]{3,2,1,0:T(8,128)S(1)} collective-permute-done((f32[4,2,64,128]{3,2,1,0:T(8,128)}, f32[4,2,64,128]{3,2,1,0:T(8,128)S(1)}, u32[]{:S(2)}, u32[]{:S(2)}) %collective-permute-start.10) | collective-permute-done | bytes 262176 | tf_op jit(solution)/shard_map/ppermute | solution.py:437
  25.9 0.5 collective-permute-done.5.refs_3_
  26.4 0.0 copy-done.4
  26.4 0.0 copy-done.5
  26.4 0.0 copy-done.7
  26.4 0.0 copy-done.10
  26.5 29.6 %replicated_steps.1 = (f32[64,128]{1,0:T(8,128)}, f32[1,8]{1,0:T(1,128)}) custom-call(s32[3]{0:T(128)S(1)} %pad_add_fusion.place, s32[2,2]{1,0:T(2,128)S(1)} %copy-done.10, f32[4,2,64,128]{3,2,1,0:T(8,128)S(1)} %pad_maximum_fusion.refs_0_, f32[4,2,64,128]{3,2,1,0:T(8,128)} %collective-permute-done.3.refs_1_, ...), custom_call_target="tpu_custom_call" | custom-call | tf_op jit(solution)/shard_map/replicated_steps/pallas_call | solution.py:492
  (5 shorter events, 0.1 us)
Async XLA Ops:
  0.6 3.1 %copy-start = (f32[64,512]{1,0:T(8,128)S(1)}, f32[64,512]{1,0:T(8,128)}, u32[]{:S(2)}) copy-start(f32[64,512]{1,0:T(8,128)} %param.12) | copy-start | bytes 393220
  0.6 18.4 %copy-start.3 = (bf16[4,256,256]{2,1,0:T(8,128)(2,1)S(1)}, bf16[4,256,256]{2,1,0:T(8,128)(2,1)}, u32[]{:S(2)}) copy-start(bf16[4,256,256]{2,1,0:T(8,128)(2,1)} %constant.52.clone.col_base) | copy-start | bytes 1572868
  0.7 18.4 %copy-start.6 = (f32[2,320,65]{2,1,0:T(8,128)S(1)}, f32[2,320,65]{2,1,0:T(8,128)}, u32[]{:S(2)}) copy-start(f32[2,320,65]{2,1,0:T(8,128)} %constant.50.clone.row_waves) | copy-start | bytes 499204
  0.7 18.4 %copy-start.9 = (f32[65,65]{1,0:T(8,128)S(1)}, f32[65,65]{1,0:T(8,128)}, u32[]{:S(2)}) copy-start(f32[65,65]{1,0:T(8,128)} %coeffs) | copy-start | bytes 50704
  0.7 5.7 %collective-permute-start = (f32[1,64,128]{2,1,0:T(8,128)}, f32[1,64,128]{2,1,0:T(8,128)S(1)}, u32[]{:S(2)}, u32[]{:S(2)}) collective-permute-start(f32[1,64,128]{2,1,0:T(8,128)} %bitcast.20), channel_id=1, source_target_pairs={{0,2},{1,3},{2,0},{3,1},{4,6},{5,7},{6,4},{7,5},{8,10},{9,11},{10,... | collective-permute-start | bytes 98312 | tf_op jit(solution)/shard_map/ppermute | solution.py:437
  3.7 15.4 %copy-start.8 = (f32[2,65,256]{2,1,0:T(8,128)S(1)}, f32[2,65,256]{2,1,0:T(8,128)}, u32[]{:S(2)}) copy-start(f32[2,65,256]{2,1,0:T(8,128)} %constant.51.clone.col_waves) | copy-start | bytes 399364
  3.8 6.0 %collective-permute-start.6 = (f32[1,2,64,128]{3,2,1,0:T(8,128)S(1)}, f32[1,2,64,128]{3,2,1,0:T(8,128)S(1)}, u32[]{:S(2)}, u32[]{:S(2)}) collective-permute-start(f32[1,2,64,128]{3,2,1,0:T(8,128)S(1)} %bitcast_bitcast_fusion), channel_id=1, source_target_pairs={{0,16},{4,20},{8,24},{12,28},{16,0},{20,4},{24,8},{28,12},{1,17},{... | collective-permute-start | bytes 196616 | tf_op jit(solution)/shard_map/ppermute | solution.py:437
  7.2 19.3 %copy-start.4 = (bf16[2,160,480]{2,1,0:T(8,128)(2,1)S(1)}, bf16[2,160,480]{2,1,0:T(8,128)(2,1)}, u32[]{:S(2)}) copy-start(bf16[2,160,480]{2,1,0:T(8,128)(2,1)} %constant.54.clone.refs_14_) | copy-start | bytes 921604
  7.2 19.3 %copy-start.5 = (bf16[2,160,480]{2,1,0:T(8,128)(2,1)S(1)}, bf16[2,160,480]{2,1,0:T(8,128)(2,1)}, u32[]{:S(2)}) copy-start(bf16[2,160,480]{2,1,0:T(8,128)(2,1)} %constant.53.clone.refs_13_) | copy-start | bytes 921604
  7.2 19.3 %copy-start.7 = (f32[512,128]{1,0:T(8,128)S(1)}, f32[512,128]{1,0:T(8,128)}, u32[]{:S(2)}) copy-start(f32[512,128]{1,0:T(8,128)} %param.13) | copy-start | bytes 786436
  7.2 19.3 %copy-start.10 = (s32[2,2]{1,0:T(2,128)S(1)}, s32[2,2]{1,0:T(2,128)}, u32[]{:S(2)}) copy-start(s32[2,2]{1,0:T(2,128)} %mask.1) | copy-start | bytes 52
  7.2 5.2 %collective-permute-start.1 = (f32[1,2,64,128]{3,2,1,0:T(8,128)S(1)}, f32[1,2,64,128]{3,2,1,0:T(8,128)S(1)}, u32[]{:S(2)}, u32[]{:S(2)}) collective-permute-start(f32[1,2,64,128]{3,2,1,0:T(8,128)S(1)} %maximum_bitcast_fusion), channel_id=1, source_target_pairs={{0,16},{4,20},{8,24},{12,28},{16,0},{20,4},{24,8},{28,12},{1,17},{... | collective-permute-start | bytes 196616 | tf_op jit(solution)/shard_map/ppermute | solution.py:437
  9.8 5.7 %collective-permute-start.7 = (f32[2,2,64,128]{3,2,1,0:T(8,128)S(1)}, f32[2,2,64,128]{3,2,1,0:T(8,128)S(1)}, u32[]{:S(2)}, u32[]{:S(2)}) collective-permute-start(f32[2,2,64,128]{3,2,1,0:T(8,128)S(1)} %pad_maximum_fusion.3), channel_id=1, source_target_pairs={{0,4},{4,0},{8,12},{12,8},{16,20},{20,16},{24,28},{28,24},{1,5},{5... | collective-permute-start | bytes 393224 | tf_op jit(solution)/shard_map/ppermute | solution.py:437
  12.5 5.0 %collective-permute-start.2 = (f32[2,2,64,128]{3,2,1,0:T(8,128)S(1)}, f32[2,2,64,128]{3,2,1,0:T(8,128)S(1)}, u32[]{:S(2)}, u32[]{:S(2)}) collective-permute-start(f32[2,2,64,128]{3,2,1,0:T(8,128)S(1)} %pad_maximum_fusion.2), channel_id=1, source_target_pairs={{0,8},{4,12},{8,0},{12,4},{16,24},{20,28},{24,16},{28,20},{1,9},{5... | collective-permute-start | bytes 393224 | tf_op jit(solution)/shard_map/ppermute | solution.py:437
  14.1 8.9 %collective-permute-start.12 = (f32[1,512,128]{2,1,0:T(8,128)}, f32[1,512,128]{2,1,0:T(8,128)S(1)}, u32[]{:S(2)}, u32[]{:S(2)}) collective-permute-start(f32[1,512,128]{2,1,0:T(8,128)} %bitcast.17), channel_id=1, source_target_pairs={{0,1},{1,0},{2,3},{3,2},{4,5},{5,4},{6,7},{7,6},{8,9},{9,8},{10,11... | collective-permute-start | bytes 786440 | tf_op jit(solution)/shard_map/ppermute | solution.py:437
  14.1 9.4 %collective-permute-start.11 = (f32[1,512,128]{2,1,0:T(8,128)}, f32[1,512,128]{2,1,0:T(8,128)}, u32[]{:S(2)}, u32[]{:S(2)}) collective-permute-start(f32[1,512,128]{2,1,0:T(8,128)} %bitcast.18), channel_id=1, source_target_pairs={{0,2},{1,3},{2,0},{3,1},{4,6},{5,7},{6,4},{7,5},{8,10},{9,11},{10,... | collective-permute-start | bytes 786440 | tf_op jit(solution)/shard_map/ppermute | solution.py:437
  15.6 8.6 %collective-permute-start.8 = (f32[4,2,64,128]{3,2,1,0:T(8,128)S(1)}, f32[4,2,64,128]{3,2,1,0:T(8,128)}, u32[]{:S(2)}, u32[]{:S(2)}) collective-permute-start(f32[4,2,64,128]{3,2,1,0:T(8,128)S(1)} %pad_maximum_fusion.1.refs_4_), channel_id=1, source_target_pairs={{0,8},{4,12},{8,0},{12,4},{16,24},{20,28},{24,16},{28,20},{1,9},{5... | collective-permute-start | bytes 786440 | tf_op jit(solution)/shard_map/ppermute | solution.py:437
  17.5 6.9 %collective-permute-start.3 = (f32[4,2,64,128]{3,2,1,0:T(8,128)S(1)}, f32[4,2,64,128]{3,2,1,0:T(8,128)}, u32[]{:S(2)}, u32[]{:S(2)}) collective-permute-start(f32[4,2,64,128]{3,2,1,0:T(8,128)S(1)} %pad_maximum_fusion.refs_0_), channel_id=1, source_target_pairs={{0,4},{4,0},{8,12},{12,8},{16,20},{20,16},{24,28},{28,24},{1,5},{5... | collective-permute-start | bytes 786440 | tf_op jit(solution)/shard_map/ppermute | solution.py:437
  19.1 5.7 %collective-permute-start.9 = (f32[4,2,64,128]{3,2,1,0:T(8,128)S(1)}, f32[4,2,64,128]{3,2,1,0:T(8,128)}, u32[]{:S(2)}, u32[]{:S(2)}) collective-permute-start(f32[4,2,64,128]{3,2,1,0:T(8,128)S(1)} %pad_maximum_fusion.1.refs_4_), channel_id=1, source_target_pairs={{0,1},{1,0},{2,3},{3,2},{4,5},{5,4},{6,7},{7,6},{8,9},{9,8},{10,11... | collective-permute-start | bytes 786440 | tf_op jit(solution)/shard_map/ppermute | solution.py:437
  21.0 1.1 %copy-start.1 = (f32[2,4,160,256]{3,2,1,0:T(8,128)}, f32[2,4,160,256]{3,2,1,0:T(8,128)S(1)}, u32[]{:S(2)}) copy-start(f32[2,4,160,256]{3,2,1,0:T(8,128)S(1)} %get-tuple-element.19.refs_12_) | copy-start | bytes 3932164
  22.1 0.9 %copy-start.2 = (f8e5m2[2,3,512,256]{3,2,1,0:T(32,128)(4,1)}, f8e5m2[2,3,512,256]{3,2,1,0:T(32,128)(4,1)S(1)}, u32[]{:S(2)}) copy-start(f8e5m2[2,3,512,256]{3,2,1,0:T(32,128)(4,1)S(1)} %get-tuple-element.21.refs_16_) | copy-start | bytes 2359300
  23.0 1.8 %collective-permute-start.4 = (f32[4,2,64,128]{3,2,1,0:T(8,128)S(1)}, f32[4,2,64,128]{3,2,1,0:T(8,128)S(1)}, u32[]{:S(2)}, u32[]{:S(2)}) collective-permute-start(f32[4,2,64,128]{3,2,1,0:T(8,128)S(1)} %pad_maximum_fusion.refs_0_), channel_id=1, source_target_pairs={{0,1},{1,0},{2,3},{3,2},{4,5},{5,4},{6,7},{7,6},{8,9},{9,8},{10,11... | collective-permute-start | bytes 786440 | tf_op jit(solution)/shard_map/ppermute | solution.py:437
  23.4 1.7 %collective-permute-start.13 = (f32[1,512,128]{2,1,0:T(8,128)}, f32[1,512,128]{2,1,0:T(8,128)S(1)}, u32[]{:S(2)}, u32[]{:S(2)}) collective-permute-start(f32[1,512,128]{2,1,0:T(8,128)} %collective-permute-done.11.refs_9_), channel_id=1, source_target_pairs={{0,1},{1,0},{2,3},{3,2},{4,5},{5,4},{6,7},{7,6},{8,9},{9,8},{10,11... | collective-permute-start | bytes 786440 | tf_op jit(solution)/shard_map/ppermute | solution.py:437
  24.2 1.7 %collective-permute-start.10 = (f32[4,2,64,128]{3,2,1,0:T(8,128)}, f32[4,2,64,128]{3,2,1,0:T(8,128)S(1)}, u32[]{:S(2)}, u32[]{:S(2)}) collective-permute-start(f32[4,2,64,128]{3,2,1,0:T(8,128)} %collective-permute-done.8.refs_5_), channel_id=1, source_target_pairs={{0,1},{1,0},{2,3},{3,2},{4,5},{5,4},{6,7},{7,6},{8,9},{9,8},{10,11... | collective-permute-start | bytes 786440 | tf_op jit(solution)/shard_map/ppermute | solution.py:437
  24.4 2.0 %collective-permute-start.5 = (f32[4,2,64,128]{3,2,1,0:T(8,128)}, f32[4,2,64,128]{3,2,1,0:T(8,128)}, u32[]{:S(2)}, u32[]{:S(2)}) collective-permute-start(f32[4,2,64,128]{3,2,1,0:T(8,128)} %collective-permute-done.3.refs_1_), channel_id=1, source_target_pairs={{0,1},{1,0},{2,3},{3,2},{4,5},{5,4},{6,7},{7,6},{8,9},{9,8},{10,11... | collective-permute-start | bytes 786440 | tf_op jit(solution)/shard_map/ppermute | solution.py:437

commit v5 on v4

--- a/solution.py
+++ b/solution.py
@@ -395,6 +395,8 @@
         tiles = [(a, b) for a in range(tile_rows) for b in range(tile_cols)]
         for b in range(col_windows):
             columns(b)
+            if tiles:
+                tile_left(*tiles.pop(0))
         for b in range(col_windows):
             for a in range(tile_rows):
                 spectral(a, b, 0)

time: 56.5 us -> 57.8 us (1.023)
  Pallas kernels: 31.5 us -> 32.8 us
    pallas_call x1, Pallas kernels: 29.6 us -> 30.9 us  [replicated(): pl.pallas_call(functools.partial(replicated_kernel, (bit_places(down), bi...]
where the time goes in v5:
time: 57.8 us; the launch traced here: 57.4 us
  Pallas kernels  32.8 us (57%)
  starting transfers between devices  16.3 us (28%)
  waiting for transfers between devices  4.67 us (8%)
  local copies, waits for them, and re-layouts  1.99 us (3%)
  other arithmetic  0.89 us (2%)
  between operations  0.77 us (1%)
    pallas_call x1, Pallas kernels, replicated(): pl.pallas_call(functools.partial(replicated_kernel, (bit_places(down), bi...  30.9 us
    ppermute x14, starting transfers between devices, swap(): lax.ppermute(value, axis, [(i, i ^ bit) for i in range(lax.axis_size(axis...  16.3 us
    ppermute x14, waiting for transfers between devices, swap(): lax.ppermute(value, axis, [(i, i ^ bit) for i in range(lax.axis_size(axis...  4.67 us
    unnamed x22, local copies, waits for them, and re-layouts  1.99 us
    pallas_call x1, Pallas kernels, setup(): pl.pallas_call(setup_kernel, out_shape=(jax.ShapeDtypeStruct((2, 4, HALF...  1.88 us
  transfers between devices with their start and end apart: 14, of which 7 were waited for; matrix products, arithmetic and copies ran while one was open for 2% of the time, Pallas kernels for 3%

profile of v5, /device:TPU:0, one launch (start us, length us, event | category | flops | bytes accessed | tf_op | source)
XLA Modules:
  0.0 57.4 jit_solution(1826568404466920154)
XLA Ops:
  0.6 0.0 copy-start
  0.6 0.0 copy-start.3
  0.7 0.0 copy-start.6
  0.7 0.0 copy-start.9
  0.7 3.1 %collective-permute-start = (f32[1,64,128]{2,1,0:T(8,128)}, f32[1,64,128]{2,1,0:T(8,128)S(1)}, u32[]{:S(2)}, u32[]{:S(2)}) collective-permute-start(f32[1,64,128]{2,1,0:T(8,128)} %bitcast.20), channel_id=1, source_target_pairs={{0,2},{1,3},{2,0},{3,1},{4,6},{5,7},{6,4},{7,5},{8,10},{9,11},{10,... | collective-permute-start | bytes 98312 | tf_op jit(solution)/shard_map/ppermute | solution.py:439
  3.7 0.0 copy-done
  3.7 0.0 copy-start.8
  3.8 2.7 %collective-permute-start.6 = (f32[1,2,64,128]{3,2,1,0:T(8,128)S(1)}, f32[1,2,64,128]{3,2,1,0:T(8,128)S(1)}, u32[]{:S(2)}, u32[]{:S(2)}) collective-permute-start(f32[1,2,64,128]{3,2,1,0:T(8,128)S(1)} %bitcast_bitcast_fusion), channel_id=1, source_target_pairs={{0,16},{4,20},{8,24},{12,28},{16,0},{20,4},{24,8},{28,12},{1,17},{... | collective-permute-start | bytes 196616 | tf_op jit(solution)/shard_map/ppermute | solution.py:439
  6.4 0.0 collective-permute-done
  6.4 0.8 %maximum_bitcast_fusion = f32[1,2,64,128]{3,2,1,0:T(8,128)S(1)} fusion(f32[1,64,128]{2,1,0:T(8,128)S(1)} %collective-permute-done, f32[1,64,128]{2,1,0:T(8,128)} %bitcast.21), kind=kLoop, calls=%fused_computation.5 | loop fusion | flops 16384 | bytes 131072 | tf_op jit(solution)/shard_map/broadcast_in_dim | solution.py:467
  7.2 0.0 copy-start.4
  7.2 0.0 copy-start.5
  7.2 0.0 copy-start.7
  7.2 0.0 copy-start.10
  7.2 2.6 %collective-permute-start.1 = (f32[1,2,64,128]{3,2,1,0:T(8,128)S(1)}, f32[1,2,64,128]{3,2,1,0:T(8,128)S(1)}, u32[]{:S(2)}, u32[]{:S(2)}) collective-permute-start(f32[1,2,64,128]{3,2,1,0:T(8,128)S(1)} %maximum_bitcast_fusion), channel_id=1, source_target_pairs={{0,16},{4,20},{8,24},{12,28},{16,0},{20,4},{24,8},{28,12},{1,17},{... | collective-permute-start | bytes 196616 | tf_op jit(solution)/shard_map/ppermute | solution.py:439
  9.8 0.0 collective-permute-done.6
  9.8 1.6 %collective-permute-start.7 = (f32[2,2,64,128]{3,2,1,0:T(8,128)S(1)}, f32[2,2,64,128]{3,2,1,0:T(8,128)S(1)}, u32[]{:S(2)}, u32[]{:S(2)}) collective-permute-start(f32[2,2,64,128]{3,2,1,0:T(8,128)S(1)} %pad_maximum_fusion.3), channel_id=1, source_target_pairs={{0,4},{4,0},{8,12},{12,8},{16,20},{20,16},{24,28},{28,24},{1,5},{5... | collective-permute-start | bytes 393224 | tf_op jit(solution)/shard_map/ppermute | solution.py:439
  11.4 1.1 %collective-permute-done.1 = f32[1,2,64,128]{3,2,1,0:T(8,128)S(1)} collective-permute-done((f32[1,2,64,128]{3,2,1,0:T(8,128)S(1)}, f32[1,2,64,128]{3,2,1,0:T(8,128)S(1)}, u32[]{:S(2)}, u32[]{:S(2)}) %collective-permute-start.1) | collective-permute-done | bytes 65568 | tf_op jit(solution)/shard_map/ppermute | solution.py:439
  12.5 1.6 %collective-permute-start.2 = (f32[2,2,64,128]{3,2,1,0:T(8,128)S(1)}, f32[2,2,64,128]{3,2,1,0:T(8,128)S(1)}, u32[]{:S(2)}, u32[]{:S(2)}) collective-permute-start(f32[2,2,64,128]{3,2,1,0:T(8,128)S(1)} %pad_maximum_fusion.2), channel_id=1, source_target_pairs={{0,8},{4,12},{8,0},{12,4},{16,24},{20,28},{24,16},{28,20},{1,9},{5... | collective-permute-start | bytes 393224 | tf_op jit(solution)/shard_map/ppermute | solution.py:439
  14.1 0.0 collective-permute-start.12
  14.1 1.5 %collective-permute-start.11 = (f32[1,512,128]{2,1,0:T(8,128)}, f32[1,512,128]{2,1,0:T(8,128)}, u32[]{:S(2)}, u32[]{:S(2)}) collective-permute-start(f32[1,512,128]{2,1,0:T(8,128)} %bitcast.18), channel_id=1, source_target_pairs={{0,2},{1,3},{2,0},{3,1},{4,6},{5,7},{6,4},{7,5},{8,10},{9,11},{10,... | collective-permute-start | bytes 786440 | tf_op jit(solution)/shard_map/ppermute | solution.py:439
  15.6 0.0 collective-permute-done.7
  15.6 0.9 %collective-permute-start.8 = (f32[4,2,64,128]{3,2,1,0:T(8,128)S(1)}, f32[4,2,64,128]{3,2,1,0:T(8,128)}, u32[]{:S(2)}, u32[]{:S(2)}) collective-permute-start(f32[4,2,64,128]{3,2,1,0:T(8,128)S(1)} %pad_maximum_fusion.1.refs_4_), channel_id=1, source_target_pairs={{0,8},{4,12},{8,0},{12,4},{16,24},{20,28},{24,16},{28,20},{1,9},{5... | collective-permute-start | bytes 786440 | tf_op jit(solution)/shard_map/ppermute | solution.py:439
  16.5 1.0 %collective-permute-done.2 = f32[2,2,64,128]{3,2,1,0:T(8,128)S(1)} collective-permute-done((f32[2,2,64,128]{3,2,1,0:T(8,128)S(1)}, f32[2,2,64,128]{3,2,1,0:T(8,128)S(1)}, u32[]{:S(2)}, u32[]{:S(2)}) %collective-permute-start.2) | collective-permute-done | bytes 131104 | tf_op jit(solution)/shard_map/ppermute | solution.py:439
  17.5 1.6 %collective-permute-start.3 = (f32[4,2,64,128]{3,2,1,0:T(8,128)S(1)}, f32[4,2,64,128]{3,2,1,0:T(8,128)}, u32[]{:S(2)}, u32[]{:S(2)}) collective-permute-start(f32[4,2,64,128]{3,2,1,0:T(8,128)S(1)} %pad_maximum_fusion.refs_0_), channel_id=1, source_target_pairs={{0,4},{4,0},{8,12},{12,8},{16,20},{20,16},{24,28},{28,24},{1,5},{5... | collective-permute-start | bytes 786440 | tf_op jit(solution)/shard_map/ppermute | solution.py:439
  19.1 0.0 collective-permute-start.9
  19.1 0.0 copy-done.3
  19.1 0.0 copy-done.6
  19.1 0.0 copy-done.9
  19.1 0.0 copy-done.8
  19.1 1.9 %setup.1 = (f32[2,4,160,256]{3,2,1,0:T(8,128)S(1)}, bf16[2,3,256,256]{3,2,1,0:T(8,128)(2,1)S(1)}, f8e5m2[2,3,512,256]{3,2,1,0:T(32,128)(4,1)S(1)}) custom-call(f32[65,65]{1,0:T(8,128)S(1)} %copy-done.9, f32[2,320,65]{2,1,0:T(8,128)S(1)} %copy-done.6, f32[2,65,256]{2,1,0:T(8,128)S(1)} %copy-done.8, bf16[4,256,256]{2,1,0:T(8,128)(2,1)S(1)} %copy-done.3), custom_call_target="tpu_custom_call" | custom-call | tf_op jit(solution)/shard_map/setup/pallas_call | solution.py:212
  21.0 0.0 copy-start.1
  21.0 1.1 %copy-done.1 = f32[2,4,160,256]{3,2,1,0:T(8,128)} copy-done((f32[2,4,160,256]{3,2,1,0:T(8,128)}, f32[2,4,160,256]{3,2,1,0:T(8,128)S(1)}, u32[]{:S(2)}) %copy-start.1) | copy-done | bytes 1310744
  22.1 0.0 copy-start.2
  22.1 0.9 %copy-done.2 = f8e5m2[2,3,512,256]{3,2,1,0:T(32,128)(4,1)} copy-done((f8e5m2[2,3,512,256]{3,2,1,0:T(32,128)(4,1)}, f8e5m2[2,3,512,256]{3,2,1,0:T(32,128)(4,1)S(1)}, u32[]{:S(2)}) %copy-start.2) | copy-done | bytes 786456
  22.9 0.0 collective-permute-done.12.refs_10_
  23.0 0.5 collective-permute-start.4
  23.4 0.0 collective-permute-done.11.refs_9_
  23.4 0.1 collective-permute-start.13
  23.5 0.7 %collective-permute-done.8.refs_5_ = f32[4,2,64,128]{3,2,1,0:T(8,128)} collective-permute-done((f32[4,2,64,128]{3,2,1,0:T(8,128)S(1)}, f32[4,2,64,128]{3,2,1,0:T(8,128)}, u32[]{:S(2)}, u32[]{:S(2)}) %collective-permute-start.8) | collective-permute-done | bytes 262176 | tf_op jit(solution)/shard_map/ppermute | solution.py:439
  24.2 0.0 collective-permute-start.10
  24.2 0.3 collective-permute-done.3.refs_1_
  24.4 0.3 collective-permute-start.5
  24.7 0.1 pad_add_fusion.place
  24.8 0.0 collective-permute-done.9.refs_6_
  24.8 0.0 collective-permute-done.4.refs_2_
  24.8 0.4 collective-permute-done.13.refs_11_
  25.2 0.7 %collective-permute-done.10.refs_7_ = f32[4,2,64,128]{3,2,1,0:T(8,128)S(1)} collective-permute-done((f32[4,2,64,128]{3,2,1,0:T(8,128)}, f32[4,2,64,128]{3,2,1,0:T(8,128)S(1)}, u32[]{:S(2)}, u32[]{:S(2)}) %collective-permute-start.10) | collective-permute-done | bytes 262176 | tf_op jit(solution)/shard_map/ppermute | solution.py:439
  25.9 0.5 collective-permute-done.5.refs_3_
  26.4 0.0 copy-done.4
  26.4 0.0 copy-done.5
  26.4 0.0 copy-done.7
  26.4 0.0 copy-done.10
  26.5 30.9 %replicated_steps.1 = (f32[64,128]{1,0:T(8,128)}, f32[1,8]{1,0:T(1,128)}) custom-call(s32[3]{0:T(128)S(1)} %pad_add_fusion.place, s32[2,2]{1,0:T(2,128)S(1)} %copy-done.10, f32[4,2,64,128]{3,2,1,0:T(8,128)S(1)} %pad_maximum_fusion.refs_0_, f32[4,2,64,128]{3,2,1,0:T(8,128)} %collective-permute-done.3.refs_1_, ...), custom_call_target="tpu_custom_call" | custom-call | tf_op jit(solution)/shard_map/replicated_steps/pallas_call | solution.py:494
  (5 shorter events, 0.1 us)
Async XLA Ops:
  0.6 3.1 %copy-start = (f32[64,512]{1,0:T(8,128)S(1)}, f32[64,512]{1,0:T(8,128)}, u32[]{:S(2)}) copy-start(f32[64,512]{1,0:T(8,128)} %param.12) | copy-start | bytes 393220
  0.6 18.4 %copy-start.3 = (bf16[4,256,256]{2,1,0:T(8,128)(2,1)S(1)}, bf16[4,256,256]{2,1,0:T(8,128)(2,1)}, u32[]{:S(2)}) copy-start(bf16[4,256,256]{2,1,0:T(8,128)(2,1)} %constant.52.clone.col_base) | copy-start | bytes 1572868
  0.7 18.4 %copy-start.6 = (f32[2,320,65]{2,1,0:T(8,128)S(1)}, f32[2,320,65]{2,1,0:T(8,128)}, u32[]{:S(2)}) copy-start(f32[2,320,65]{2,1,0:T(8,128)} %constant.50.clone.row_waves) | copy-start | bytes 499204
  0.7 18.4 %copy-start.9 = (f32[65,65]{1,0:T(8,128)S(1)}, f32[65,65]{1,0:T(8,128)}, u32[]{:S(2)}) copy-start(f32[65,65]{1,0:T(8,128)} %coeffs) | copy-start | bytes 50704
  0.7 5.7 %collective-permute-start = (f32[1,64,128]{2,1,0:T(8,128)}, f32[1,64,128]{2,1,0:T(8,128)S(1)}, u32[]{:S(2)}, u32[]{:S(2)}) collective-permute-start(f32[1,64,128]{2,1,0:T(8,128)} %bitcast.20), channel_id=1, source_target_pairs={{0,2},{1,3},{2,0},{3,1},{4,6},{5,7},{6,4},{7,5},{8,10},{9,11},{10,... | collective-permute-start | bytes 98312 | tf_op jit(solution)/shard_map/ppermute | solution.py:439
  3.7 15.4 %copy-start.8 = (f32[2,65,256]{2,1,0:T(8,128)S(1)}, f32[2,65,256]{2,1,0:T(8,128)}, u32[]{:S(2)}) copy-start(f32[2,65,256]{2,1,0:T(8,128)} %constant.51.clone.col_waves) | copy-start | bytes 399364
  3.8 6.0 %collective-permute-start.6 = (f32[1,2,64,128]{3,2,1,0:T(8,128)S(1)}, f32[1,2,64,128]{3,2,1,0:T(8,128)S(1)}, u32[]{:S(2)}, u32[]{:S(2)}) collective-permute-start(f32[1,2,64,128]{3,2,1,0:T(8,128)S(1)} %bitcast_bitcast_fusion), channel_id=1, source_target_pairs={{0,16},{4,20},{8,24},{12,28},{16,0},{20,4},{24,8},{28,12},{1,17},{... | collective-permute-start | bytes 196616 | tf_op jit(solution)/shard_map/ppermute | solution.py:439
  7.2 19.3 %copy-start.4 = (bf16[2,160,480]{2,1,0:T(8,128)(2,1)S(1)}, bf16[2,160,480]{2,1,0:T(8,128)(2,1)}, u32[]{:S(2)}) copy-start(bf16[2,160,480]{2,1,0:T(8,128)(2,1)} %constant.54.clone.refs_14_) | copy-start | bytes 921604
  7.2 19.3 %copy-start.5 = (bf16[2,160,480]{2,1,0:T(8,128)(2,1)S(1)}, bf16[2,160,480]{2,1,0:T(8,128)(2,1)}, u32[]{:S(2)}) copy-start(bf16[2,160,480]{2,1,0:T(8,128)(2,1)} %constant.53.clone.refs_13_) | copy-start | bytes 921604
  7.2 19.3 %copy-start.7 = (f32[512,128]{1,0:T(8,128)S(1)}, f32[512,128]{1,0:T(8,128)}, u32[]{:S(2)}) copy-start(f32[512,128]{1,0:T(8,128)} %param.13) | copy-start | bytes 786436
  7.2 19.3 %copy-start.10 = (s32[2,2]{1,0:T(2,128)S(1)}, s32[2,2]{1,0:T(2,128)}, u32[]{:S(2)}) copy-start(s32[2,2]{1,0:T(2,128)} %mask.1) | copy-start | bytes 52
  7.2 5.2 %collective-permute-start.1 = (f32[1,2,64,128]{3,2,1,0:T(8,128)S(1)}, f32[1,2,64,128]{3,2,1,0:T(8,128)S(1)}, u32[]{:S(2)}, u32[]{:S(2)}) collective-permute-start(f32[1,2,64,128]{3,2,1,0:T(8,128)S(1)} %maximum_bitcast_fusion), channel_id=1, source_target_pairs={{0,16},{4,20},{8,24},{12,28},{16,0},{20,4},{24,8},{28,12},{1,17},{... | collective-permute-start | bytes 196616 | tf_op jit(solution)/shard_map/ppermute | solution.py:439
  9.8 5.7 %collective-permute-start.7 = (f32[2,2,64,128]{3,2,1,0:T(8,128)S(1)}, f32[2,2,64,128]{3,2,1,0:T(8,128)S(1)}, u32[]{:S(2)}, u32[]{:S(2)}) collective-permute-start(f32[2,2,64,128]{3,2,1,0:T(8,128)S(1)} %pad_maximum_fusion.3), channel_id=1, source_target_pairs={{0,4},{4,0},{8,12},{12,8},{16,20},{20,16},{24,28},{28,24},{1,5},{5... | collective-permute-start | bytes 393224 | tf_op jit(solution)/shard_map/ppermute | solution.py:439
  12.5 5.0 %collective-permute-start.2 = (f32[2,2,64,128]{3,2,1,0:T(8,128)S(1)}, f32[2,2,64,128]{3,2,1,0:T(8,128)S(1)}, u32[]{:S(2)}, u32[]{:S(2)}) collective-permute-start(f32[2,2,64,128]{3,2,1,0:T(8,128)S(1)} %pad_maximum_fusion.2), channel_id=1, source_target_pairs={{0,8},{4,12},{8,0},{12,4},{16,24},{20,28},{24,16},{28,20},{1,9},{5... | collective-permute-start | bytes 393224 | tf_op jit(solution)/shard_map/ppermute | solution.py:439
  14.1 8.9 %collective-permute-start.12 = (f32[1,512,128]{2,1,0:T(8,128)}, f32[1,512,128]{2,1,0:T(8,128)S(1)}, u32[]{:S(2)}, u32[]{:S(2)}) collective-permute-start(f32[1,512,128]{2,1,0:T(8,128)} %bitcast.17), channel_id=1, source_target_pairs={{0,1},{1,0},{2,3},{3,2},{4,5},{5,4},{6,7},{7,6},{8,9},{9,8},{10,11... | collective-permute-start | bytes 786440 | tf_op jit(solution)/shard_map/ppermute | solution.py:439
  14.1 9.4 %collective-permute-start.11 = (f32[1,512,128]{2,1,0:T(8,128)}, f32[1,512,128]{2,1,0:T(8,128)}, u32[]{:S(2)}, u32[]{:S(2)}) collective-permute-start(f32[1,512,128]{2,1,0:T(8,128)} %bitcast.18), channel_id=1, source_target_pairs={{0,2},{1,3},{2,0},{3,1},{4,6},{5,7},{6,4},{7,5},{8,10},{9,11},{10,... | collective-permute-start | bytes 786440 | tf_op jit(solution)/shard_map/ppermute | solution.py:439
  15.6 8.6 %collective-permute-start.8 = (f32[4,2,64,128]{3,2,1,0:T(8,128)S(1)}, f32[4,2,64,128]{3,2,1,0:T(8,128)}, u32[]{:S(2)}, u32[]{:S(2)}) collective-permute-start(f32[4,2,64,128]{3,2,1,0:T(8,128)S(1)} %pad_maximum_fusion.1.refs_4_), channel_id=1, source_target_pairs={{0,8},{4,12},{8,0},{12,4},{16,24},{20,28},{24,16},{28,20},{1,9},{5... | collective-permute-start | bytes 786440 | tf_op jit(solution)/shard_map/ppermute | solution.py:439
  17.5 6.9 %collective-permute-start.3 = (f32[4,2,64,128]{3,2,1,0:T(8,128)S(1)}, f32[4,2,64,128]{3,2,1,0:T(8,128)}, u32[]{:S(2)}, u32[]{:S(2)}) collective-permute-start(f32[4,2,64,128]{3,2,1,0:T(8,128)S(1)} %pad_maximum_fusion.refs_0_), channel_id=1, source_target_pairs={{0,4},{4,0},{8,12},{12,8},{16,20},{20,16},{24,28},{28,24},{1,5},{5... | collective-permute-start | bytes 786440 | tf_op jit(solution)/shard_map/ppermute | solution.py:439
  19.1 5.7 %collective-permute-start.9 = (f32[4,2,64,128]{3,2,1,0:T(8,128)S(1)}, f32[4,2,64,128]{3,2,1,0:T(8,128)}, u32[]{:S(2)}, u32[]{:S(2)}) collective-permute-start(f32[4,2,64,128]{3,2,1,0:T(8,128)S(1)} %pad_maximum_fusion.1.refs_4_), channel_id=1, source_target_pairs={{0,1},{1,0},{2,3},{3,2},{4,5},{5,4},{6,7},{7,6},{8,9},{9,8},{10,11... | collective-permute-start | bytes 786440 | tf_op jit(solution)/shard_map/ppermute | solution.py:439
  21.0 1.1 %copy-start.1 = (f32[2,4,160,256]{3,2,1,0:T(8,128)}, f32[2,4,160,256]{3,2,1,0:T(8,128)S(1)}, u32[]{:S(2)}) copy-start(f32[2,4,160,256]{3,2,1,0:T(8,128)S(1)} %get-tuple-element.19.refs_12_) | copy-start | bytes 3932164
  22.1 0.9 %copy-start.2 = (f8e5m2[2,3,512,256]{3,2,1,0:T(32,128)(4,1)}, f8e5m2[2,3,512,256]{3,2,1,0:T(32,128)(4,1)S(1)}, u32[]{:S(2)}) copy-start(f8e5m2[2,3,512,256]{3,2,1,0:T(32,128)(4,1)S(1)} %get-tuple-element.21.refs_16_) | copy-start | bytes 2359300
  23.0 1.8 %collective-permute-start.4 = (f32[4,2,64,128]{3,2,1,0:T(8,128)S(1)}, f32[4,2,64,128]{3,2,1,0:T(8,128)S(1)}, u32[]{:S(2)}, u32[]{:S(2)}) collective-permute-start(f32[4,2,64,128]{3,2,1,0:T(8,128)S(1)} %pad_maximum_fusion.refs_0_), channel_id=1, source_target_pairs={{0,1},{1,0},{2,3},{3,2},{4,5},{5,4},{6,7},{7,6},{8,9},{9,8},{10,11... | collective-permute-start | bytes 786440 | tf_op jit(solution)/shard_map/ppermute | solution.py:439
  23.4 1.7 %collective-permute-start.13 = (f32[1,512,128]{2,1,0:T(8,128)}, f32[1,512,128]{2,1,0:T(8,128)S(1)}, u32[]{:S(2)}, u32[]{:S(2)}) collective-permute-start(f32[1,512,128]{2,1,0:T(8,128)} %collective-permute-done.11.refs_9_), channel_id=1, source_target_pairs={{0,1},{1,0},{2,3},{3,2},{4,5},{5,4},{6,7},{7,6},{8,9},{9,8},{10,11... | collective-permute-start | bytes 786440 | tf_op jit(solution)/shard_map/ppermute | solution.py:439
  24.2 1.7 %collective-permute-start.10 = (f32[4,2,64,128]{3,2,1,0:T(8,128)}, f32[4,2,64,128]{3,2,1,0:T(8,128)S(1)}, u32[]{:S(2)}, u32[]{:S(2)}) collective-permute-start(f32[4,2,64,128]{3,2,1,0:T(8,128)} %collective-permute-done.8.refs_5_), channel_id=1, source_target_pairs={{0,1},{1,0},{2,3},{3,2},{4,5},{5,4},{6,7},{7,6},{8,9},{9,8},{10,11... | collective-permute-start | bytes 786440 | tf_op jit(solution)/shard_map/ppermute | solution.py:439
  24.4 2.0 %collective-permute-start.5 = (f32[4,2,64,128]{3,2,1,0:T(8,128)}, f32[4,2,64,128]{3,2,1,0:T(8,128)}, u32[]{:S(2)}, u32[]{:S(2)}) collective-permute-start(f32[4,2,64,128]{3,2,1,0:T(8,128)} %collective-permute-done.3.refs_1_), channel_id=1, source_target_pairs={{0,1},{1,0},{2,3},{3,2},{4,5},{5,4},{6,7},{7,6},{8,9},{9,8},{10,11... | collective-permute-start | bytes 786440 | tf_op jit(solution)/shard_map/ppermute | solution.py:439
